TPU v7x, 128 devices: a whole 4x4x4 slice. The times are simulated.
128 devices in a mesh: dp: 4 (over x), expert: 32 (over z, y, core).
Axes of the slice: x: 4, y: 4, z: 4, core: 2. Of those that a mesh axis runs over, the one named last changes fastest.
Arguments:
- tokens: bfloat16 [2, 8192, 4096], P(None, ('dp', 'expert')), may hold values from -64 to 64
- expert_of: int32 [2, 8192], P(None, ('dp', 'expert')), may hold values from 0 to 15, as said below
- w_gate: bfloat16 [32, 4096, 3584], P('expert', None, 'dp'), may hold values from -0.09375 to 0.09375
- w_up: bfloat16 [32, 4096, 3584], P('expert', None, 'dp'), may hold values from -0.09375 to 0.09375
- w_down: bfloat16 [32, 3584, 4096], P('expert', 'dp'), may hold values from -1 to 1
Outputs:
- out: bfloat16 [2, 8192, 4096], P(None, ('dp', 'expert'))
- next_scale: float32 [16], replicated
Inputs may be any that keep to these rules, and one draw needn't show every extreme that they name: `expert_of`: in each microbatch the 64 tokens of one device name each expert at most 4 times, and one expert, the same for all devices of that microbatch, exactly 4 times.
All inputs are finite; a program needn't handle non-finite values.
Results may differ from a plain program's by a relative error of at most 0.012.
Values may be sent and summed in bfloat16 or wider, within the bound.
No kernel may reach another device: no remote copies, remote signals or barrier semaphores. Data moves between devices by JAX's collectives and lax.ppermute only.
A program may use at most 128 MiB of HBM per device.

v0:
```python
import functools

import jax
import jax.numpy as jnp
from jax import lax
from jax.sharding import Mesh
from jax.sharding import PartitionSpec as P

SPAN = 2
EXPERT = ("expert_0", "expert_1", "expert_2")
DP_EXPERT = ("dp", "expert_0", "expert_1", "expert_2")


clip_target = 2.0


def cut_along(shard, dim, devices):
    before, after = (shard.shape[:dim], shard.shape[dim + 1 :])
    return jnp.moveaxis(shard.reshape(*before, devices, -1, *after), dim, 0)


def summed_on_arrival(shard, axis, dim):
    devices = lax.axis_size(axis)
    parts = lax.all_to_all(cut_along(shard, dim, devices), axis, 0, 0, tiled=True)
    return jnp.sum(parts.astype(jnp.float32), axis=0)


def by_axis(shard, axes):
    return functools.reduce(lax.psum, axes, shard)


def body(tokens, expert_of, w_gate, w_up, w_down):
    micro_count = tokens.shape[0]
    tok_rows = tokens.shape[1]
    model_width = tokens.shape[2]
    expert_size = lax.axis_size(EXPERT)
    expert_count = expert_size // SPAN
    capacity = max(2, 9 * tok_rows // (8 * expert_count))
    my_expert = lax.axis_index(EXPERT) // SPAN
    gate_local = w_gate[0]
    up_local = w_up[0]
    down_local = w_down[0]
    slot_range = jnp.arange(expert_count * capacity, dtype=jnp.int32)
    expert_range = jnp.arange(expert_count, dtype=jnp.int32)
    clip_scale = jnp.ones((expert_count,), jnp.float32)
    results = []
    for micro_idx in range(micro_count):
        token_ids = expert_of[micro_idx]
        onehot_ids = (token_ids[:, None] == expert_range[None, :]).astype(jnp.int32)
        earlier = jnp.cumsum(onehot_ids, axis=0) - onehot_ids
        slot_of = jnp.sum(earlier * onehot_ids, axis=1)
        position = token_ids * capacity + slot_of
        placing = (position[None, :] == slot_range[:, None]).astype(jnp.bfloat16)
        tokens_now = tokens[micro_idx]
        packed = jnp.dot(placing, tokens_now, preferred_element_type=jnp.float32).astype(
            jnp.bfloat16
        )
        packed = packed.reshape(expert_count, capacity, model_width)
        factor = clip_scale[my_expert]
        sending_all = jnp.repeat(packed, SPAN, axis=0)
        arrived = lax.all_to_all(sending_all, EXPERT, split_axis=0, concat_axis=0, tiled=True)
        flat_rows = arrived.reshape(expert_size * capacity, model_width)
        rows_in = lax.all_gather(flat_rows, "dp", axis=0, tiled=True)
        rows_in = (factor * rows_in.astype(jnp.float32)).astype(jnp.bfloat16)
        gate_vals = jnp.dot(rows_in, gate_local, preferred_element_type=jnp.float32)
        up_vals = jnp.dot(rows_in, up_local, preferred_element_type=jnp.float32)
        hidden = (jax.nn.silu(gate_vals) * up_vals).astype(jnp.bfloat16)
        summed = summed_on_arrival(
            jnp.dot(hidden, down_local, preferred_element_type=jnp.float32).astype(jnp.bfloat16),
            "dp",
            0,
        )
        halves = summed.astype(jnp.bfloat16).reshape(expert_size, capacity, model_width)
        returned = lax.all_to_all(halves, EXPERT, split_axis=0, concat_axis=0, tiled=True)
        returned = lax.optimization_barrier(returned)
        joined = jnp.sum(
            returned.reshape(expert_count, SPAN, capacity, model_width).astype(jnp.float32), axis=1
        )
        token_out = jnp.take(joined.reshape(expert_count * capacity, model_width), position, axis=0)
        results.append(token_out.astype(jnp.bfloat16))
        squares = jnp.sum(token_out * token_out, axis=1)
        onehot_float = onehot_ids.astype(jnp.float32)
        counts_local = jnp.sum(onehot_float, axis=0)
        square_local = jnp.dot(squares[None, :], onehot_float)[0]
        counts, square_sums = (by_axis(counts_local, DP_EXPERT), by_axis(square_local, DP_EXPERT))
        clip_scale = jnp.minimum(
            1.0,
            clip_target / jnp.sqrt((square_sums + model_width) / (model_width * (counts + 1.0))),
        )
    return (jnp.stack(results), clip_scale)


def solution(mesh):
    finer = Mesh(
        mesh.devices.reshape(mesh.shape["dp"], 4, 4, 2), ("dp", "expert_0", "expert_1", "expert_2")
    )
    placed = (
        P(None, DP_EXPERT, None),
        P(None, DP_EXPERT),
        P(EXPERT, None, "dp"),
        P(EXPERT, None, "dp"),
        P(EXPERT, "dp", None),
    )
    return jax.shard_map(
        body,
        mesh=finer,
        in_specs=placed,
        out_specs=(P(None, DP_EXPERT, None), P()),
        check_vma=False,
    )
```

profile of v0, /device:TPU:1, one launch (start us, length us, event | category | flops | bytes accessed | tf_op | source)
XLA Modules:
  0.0 390.0 jit_solution(15823741617746679919)
XLA Ops:
  9.0 1.3 convolution_convert_fusion.1
  11.0 26.4 %all_to_all.30 = bf16[32,4,4096]{2,1,0:T(4,128)(2,1)S(1)} all-to-all(bf16[32,4,4096]{2,1,0:T(4,128)(2,1)S(1)} %bitcast.83), channel_id=1, replica_groups=mesh['dp'=4,'expert_0'=4,'expert_1'=4,'expert_2'=2] {'expert_0','expert_..., dimensions={0} | all-to-all | bytes 2097152 | tf_op jit(solution)/shard_map/all_to_all | solution.py:61
  37.5 1.2 reshape.65
  40.1 20.7 %all_to_all.31 = bf16[32,4,4096]{2,1,0:T(4,128)(2,1)S(1)} all-to-all(bf16[32,4,4096]{2,1,0:T(4,128)(2,1)S(1)} %bitcast.84), channel_id=1, replica_groups=mesh['dp'=4,'expert_0'=4,'expert_1'=4,'expert_2'=2] {'expert_0','expert_..., dimensions={0} | all-to-all | bytes 2097152 | tf_op jit(solution)/shard_map/all_to_all | solution.py:61
  60.8 1.1 reshape.71
  61.9 22.4 %all-gather.3.cloned.1.call-done = bf16[512,4096]{1,0:T(8,128)(2,1)} async-done(((bf16[128,4096]{1,0:T(8,128)(2,1)}), bf16[512,4096]{1,0:T(8,128)(2,1)}) %all-gather.3.cloned.1.call-update) | async-done | bytes 4194320 | tf_op jit(solution)/shard_map/all_gather | solution.py:63
  84.3 9.8 %fusion.10 = f32[512,896]{1,0:T(8,128)S(1)} fusion(bf16[512,4096]{1,0:T(8,128)(2,1)} %all-gather.3.cloned.1.call-done, bf16[1,4096,896]{2,1,0:T(8,128)(2,1)} %param.9), kind=kOutput, calls=%fused_computation.13 | convolution fusion | flops 3758096384 | bytes 13369344 | tf_op jit(solution)/shard_map/dot_general | solution.py:65
  94.1 17.3 %fusion.12 = bf16[512,4096]{1,0:T(8,128)(2,1)} fusion(bf16[1,896,4096]{2,1,0:T(8,128)(2,1)} %param.11, f32[512,896]{1,0:T(8,128)S(1)} %fusion.10, bf16[512,4096]{1,0:T(8,128)(2,1)} %all-gather.3.cloned.1.call-done, bf16[1,4096,896]{2,1,0:T(8,128)(2,1)} %param.10), kind=kOutput, calls=%fused_computation.15 | convolution fusion | flops 7521042432 | bytes 24903680 | tf_op jit(solution)/shard_map/dot_general | solution.py:69
  111.4 68.4 %all_to_all.32 = bf16[4,128,4096]{2,1,0:T(8,128)(2,1)} all-to-all(bf16[4,128,4096]{2,1,0:T(8,128)(2,1)} %bitcast.82), channel_id=1, replica_groups=mesh['dp'=4,'expert_0'=4,'expert_1'=4,'expert_2'=2] {'dp'}, dimensions={0} | all-to-all | bytes 8388608 | tf_op jit(solution)/shard_map/all_to_all | solution.py:24
  179.8 3.1 reduce_sum.102
  182.9 1.2 reshape.67
  184.2 8.1 %all-to-all-start.2 = ((bf16[32,4,4096]{2,1,0:T(4,128)(2,1)}), bf16[32,4,4096]{2,1,0:T(4,128)(2,1)S(1)}, u32[]{:S(2)}, u32[]{:S(2)}) async-start(bf16[32,4,4096]{2,1,0:T(4,128)(2,1)} %reshape.67), calls=%async_computation.2 | async-start | bytes 2097152 | tf_op jit(solution)/shard_map/all_to_all | solution.py:74
  192.4 16.9 %all-to-all-done.2 = bf16[32,4,4096]{2,1,0:T(4,128)(2,1)S(1)} async-done(((bf16[32,4,4096]{2,1,0:T(4,128)(2,1)}), bf16[32,4,4096]{2,1,0:T(4,128)(2,1)S(1)}, u32[]{:S(2)}, u32[]{:S(2)}) %all-to-all-start.2) | async-done | bytes 1048608 | tf_op jit(solution)/shard_map/all_to_all | solution.py:74
  210.3 0.9 gather_fusion
  211.7 7.5 %all-reduce.5 = (f32[16]{0:T(128)S(1)}, f32[16]{0:T(128)S(1)}) all-reduce(f32[16]{0:T(128)S(1)} %convert_reduce_fusion.3, f32[16]{0:T(128)S(1)} %convolution_bitcast_fusion.1), channel_id=1, replica_groups=mesh['dp'=4,'expert_0'=4,'expert_1'=4,'expert_2'=2] {'dp'}, use_global_device_ids=true, to_apply=%region_10.12 | all-reduce | flops 32 | bytes 256 | tf_op jit(solution)/shard_map/psum | solution.py:29
  219.2 6.5 %all-reduce.3 = (f32[16]{0:T(128)S(1)}, f32[16]{0:T(128)S(1)}) all-reduce(f32[16]{0:T(128)S(1)} %get-tuple-element.13, f32[16]{0:T(128)S(1)} %get-tuple-element.14), channel_id=1, replica_groups=mesh['dp'=4,'expert_0'=4,'expert_1'=4,'expert_2'=2] {'expert_0'}, use_global_device_ids=true, to_apply=%region_11.13 | all-reduce | flops 32 | bytes 256 | tf_op jit(solution)/shard_map/psum | solution.py:29
  225.7 7.9 %all-reduce.1 = (f32[16]{0:T(128)S(1)}, f32[16]{0:T(128)S(1)}) all-reduce(f32[16]{0:T(128)S(1)} %get-tuple-element.9, f32[16]{0:T(128)S(1)} %get-tuple-element.10), channel_id=1, replica_groups=mesh['dp'=4,'expert_0'=4,'expert_1'=4,'expert_2'=2] {'expert_1'}, use_global_device_ids=true, to_apply=%region_12.14 | all-reduce | flops 32 | bytes 256 | tf_op jit(solution)/shard_map/psum | solution.py:29
  233.6 7.4 %all-reduce.7 = (f32[16]{0:T(128)S(1)}, f32[16]{0:T(128)S(1)}) all-reduce(f32[16]{0:T(128)S(1)} %get-tuple-element.5, f32[16]{0:T(128)S(1)} %get-tuple-element.6), channel_id=1, replica_groups=mesh['dp'=4,'expert_0'=4,'expert_1'=4,'expert_2'=2] {'expert_2'}, use_global_device_ids=true, to_apply=%region_13.15 | all-reduce | flops 32 | bytes 256 | tf_op jit(solution)/shard_map/psum | solution.py:29
  241.6 11.6 %fusion.8 = f32[512,896]{1,0:T(8,128)S(1)} fusion(bf16[1,4096,896]{2,1,0:T(8,128)(2,1)} %param.9, bf16[512,4096]{1,0:T(8,128)(2,1)} %all-gather.5.cloned.1.call-done, f32[]{:T(128)} %bitcast.14), kind=kOutput, calls=%fused_computation.11 | convolution fusion | flops 3764387840 | bytes 13369348 | tf_op jit(solution)/shard_map/dot_general | solution.py:65
  253.2 8.3 %multiply_convert_fusion.3 = bf16[512,896]{1,0:T(8,128)(2,1)S(1)} fusion(f32[512,896]{1,0:T(8,128)S(1)} %fusion.8, bf16[1,4096,896]{2,1,0:T(8,128)(2,1)} %param.10, bf16[512,4096]{1,0:T(8,128)(2,1)S(1)} %copy-done.2, f32[]{:T(128)} %bitcast.14), kind=kOutput, calls=%fused_computation.21 | convolution fusion | flops 3767140352 | bytes 14286852 | tf_op jit(solution)/shard_map/dot_general | solution.py:66
  261.5 9.1 %fusion.15 = bf16[512,4096]{1,0:T(8,128)(2,1)} fusion(bf16[512,896]{1,0:T(8,128)(2,1)S(1)} %multiply_convert_fusion.3, bf16[1,896,4096]{2,1,0:T(8,128)(2,1)} %param.11), kind=kOutput, calls=%fused_computation.16 | convolution fusion | flops 3760193536 | bytes 12451840 | tf_op jit(solution)/shard_map/dot_general | solution.py:69
  270.7 4.9 %all-to-all-start.4 = ((bf16[4,128,4096]{2,1,0:T(8,128)(2,1)}), bf16[4,128,4096]{2,1,0:T(8,128)(2,1)}, u32[]{:S(2)}, u32[]{:S(2)}) async-start(bf16[4,128,4096]{2,1,0:T(8,128)(2,1)} %bitcast.81), calls=%async_computation.4 | async-start | bytes 8388608 | tf_op jit(solution)/shard_map/all_to_all | solution.py:24
  275.6 48.5 %all-to-all-done.4 = bf16[4,128,4096]{2,1,0:T(8,128)(2,1)} async-done(((bf16[4,128,4096]{2,1,0:T(8,128)(2,1)}), bf16[4,128,4096]{2,1,0:T(8,128)(2,1)}, u32[]{:S(2)}, u32[]{:S(2)}) %all-to-all-start.4) | async-done | bytes 4194336 | tf_op jit(solution)/shard_map/all_to_all | solution.py:24
  324.2 3.1 reduce_sum.108
  327.2 1.2 reshape.73
  328.4 4.8 %all-to-all-start.5 = ((bf16[32,4,4096]{2,1,0:T(4,128)(2,1)}), bf16[32,4,4096]{2,1,0:T(4,128)(2,1)S(1)}, u32[]{:S(2)}, u32[]{:S(2)}) async-start(bf16[32,4,4096]{2,1,0:T(4,128)(2,1)} %reshape.73), calls=%async_computation.5 | async-start | bytes 2097152 | tf_op jit(solution)/shard_map/all_to_all | solution.py:74
  333.4 17.0 %all-to-all-done.5 = bf16[32,4,4096]{2,1,0:T(4,128)(2,1)S(1)} async-done(((bf16[32,4,4096]{2,1,0:T(4,128)(2,1)}), bf16[32,4,4096]{2,1,0:T(4,128)(2,1)S(1)}, u32[]{:S(2)}, u32[]{:S(2)}) %all-to-all-start.5) | async-done | bytes 1048608 | tf_op jit(solution)/shard_map/all_to_all | solution.py:74
  352.9 6.9 %all-reduce.4 = (f32[16]{0:T(128)S(1)}, f32[16]{0:T(128)S(1)}) all-reduce(f32[16]{0:T(128)S(1)} %convert_reduce_fusion.2, f32[16]{0:T(128)S(1)} %convolution_bitcast_fusion), channel_id=1, replica_groups=mesh['dp'=4,'expert_0'=4,'expert_1'=4,'expert_2'=2] {'dp'}, use_global_device_ids=true, to_apply=%region_24.26 | all-reduce | flops 32 | bytes 256 | tf_op jit(solution)/shard_map/psum | solution.py:29
  359.8 6.5 %all-reduce.2 = (f32[16]{0:T(128)S(1)}, f32[16]{0:T(128)S(1)}) all-reduce(f32[16]{0:T(128)S(1)} %get-tuple-element.11, f32[16]{0:T(128)S(1)} %get-tuple-element.12), channel_id=1, replica_groups=mesh['dp'=4,'expert_0'=4,'expert_1'=4,'expert_2'=2] {'expert_0'}, use_global_device_ids=true, to_apply=%region_25.27 | all-reduce | flops 32 | bytes 256 | tf_op jit(solution)/shard_map/psum | solution.py:29
  366.3 7.8 %all-reduce = (f32[16]{0:T(128)S(1)}, f32[16]{0:T(128)S(1)}) all-reduce(f32[16]{0:T(128)S(1)} %get-tuple-element.7, f32[16]{0:T(128)S(1)} %get-tuple-element.8), channel_id=1, replica_groups=mesh['dp'=4,'expert_0'=4,'expert_1'=4,'expert_2'=2] {'expert_1'}, use_global_device_ids=true, to_apply=%region_26.28 | all-reduce | flops 32 | bytes 256 | tf_op jit(solution)/shard_map/psum | solution.py:29
  374.1 7.4 %all-reduce.6 = (f32[16]{0:T(128)S(1)}, f32[16]{0:T(128)S(1)}) all-reduce(f32[16]{0:T(128)S(1)} %get-tuple-element.3, f32[16]{0:T(128)S(1)} %get-tuple-element.4), channel_id=1, replica_groups=mesh['dp'=4,'expert_0'=4,'expert_1'=4,'expert_2'=2] {'expert_2'}, use_global_device_ids=true, to_apply=%region_27.29 | all-reduce | flops 32 | bytes 256 | tf_op jit(solution)/shard_map/psum | solution.py:29
  382.1 1.1 pad_maximum_fusion
  (44 shorter events, 9.3 us)
Async XLA Ops:
  7.2 77.1 %all-gather.3.cloned.1.call-start = ((), (), s32[]{:S(2)}) async-start(), calls=%async_computation.6 | async-start | bytes 5242880 | tf_op jit(solution)/shard_map/all_gather | solution.py:63
  10.3 28.8 %copy-start.1 = (s32[2,64]{1,0:T(2,128)S(1)}, s32[2,64]{1,0:T(2,128)}, u32[]{:S(2)}) copy-start(s32[2,64]{1,0:T(2,128)} %param.8) | copy-start | bytes 1540
  10.4 28.8 %copy-start = (bf16[2,64,4096]{2,1,0:T(8,128)(2,1)S(1)}, bf16[2,64,4096]{2,1,0:T(8,128)(2,1)}, u32[]{:S(2)}) copy-start(bf16[2,64,4096]{2,1,0:T(8,128)(2,1)} %param.7) | copy-start | bytes 3145732
  38.7 202.9 %all-gather.5.cloned.1.call-start = ((), (), s32[]{:S(2)}) async-start(), calls=%async_computation.7 | async-start | bytes 5242880 | tf_op jit(solution)/shard_map/all_gather | solution.py:63
  184.2 25.2 %all-to-all-start.2 = ((bf16[32,4,4096]{2,1,0:T(4,128)(2,1)}), bf16[32,4,4096]{2,1,0:T(4,128)(2,1)S(1)}, u32[]{:S(2)}, u32[]{:S(2)}) async-start(bf16[32,4,4096]{2,1,0:T(4,128)(2,1)} %reshape.67), calls=%async_computation.2 | async-start | bytes 2097152 | tf_op jit(solution)/shard_map/all_to_all | solution.py:74
  241.6 11.6 %copy-start.2 = (bf16[512,4096]{1,0:T(8,128)(2,1)S(1)}, bf16[512,4096]{1,0:T(8,128)(2,1)}, u32[]{:S(2)}) copy-start(bf16[512,4096]{1,0:T(8,128)(2,1)} %all-gather.5.cloned.1.call-done) | copy-start | bytes 12582916
  270.7 53.5 %all-to-all-start.4 = ((bf16[4,128,4096]{2,1,0:T(8,128)(2,1)}), bf16[4,128,4096]{2,1,0:T(8,128)(2,1)}, u32[]{:S(2)}, u32[]{:S(2)}) async-start(bf16[4,128,4096]{2,1,0:T(8,128)(2,1)} %bitcast.81), calls=%async_computation.4 | async-start | bytes 8388608 | tf_op jit(solution)/shard_map/all_to_all | solution.py:24
  328.4 22.0 %all-to-all-start.5 = ((bf16[32,4,4096]{2,1,0:T(4,128)(2,1)}), bf16[32,4,4096]{2,1,0:T(4,128)(2,1)S(1)}, u32[]{:S(2)}, u32[]{:S(2)}) async-start(bf16[32,4,4096]{2,1,0:T(4,128)(2,1)} %reshape.73), calls=%async_computation.5 | async-start | bytes 2097152 | tf_op jit(solution)/shard_map/all_to_all | solution.py:74
Sparse Core Ops, SparseCore 0:
  38.8 45.4 all-gather.2
  86.5 73.8 all-gather.4
where the time goes:
time: 391 us; the launch traced here: 390 us
  blocking collectives  173 us (44%)
  waiting for transfers between devices  105 us (27%)
  matrix products  58.1 us (15%)
  starting transfers between devices  17.8 us (5%)
  between operations  14.3 us (4%)
  other arithmetic  11.5 us (3%)
  local copies, waits for them, and re-layouts  9.91 us (3%)
    all_to_all x1, blocking collectives, summed_on_arrival(): lax.all_to_all(cut_along(shard, dim, devices), axis, 0, 0, tiled=True)  68.4 us
    psum x8, blocking collectives, by_axis(): return functools.reduce(lax.psum, axes, shard)  57.9 us
    all_to_all x1, waiting for transfers between devices, summed_on_arrival(): lax.all_to_all(cut_along(shard, dim, devices), axis, 0, 0, tiled=True)  48.5 us
    all_to_all x2, blocking collectives, body(): lax.all_to_all(sending_all, EXPERT, split_axis=0, concat_axis=0, tiled=True)  47.1 us
    all_to_all x2, waiting for transfers between devices, body(): lax.all_to_all(halves, EXPERT, split_axis=0, concat_axis=0, tiled=True)  33.9 us
    dot_general x2, matrix products, body(): jnp.dot(hidden, down_local, preferred_element_type=jnp.float32)  26.5 us
    all_gather x2, waiting for transfers between devices, body(): rows_in = lax.all_gather(flat_rows, 'dp', axis=0, tiled=True)  22.4 us
    dot_general x2, matrix products, body(): gate_vals = jnp.dot(rows_in, gate_local, preferred_element_type=jnp.float32)  21.4 us
  transfers between devices with their start and end apart: 5, of which 4 were waited for; matrix products, arithmetic and copies ran while one was open for 10% of the time, Pallas kernels for 0%

commit v1 on v0

v1 whole, which is shorter than its diff:
```python
import functools

import jax
import jax.numpy as jnp
from jax import lax
from jax.experimental import pallas as pl
from jax.experimental.pallas import tpu as pltpu
from jax.sharding import Mesh
from jax.sharding import PartitionSpec as P

X = "dp"
PLANE = ("expert_0", "expert_1")
CORE = "expert_2"
EXPERT = ("expert_0", "expert_1", "expert_2")
DP_EXPERT = ("dp", "expert_0", "expert_1", "expert_2")
STAT = 128
MIB = 1 << 20

clip_target = 2.0


WHOLE = pl.BlockSpec(memory_space=pltpu.VMEM)
SCALAR = pl.BlockSpec(memory_space=pltpu.SMEM)
HBM = pl.BlockSpec(memory_space=pltpu.HBM)
f32 = jnp.float32
bf16 = jnp.bfloat16


def along_x(v, sign):
    n = lax.axis_size(X)
    pairs = []
    for i in range(n):
        pairs.append((2 * i, 2 * ((i + sign) % n)))
        pairs.append((2 * i + 1, 2 * ((i - sign) % n) + 1))
    return lax.ppermute(v, (X, CORE), pairs)


def swap_core(v):
    return lax.ppermute(v, CORE, [(0, 1), (1, 0)])


def line_sum(v):
    v = v + swap_core(v)
    v = v + lax.ppermute(v, X, [(0, 1), (1, 0), (2, 3), (3, 2)])
    return v + lax.ppermute(v, X, [(0, 3), (3, 0), (1, 2), (2, 1)])


def call(kernel, out_shape, limit, *args, scratch=(), specs=None):
    return pl.pallas_call(
        kernel,
        in_specs=specs or [WHOLE] * len(args),
        out_specs=[WHOLE] * len(out_shape),
        out_shape=out_shape,
        scratch_shapes=list(scratch),
        compiler_params=pltpu.CompilerParams(vmem_limit_bytes=limit),
    )(*args)


def shape_of(*dims, dtype=bf16):
    return jax.ShapeDtypeStruct(dims, dtype)


def load_kernel(*refs):
    n = len(refs) // 2
    sems = refs[-1]
    copies = [pltpu.make_async_copy(refs[i], refs[n + i], sems.at[i]) for i in range(n)]
    for c in copies:
        c.start()
    for c in copies:
        c.wait()


def load(*weights):
    weights = [pltpu.with_memory_space_constraint(w, pltpu.HBM) for w in weights]
    return call(
        load_kernel,
        [pltpu.VMEM(w.shape, w.dtype) for w in weights],
        2 * MIB,
        *weights,
        specs=[HBM] * len(weights),
        scratch=[pltpu.SemaphoreType.DMA((len(weights),))],
    )


OVER_ROWS = (((0,), (0,)), ((), ()))


def pick(rows, cols, which, target):
    s = lax.broadcasted_iota(jnp.int32, (rows, cols), 0)
    slot = (s // 8) * 4 + s % 4
    hit = jnp.where((s // 4) % 2 == which, slot, -1) == target
    return jnp.where(hit, 1.0, 0.0).astype(bf16)


def positions(ids, experts):
    n = ids.shape[1]
    onehot = jnp.where(lax.broadcasted_iota(jnp.int32, (experts, n), 0) == ids, 1.0, 0.0)
    row = lax.broadcasted_iota(jnp.int32, (n, n), 0)
    col = lax.broadcasted_iota(jnp.int32, (n, n), 1)
    before = jnp.where(row < col, 1.0, 0.0).astype(bf16)
    earlier = jnp.dot(onehot.astype(bf16), before, preferred_element_type=f32)
    slot = jnp.sum(earlier * onehot, axis=0, keepdims=True).astype(jnp.int32)
    return ids * (n // experts) + slot


def pack_kernel(tokens, ids, sending, *, experts):
    micros, n, width = tokens.shape
    places = [pick(2 * n, n, m, positions(ids[m : m + 1, :], experts)) for m in range(micros)]
    for lo in range(0, width, 1024):
        at = slice(lo, lo + 1024)
        out = jnp.dot(places[0], tokens[0, :, at], preferred_element_type=f32)
        out = out + jnp.dot(places[1], tokens[1, :, at], preferred_element_type=f32)
        sending[:, at] = out.astype(bf16)
    ones = jnp.ones((n, STAT), bf16)
    fill = jnp.dot(places[0], ones, preferred_element_type=f32)
    fill = fill + jnp.dot(places[1], ones, preferred_element_type=f32)
    sending[:, width:] = fill.astype(bf16)


def pack(tokens, ids, experts):
    micros, n, width = tokens.shape
    return call(
        functools.partial(pack_kernel, experts=experts),
        [shape_of(micros * n, width + STAT)],
        8 * MIB,
        tokens,
        ids,
    )[0]


def split_kernel(arrived, *outs):
    *mine, counts = outs
    n, width = mine[0].shape
    rows = arrived.shape[0]
    for m, out in enumerate(mine):
        take = pick(rows, n, m, lax.broadcasted_iota(jnp.int32, (rows, n), 1))
        for lo in range(0, width, 1024):
            at = slice(lo, lo + 1024)
            out[:, at] = lax.dot_general(
                take, arrived[:, at], OVER_ROWS, preferred_element_type=f32
            ).astype(bf16)
    fill = arrived[:, width:].astype(f32)
    s = lax.broadcasted_iota(jnp.int32, fill.shape, 0)
    for m in range(len(mine)):
        count = jnp.sum(jnp.where((s // 4) % 2 == m, fill, 0.0), axis=0, keepdims=True)
        counts[m * 8 : m * 8 + 8, :] = jnp.broadcast_to(count, (8, STAT))


def split(arrived, micros, width):
    n = arrived.shape[0] // micros
    *mine, counts = call(
        split_kernel,
        [shape_of(n, width)] * micros + [shape_of(8 * micros, STAT, dtype=f32)],
        8 * MIB,
        arrived,
    )
    return mine, counts


def silu_mul(g, u):
    return (g / (1.0 + jnp.exp(-g)) * u).astype(bf16)


def gate_up_kernel(*refs, groups, keep):
    parts = refs[:groups]
    wg, wu = refs[groups : groups + 2]
    outs = refs[groups + 2 : -1]
    x = refs[-1]
    rows = parts[0].shape[0]
    for i, part in enumerate(parts):
        x[i * rows : (i + 1) * rows, :] = part[...]
    tile = 128

    def step(i, carry):
        at = pl.ds(pl.multiple_of(i * tile, tile), tile)
        w = jnp.concatenate([wg[0, :, at], wu[0, :, at]], axis=1)
        both = jnp.dot(x[...], w, preferred_element_type=f32)
        g = both[:, :tile]
        u = both[:, tile:]
        if keep:
            outs[0][:, at] = g
            outs[1][:, at] = u
        else:
            outs[0][:, at] = silu_mul(g, u)
        return carry

    lax.fori_loop(0, wg.shape[2] // tile, step, 0)


def gate_up(parts, w_gate, w_up, keep):
    rows, k = parts[0].shape
    dims = (len(parts) * rows, w_gate.shape[2])
    return call(
        functools.partial(gate_up_kernel, groups=len(parts), keep=keep),
        [shape_of(*dims, dtype=f32)] * 2 if keep else [shape_of(*dims)],
        14 * MIB,
        *parts,
        w_gate,
        w_up,
        scratch=[pltpu.VMEM((dims[0], k), bf16)],
    )


def down_kernel(*refs, groups, keep):
    if keep:
        clip = refs[0][0, 0]
        parts = refs[1 : 1 + 2 * groups]
        sizes = [parts[2 * i].shape[0] // 2 for i in range(groups)]
    else:
        parts = refs[:groups]
        sizes = [p.shape[0] // 2 for p in parts]
    w, *owns, oth, h = refs[int(keep) + len(parts) :]
    n = owns[0].shape[0]
    rows = oth.shape[0]
    at = 0
    for i, size in enumerate(sizes):
        for side in range(2):
            src = slice(side * size, (side + 1) * size)
            dst = slice(side * rows + at, side * rows + at + size)
            if keep:
                h[dst, :] = silu_mul(clip * parts[2 * i][src, :], clip * parts[2 * i + 1][src, :])
            else:
                h[dst, :] = parts[i][src, :]
        at += size
    tile = 512

    def step(i, carry):
        cols = pl.ds(pl.multiple_of(i * tile, tile), tile)
        y = jnp.dot(h[...], w[0, :, cols], preferred_element_type=f32)
        for j, own in enumerate(owns):
            own[:, cols] = y[j * n : (j + 1) * n]
        oth[:, cols] = y[rows:].astype(oth.dtype)
        return carry

    lax.fori_loop(0, w.shape[2] // tile, step, 0)


def down(groups, w_down, n, clip):
    keep = clip is not None
    rows = sum(g[0].shape[0] for g in groups) // 2
    k, width = w_down.shape[1:]
    args = [a for g in groups for a in g]
    specs = [WHOLE] * (len(args) + 1)
    if keep:
        args = [clip] + args
        specs = [SCALAR] + specs
    return call(
        functools.partial(down_kernel, groups=len(groups), keep=keep),
        [shape_of(n, width, dtype=f32)] * (rows // n) + [shape_of(rows, width)],
        12 * MIB,
        *args,
        w_down,
        scratch=[pltpu.VMEM((2 * rows, k), bf16)],
        specs=specs,
    )


def finish_kernel(own, other, near_a, near_b, counts, *outs, micro, last):
    n, width = own.shape
    half = width // 2
    tile = 512
    rows = 2 * n
    places = [pick(rows, n, h, lax.broadcasted_iota(jnp.int32, (rows, n), 1)) for h in range(2)]

    def step(i, total):
        out = None
        for h in range(2):
            cols = pl.ds(pl.multiple_of(h * half + i * tile, tile), tile)
            fin = own[:, cols] + other[:n, cols].astype(f32)
            fin = fin + (near_a[:, cols].astype(f32) + near_b[:, cols].astype(f32))
            part = jnp.dot(places[h], fin.astype(bf16), preferred_element_type=f32)
            out = part if out is None else out + part
            sq = fin * fin
            for j in range(0, tile, STAT):
                total = total + sq[:, j : j + STAT]
        outs[0][:, pl.ds(pl.multiple_of(i * tile, tile), tile)] = out.astype(bf16)
        return total

    total = lax.fori_loop(0, half // tile, step, jnp.zeros((n, STAT), f32))
    total = jnp.sum(jnp.sum(total, axis=0, keepdims=True), axis=1, keepdims=True)
    count = counts[micro * 8 : micro * 8 + 1, :1]
    if last:
        total = jnp.broadcast_to(total, (rows, STAT))
        lane = lax.broadcasted_iota(jnp.int32, (rows, STAT), 1)
        high = total.astype(bf16).astype(f32)
        middle = (total - high).astype(bf16).astype(f32)
        low = total - high - middle
        stats = jnp.where(lane == 0, high, jnp.where(lane == 1, middle, low))
        stats = jnp.where(lane < 3, stats, jnp.where(lane == 3, count, 0.0))
        outs[0][:, half:] = stats.astype(bf16)
    else:
        lane = lax.broadcasted_iota(jnp.int32, (8, STAT), 1)
        total = jnp.broadcast_to(total, (8, STAT))
        outs[1][...] = jnp.where(lane == 0, total, jnp.where(lane == 1, count, 0.0))


def finish(own, other, near_a, near_b, counts, micro, last):
    n, width = own.shape
    half = width // 2
    if last:
        outs = [shape_of(2 * n, half + STAT)]
    else:
        outs = [shape_of(2 * n, half), shape_of(8, STAT, dtype=f32)]
    return call(
        functools.partial(finish_kernel, micro=micro, last=last),
        outs,
        10 * MIB,
        own,
        other,
        near_a,
        near_b,
        counts,
    )


def unpack_kernel(*refs, experts):
    *backs, ids, out = refs
    n, width = out.shape[1:]
    half = width // 2
    for m, back in enumerate(backs):
        position = positions(ids[m : m + 1, :], experts)
        for h in range(2):
            take = pick(2 * n, n, h, position)
            for lo in range(0, half, 1024):
                out[m, :, h * half + lo : h * half + lo + 1024] = lax.dot_general(
                    take, back[:, lo : lo + 1024], OVER_ROWS, preferred_element_type=f32
                ).astype(bf16)


def exchange(v):
    experts = lax.axis_size(PLANE)
    rows, width = v.shape
    out = lax.all_to_all(v.reshape(experts, rows // experts, width), PLANE, 0, 0, tiled=True)
    return out.reshape(rows, width)


def body(tokens, expert_of, w_gate, w_up, w_down):
    micros, n, width = tokens.shape
    experts = lax.axis_size(PLANE)
    tie = lax.optimization_barrier

    def clip_of(sumsq, count):
        return jnp.minimum(
            1.0, clip_target / jnp.sqrt((sumsq + width) / (width * (count + 1.0)))
        )

    arrived = exchange(pack(tokens, expert_of, experts))
    mine, counts = split(arrived, micros, width)
    w_gate, w_up, w_down = load(w_gate, w_up, w_down)

    def spread_near(m):
        a = along_x(mine[m], 1)
        b = along_x(mine[m], -1)
        o = swap_core(mine[m])
        own = gate_up([mine[m], o], w_gate, w_up, m > 0)
        return a, b, own

    def spread_far(m, a, b):
        far = along_x(a, 1)
        ao = swap_core(a)
        bo = swap_core(b)
        near = gate_up([a, b, ao, bo], w_gate, w_up, m > 0)
        return far, near

    def spread_last(m, far):
        return gate_up([far, swap_core(far)], w_gate, w_up, m > 0)

    def collect(m, own, near, far, clip, fill_in):
        mid, send_far = down([far], w_down, n, clip)
        mid = mid + swap_core(send_far).astype(f32)
        relay = along_x(mid.astype(bf16), 1)
        mine_o, a_o, b_o, send = down([own, near], w_down, n, clip)
        got = swap_core(send)
        to_a = (a_o + got[n : 2 * n].astype(f32)).astype(bf16)
        from_b = along_x(to_a, -1)
        got_b, relay = tie((got, relay))
        to_b = (b_o + got_b[2 * n :].astype(f32) + relay.astype(f32)).astype(bf16)
        from_a = along_x(to_b, 1)
        from_a, from_b, extra = fill_in(from_a, from_b)
        last = m + 1 == micros
        return finish(mine_o, got, from_a, from_b, counts, m, last), extra

    a0, b0, own0 = spread_near(0)
    far0, near0 = spread_far(0, a0, b0)
    mine[1], near0 = tie((mine[1], near0))
    a1, b1, own1 = spread_near(1)
    far0 = spread_last(0, far0)

    def gates_of_1(from_a, from_b):
        ao = swap_core(a1)
        bo = swap_core(b1)
        near1 = gate_up([a1, b1, ao, bo], w_gate, w_up, True)
        from_a, from_b, near1, a = tie((from_a, from_b, near1, a1))
        far1 = along_x(a, 1)
        return from_a, from_b, (near1, far1)

    (out0, stats), (near1, far1) = collect(0, own0, near0, far0, None, gates_of_1)
    stats = line_sum(stats)
    far1 = spread_last(1, far1)
    clip = clip_of(stats[:1, :1], stats[:1, 1:2])

    def return_0(from_a, from_b):
        back = exchange(out0)
        from_a, from_b, back = tie((from_a, from_b, back))
        return from_a, from_b, back

    (out1,), back0 = collect(1, own1, near1, far1, clip, return_0)
    back1 = exchange(out1)
    got = line_sum(back1[:: 2 * n // experts, width // 2 :].astype(f32))
    scale = clip_of(got[:, 0] + got[:, 1] + got[:, 2], got[:, 3])
    (out,) = call(
        functools.partial(unpack_kernel, experts=experts),
        [shape_of(micros, n, width)],
        8 * MIB,
        back0,
        back1[:, : width // 2],
        expert_of,
    )
    return out, scale


def solution(mesh):
    finer = Mesh(
        mesh.devices.reshape(mesh.shape["dp"], 4, 4, 2), ("dp", "expert_0", "expert_1", "expert_2")
    )
    placed = (
        P(None, DP_EXPERT, None),
        P(None, DP_EXPERT),
        P(EXPERT, None, "dp"),
        P(EXPERT, None, "dp"),
        P(EXPERT, "dp", None),
    )
    return jax.shard_map(
        body,
        mesh=finer,
        in_specs=placed,
        out_specs=(P(None, DP_EXPERT, None), P()),
        check_vma=False,
    )
```

time: 391 us -> 213 us (0.54)
  blocking collectives: 173 us -> 52.6 us
  matrix products: 58.1 us -> 0 us
  Pallas kernels: 0 us -> 52.1 us
  waiting for transfers between devices: 105 us -> 64.3 us
  starting transfers between devices: 17.8 us -> 35.8 us
  between operations: 14.3 us -> 2.25 us
  other arithmetic: 11.5 us -> 1.52 us
  local copies, waits for them, and re-layouts: 9.91 us -> 2.56 us
    all_to_all x3 -> x0, waiting for transfers between devices: 82.4 us -> none  [the longest x1 48.5 us: summed_on_arrival(): lax.all_to_all(cut_along(shard, dim, devices), axis, 0, 0, tiled=True)]
    ppermute x0 -> x30, waiting for transfers between devices: none -> 64.3 us  [the longest x12 54.2 us: along_x(): return lax.ppermute(v, (X, CORE), pairs)]
    all_to_all x3, blocking collectives: 116 us -> 52.6 us  [exchange(): lax.all_to_all(v.reshape(experts, rows // experts, width), PLANE, 0, 0, t...]
    dot_general x9 -> x0, matrix products: 58.1 us -> none  [the longest x2 26.5 us: body(): jnp.dot(hidden, down_local, preferred_element_type=jnp.float32)]
    psum x8 -> x0, blocking collectives: 57.9 us -> none  [by_axis(): return functools.reduce(lax.psum, axes, shard)]
    pallas_call x0 -> x16, Pallas kernels: none -> 52.1 us  [call(): pl.pallas_call(kernel, in_specs=specs or [WHOLE] * len(args), out_specs=[...]
    ppermute x0 -> x30, starting transfers between devices: none -> 35.8 us  [the longest x14 21.7 us: swap_core(): return lax.ppermute(v, CORE, [(0, 1), (1, 0)])]
    all_gather x2 -> x0, waiting for transfers between devices: 22.4 us -> none  [body(): rows_in = lax.all_gather(flat_rows, 'dp', axis=0, tiled=True)]
  transfers between devices with their start and end apart: 5 -> 30, of which waited for: 4 -> 15; matrix products, arithmetic and copies ran while one was open for 10% -> 1% of each run, Pallas kernels for 0% -> 24%
where the time goes in v1:
time: 213 us; the launch traced here: 211 us
  waiting for transfers between devices  64.3 us (30%)
  blocking collectives  52.6 us (25%)
  Pallas kernels  52.1 us (24%)
  starting transfers between devices  35.8 us (17%)
  local copies, waits for them, and re-layouts  2.56 us (1%)
  between operations  2.25 us (1%)
    ppermute x12, waiting for transfers between devices, along_x(): return lax.ppermute(v, (X, CORE), pairs)  54.2 us
    all_to_all x3, blocking collectives, exchange(): lax.all_to_all(v.reshape(experts, rows // experts, width), PLANE, 0, 0, t...  52.6 us
    pallas_call x16, Pallas kernels, call(): pl.pallas_call(kernel, in_specs=specs or [WHOLE] * len(args), out_specs=[...  52.1 us
    ppermute x14, starting transfers between devices, swap_core(): return lax.ppermute(v, CORE, [(0, 1), (1, 0)])  21.7 us
    ppermute x12, starting transfers between devices, along_x(): return lax.ppermute(v, (X, CORE), pairs)  13.2 us
    ppermute x2, waiting for transfers between devices, line_sum(): v = v + lax.ppermute(v, X, [(0, 1), (1, 0), (2, 3), (3, 2)])  4.68 us
  transfers between devices with their start and end apart: 30, of which 15 were waited for; matrix products, arithmetic and copies ran while one was open for 1% of the time, Pallas kernels for 24%

profile of v1, /device:TPU:1, one launch (start us, length us, event | category | flops | bytes accessed | tf_op | source)
XLA Modules:
  0.0 211.1 jit_solution(3615377030794563778)
XLA Ops:
  3.4 25.2 %all_to_all.15 = bf16[16,8,4224]{2,1,0:T(8,128)(2,1)S(1)} all-to-all(bf16[16,8,4224]{2,1,0:T(8,128)(2,1)S(1)} %bitcast.7), channel_id=1, replica_groups=mesh['dp'=4,'expert_0'=4,'expert_1'=4,'expert_2'=2] {'expert_0','expert_1'}, dimensions={0} | all-to-all | bytes 2162688 | tf_op jit(solution)/shard_map/all_to_all | solution.py:333
  29.1 2.5 %collective-permute-start.1 = (bf16[64,4096]{1,0:T(8,128)(2,1)S(1)}, bf16[64,4096]{1,0:T(8,128)(2,1)S(1)}, u32[]{:S(2)}, u32[]{:S(2)}) collective-permute-start(bf16[64,4096]{1,0:T(8,128)(2,1)S(1)} %get-tuple-element.42.refs_0_), channel_id=1, source_target_pairs={{0,32},{1,97},{32,64},{33,1},{64,96},{65,33},{96,0},{97,65},{2,34}... | collective-permute-start | bytes 1572872 | tf_op jit(solution)/shard_map/ppermute | solution.py:35
  31.6 6.1 %collective-permute-done.1.refs_0_ = bf16[64,4096]{1,0:T(8,128)(2,1)S(1)} collective-permute-done((bf16[64,4096]{1,0:T(8,128)(2,1)S(1)}, bf16[64,4096]{1,0:T(8,128)(2,1)S(1)}, u32[]{:S(2)}, u32[]{:S(2)}) %collective-permute-start.1) | collective-permute-done | bytes 524320 | tf_op jit(solution)/shard_map/ppermute | solution.py:35
  37.7 3.1 %collective-permute-start.6 = (bf16[64,4096]{1,0:T(8,128)(2,1)S(1)}, bf16[64,4096]{1,0:T(8,128)(2,1)S(1)}, u32[]{:S(2)}, u32[]{:S(2)}) collective-permute-start(bf16[64,4096]{1,0:T(8,128)(2,1)S(1)} %collective-permute-done.1.refs_0_), channel_id=1, source_target_pairs={{0,32},{1,97},{32,64},{33,1},{64,96},{65,33},{96,0},{97,65},{2,34}... | collective-permute-start | bytes 1572872 | tf_op jit(solution)/shard_map/ppermute | solution.py:35
  40.9 7.9 %collective-permute-done.6.refs_0_ = bf16[64,4096]{1,0:T(8,128)(2,1)S(1)} collective-permute-done((bf16[64,4096]{1,0:T(8,128)(2,1)S(1)}, bf16[64,4096]{1,0:T(8,128)(2,1)S(1)}, u32[]{:S(2)}, u32[]{:S(2)}) %collective-permute-start.6) | collective-permute-done | bytes 524320 | tf_op jit(solution)/shard_map/ppermute | solution.py:35
  48.7 7.7 %collective-permute-start.7 = (bf16[64,4096]{1,0:T(8,128)(2,1)S(1)}, bf16[64,4096]{1,0:T(8,128)(2,1)S(1)}, u32[]{:S(2)}, u32[]{:S(2)}) collective-permute-start(bf16[64,4096]{1,0:T(8,128)(2,1)S(1)} %collective-permute-done.6.refs_0_), channel_id=1, source_target_pairs={{0,1},{1,0},{2,3},{3,2},{4,5},{5,4},{6,7},{7,6},{8,9},{9,8},{10,11... | collective-permute-start | bytes 1572872 | tf_op jit(solution)/shard_map/ppermute | solution.py:39
  56.9 7.3 %shard_map.70 = (bf16[1,4096,896]{2,1,0:T(8,128)(2,1)S(1)}, bf16[1,4096,896]{2,1,0:T(8,128)(2,1)S(1)}, bf16[1,896,4096]{2,1,0:T(8,128)(2,1)S(1)}) custom-call(bf16[1,4096,896]{2,1,0:T(8,128)(2,1)} %refs_0_.1, bf16[1,4096,896]{2,1,0:T(8,128)(2,1)} %refs_1_.1, bf16[1,896,4096]{2,1,0:T(8,128)(2,1)} %refs_2_.2), custom_call_target="tpu_custom_call" | custom-call | tf_op jit(solution)/shard_map/pallas_call | solution.py:49
  64.2 3.5 %shard_map.74.refs_0_ = bf16[128,896]{1,0:T(8,128)(2,1)S(1)} custom-call(bf16[64,4096]{1,0:T(8,128)(2,1)S(1)} %collective-permute-done.6.refs_0_, bf16[64,4096]{1,0:T(8,128)(2,1)S(1)} %collective-permute-done.7.refs_1_, bf16[1,4096,896]{2,1,0:T(8,128)(2,1)S(1)} %get-tuple-element.43.refs_2_.refs_4_, bf16[1,4096,896]{2,1,0:T(8,128)(2,1)S(1)} %get-tuple-element.44.refs_3_.refs_5_), custom_call_target="tpu_custom_call" | custom-call | tf_op jit(solution)/shard_map/pallas_call | solution.py:49
  67.7 2.5 %shard_map.75 = (f32[64,4096]{1,0:T(8,128)S(1)}, bf16[64,4096]{1,0:T(8,128)(2,1)S(1)}) custom-call(bf16[128,896]{1,0:T(8,128)(2,1)S(1)} %shard_map.74.refs_0_, bf16[1,896,4096]{2,1,0:T(8,128)(2,1)S(1)} %get-tuple-element.47.refs_2_.refs_1_.refs_5_.refs_3_), custom_call_target="tpu_custom_call" | custom-call | tf_op jit(solution)/shard_map/pallas_call | solution.py:49
  70.9 3.5 %shard_map.71.refs_0_ = bf16[128,896]{1,0:T(8,128)(2,1)S(1)} custom-call(bf16[64,4096]{1,0:T(8,128)(2,1)S(1)} %get-tuple-element.42.refs_0_, bf16[64,4096]{1,0:T(8,128)(2,1)S(1)} %collective-permute-done.refs_1_, bf16[1,4096,896]{2,1,0:T(8,128)(2,1)S(1)} %get-tuple-element.43.refs_2_.refs_4_, bf16[1,4096,896]{2,1,0:T(8,128)(2,1)S(1)} %get-tuple-element.44.refs_3_.refs_5_), custom_call_target="tpu_custom_call" | custom-call | tf_op jit(solution)/shard_map/pallas_call | solution.py:49
  74.4 5.4 %shard_map.72.refs_1_ = bf16[256,896]{1,0:T(8,128)(2,1)S(1)} custom-call(bf16[64,4096]{1,0:T(8,128)(2,1)S(1)} %collective-permute-done.1.refs_0_, bf16[64,4096]{1,0:T(8,128)(2,1)S(1)} %collective-permute-done.2.refs_1_, bf16[64,4096]{1,0:T(8,128)(2,1)S(1)} %collective-permute-done.3.refs_2_, bf16[64,4096]{1,0:T(8,128)(2,1)S(1)} %collective-permute-done.4.refs_3_, ...), custom_call_target="tpu_custom_call" | custom-call | tf_op jit(solution)/shard_map/pallas_call | solution.py:49
  79.8 4.7 %shard_map.73 = (f32[64,4096]{1,0:T(8,128)S(1)}, f32[64,4096]{1,0:T(8,128)S(1)}, f32[64,4096]{1,0:T(8,128)S(1)}, bf16[192,4096]{1,0:T(8,128)(2,1)S(1)}) custom-call(bf16[128,896]{1,0:T(8,128)(2,1)S(1)} %shard_map.71.refs_0_, bf16[256,896]{1,0:T(8,128)(2,1)S(1)} %shard_map.72.refs_1_, bf16[1,896,4096]{2,1,0:T(8,128)(2,1)S(1)} %get-tuple-element.47.refs_2_.refs_1_.refs_5_.refs_3_), custom_call_target="tpu_custom_call" | custom-call | tf_op jit(solution)/shard_map/pallas_call | solution.py:49
  87.6 10.1 %collective-permute-done.12.refs_0_ = bf16[64,4096]{1,0:T(8,128)(2,1)S(1)} collective-permute-done((bf16[64,4096]{1,0:T(8,128)(2,1)S(1)}, bf16[64,4096]{1,0:T(8,128)(2,1)S(1)}, u32[]{:S(2)}, u32[]{:S(2)}) %collective-permute-start.12) | collective-permute-done | bytes 524320 | tf_op jit(solution)/shard_map/ppermute | solution.py:35
  97.7 2.6 %collective-permute-start.14 = (bf16[64,4096]{1,0:T(8,128)(2,1)S(1)}, bf16[64,4096]{1,0:T(8,128)(2,1)S(1)}, u32[]{:S(2)}, u32[]{:S(2)}) collective-permute-start(bf16[64,4096]{1,0:T(8,128)(2,1)S(1)} %collective-permute-done.12.refs_0_), channel_id=1, source_target_pairs={{0,1},{1,0},{2,3},{3,2},{4,5},{5,4},{6,7},{7,6},{8,9},{9,8},{10,11... | collective-permute-start | bytes 1572872 | tf_op jit(solution)/shard_map/ppermute | solution.py:39
  100.6 3.6 %collective-permute-done.9 = bf16[64,4096]{1,0:T(8,128)(2,1)S(1)} collective-permute-done((bf16[64,4096]{1,0:T(8,128)(2,1)S(1)}, bf16[64,4096]{1,0:T(8,128)(2,1)S(1)}, u32[]{:S(2)}, u32[]{:S(2)}) %collective-permute-start.9) | collective-permute-done | bytes 524320 | tf_op jit(solution)/shard_map/ppermute | solution.py:35
  106.1 5.3 %shard_map.76 = (f32[256,896]{1,0:T(8,128)S(1)}, f32[256,896]{1,0:T(8,128)S(1)}) custom-call(bf16[64,4096]{1,0:T(8,128)(2,1)S(1)} %collective-permute-done.12.refs_0_, bf16[64,4096]{1,0:T(8,128)(2,1)S(1)} %collective-permute-done.13.refs_1_, bf16[64,4096]{1,0:T(8,128)(2,1)S(1)} %collective-permute-done.14.refs_2_, ...), custom_call_target="tpu_custom_call" | custom-call | tf_op jit(solution)/shard_map/pallas_call | solution.py:49
  111.4 4.7 %collective-permute-done.10.near_a = bf16[64,4096]{1,0:T(8,128)(2,1)S(1)} collective-permute-done((bf16[64,4096]{1,0:T(8,128)(2,1)S(1)}, bf16[64,4096]{1,0:T(8,128)(2,1)S(1)}, u32[]{:S(2)}, u32[]{:S(2)}) %collective-permute-start.10) | collective-permute-done | bytes 524320 | tf_op jit(solution)/shard_map/ppermute | solution.py:35
  116.1 3.6 %collective-permute-done.11.near_b = bf16[64,4096]{1,0:T(8,128)(2,1)S(1)} collective-permute-done((bf16[64,4096]{1,0:T(8,128)(2,1)S(1)}, bf16[64,4096]{1,0:T(8,128)(2,1)S(1)}, u32[]{:S(2)}, u32[]{:S(2)}) %collective-permute-start.11) | collective-permute-done | bytes 524320 | tf_op jit(solution)/shard_map/ppermute | solution.py:35
  121.1 6.9 %collective-permute-done.21.refs_0_ = bf16[64,4096]{1,0:T(8,128)(2,1)S(1)} collective-permute-done((bf16[64,4096]{1,0:T(8,128)(2,1)S(1)}, bf16[64,4096]{1,0:T(8,128)(2,1)S(1)}, u32[]{:S(2)}, u32[]{:S(2)}) %collective-permute-start.21) | collective-permute-done | bytes 524320 | tf_op jit(solution)/shard_map/ppermute | solution.py:35
  128.0 3.5 %collective-permute-start.22 = (bf16[64,4096]{1,0:T(8,128)(2,1)S(1)}, bf16[64,4096]{1,0:T(8,128)(2,1)S(1)}, u32[]{:S(2)}, u32[]{:S(2)}) collective-permute-start(bf16[64,4096]{1,0:T(8,128)(2,1)S(1)} %collective-permute-done.21.refs_0_), channel_id=1, source_target_pairs={{0,1},{1,0},{2,3},{3,2},{4,5},{5,4},{6,7},{7,6},{8,9},{9,8},{10,11... | collective-permute-start | bytes 1572872 | tf_op jit(solution)/shard_map/ppermute | solution.py:39
  133.8 2.5 %collective-permute-done.17 = f32[8,128]{1,0:T(8,128)S(1)} collective-permute-done((f32[8,128]{1,0:T(8,128)S(1)}, f32[8,128]{1,0:T(8,128)S(1)}, u32[]{:S(2)}, u32[]{:S(2)}) %collective-permute-start.17) | collective-permute-done | bytes 4128 | tf_op jit(solution)/shard_map/ppermute | solution.py:44
  136.3 3.4 %shard_map.78 = (f32[128,896]{1,0:T(8,128)S(1)}, f32[128,896]{1,0:T(8,128)S(1)}) custom-call(bf16[64,4096]{1,0:T(8,128)(2,1)S(1)} %get-tuple-element.56.refs_0_, bf16[64,4096]{1,0:T(8,128)(2,1)S(1)} %collective-permute-done.19.refs_1_, bf16[1,4096,896]{2,1,0:T(8,128)(2,1)S(1)} %get-tuple-element.43.refs_2_.refs_4_, ...), custom_call_target="tpu_custom_call" | custom-call | tf_op jit(solution)/shard_map/pallas_call | solution.py:49
  141.9 5.1 %shard_map.79 = (f32[64,4096]{1,0:T(8,128)S(1)}, f32[64,4096]{1,0:T(8,128)S(1)}, f32[64,4096]{1,0:T(8,128)S(1)}, bf16[192,4096]{1,0:T(8,128)(2,1)S(1)}) custom-call(f32[1,1]{1,0:T(1,128)S(6)} %min.6.refs_0_, f32[128,896]{1,0:T(8,128)S(1)} %get-tuple-element.63.refs_1_, f32[128,896]{1,0:T(8,128)S(1)} %get-tuple-element.64.refs_2_, ...), custom_call_target="tpu_custom_call" | custom-call | tf_op jit(solution)/shard_map/pallas_call | solution.py:49
  147.0 2.6 %collective-permute-start.20 = (bf16[192,4096]{1,0:T(8,128)(2,1)S(1)}, bf16[192,4096]{1,0:T(8,128)(2,1)S(1)}, u32[]{:S(2)}, u32[]{:S(2)}) collective-permute-start(bf16[192,4096]{1,0:T(8,128)(2,1)S(1)} %get-tuple-element.68), channel_id=1, source_target_pairs={{0,1},{1,0},{2,3},{3,2},{4,5},{5,4},{6,7},{7,6},{8,9},{9,8},{10,11... | collective-permute-start | bytes 4718600 | tf_op jit(solution)/shard_map/ppermute | solution.py:39
  149.6 3.4 %shard_map.80 = (f32[128,896]{1,0:T(8,128)S(1)}, f32[128,896]{1,0:T(8,128)S(1)}) custom-call(bf16[64,4096]{1,0:T(8,128)(2,1)S(1)} %collective-permute-done.21.refs_0_, bf16[64,4096]{1,0:T(8,128)(2,1)S(1)} %collective-permute-done.22.refs_1_, bf16[1,4096,896]{2,1,0:T(8,128)(2,1)S(1)} %get-tuple-element.43.refs_2_.refs_4_, ...), custom_call_target="tpu_custom_call" | custom-call | tf_op jit(solution)/shard_map/pallas_call | solution.py:49
  152.9 2.7 %shard_map.81 = (f32[64,4096]{1,0:T(8,128)S(1)}, bf16[64,4096]{1,0:T(8,128)(2,1)S(1)}) custom-call(f32[1,1]{1,0:T(1,128)S(6)} %min.6.refs_0_, f32[128,896]{1,0:T(8,128)S(1)} %get-tuple-element.70.refs_1_, f32[128,896]{1,0:T(8,128)S(1)} %get-tuple-element.71.refs_2_, bf16[1,896,4096]{2,1,0:T(8,128)(2,1)S(1)} %get-tuple-element.47.refs_2_.refs_1_.refs_5_.refs_3_), custom_call_target="tpu_custom_call" | custom-call | tf_op jit(solution)/shard_map/pallas_call | solution.py:49
  155.7 1.9 collective-permute-done.23
  159.6 11.4 %collective-permute-done.24 = bf16[64,4096]{1,0:T(8,128)(2,1)S(1)} collective-permute-done((bf16[64,4096]{1,0:T(8,128)(2,1)S(1)}, bf16[64,4096]{1,0:T(8,128)(2,1)S(1)}, u32[]{:S(2)}, u32[]{:S(2)}) %collective-permute-start.24) | collective-permute-done | bytes 524320 | tf_op jit(solution)/shard_map/ppermute | solution.py:35
  172.5 13.3 %all_to_all.16 = bf16[16,8,2048]{2,1,0:T(8,128)(2,1)S(1)} all-to-all(bf16[16,8,2048]{2,1,0:T(8,128)(2,1)S(1)} %bitcast.10), channel_id=1, replica_groups=mesh['dp'=4,'expert_0'=4,'expert_1'=4,'expert_2'=2] {'expert_0','expert_1'}, dimensions={0} | all-to-all | bytes 1048576 | tf_op jit(solution)/shard_map/all_to_all | solution.py:333
  187.0 14.1 %all_to_all.17 = bf16[16,8,2176]{2,1,0:T(8,128)(2,1)S(1)} all-to-all(bf16[16,8,2176]{2,1,0:T(8,128)(2,1)S(1)} %bitcast.8), channel_id=1, replica_groups=mesh['dp'=4,'expert_0'=4,'expert_1'=4,'expert_2'=2] {'expert_0','expert_1'}, dimensions={0} | all-to-all | bytes 1114112 | tf_op jit(solution)/shard_map/all_to_all | solution.py:333
  201.1 2.2 %collective-permute-start.27 = (f32[16,128]{1,0:T(8,128)S(1)}, f32[16,128]{1,0:T(8,128)S(1)}, u32[]{:S(2)}, u32[]{:S(2)}) collective-permute-start(f32[16,128]{1,0:T(8,128)S(1)} %convert_element_type.59), channel_id=1, source_target_pairs={{0,1},{1,0},{2,3},{3,2},{4,5},{5,4},{6,7},{7,6},{8,9},{9,8},{10,11... | collective-permute-start | bytes 24584 | tf_op jit(solution)/shard_map/ppermute | solution.py:39
  204.5 2.2 %collective-permute-done.28 = f32[16,128]{1,0:T(8,128)S(1)} collective-permute-done((f32[16,128]{1,0:T(8,128)S(1)}, f32[16,128]{1,0:T(8,128)S(1)}, u32[]{:S(2)}, u32[]{:S(2)}) %collective-permute-start.28) | collective-permute-done | bytes 8224 | tf_op jit(solution)/shard_map/ppermute | solution.py:44
  (70 shorter events, 24.7 us)
Async XLA Ops:
  0.6 1.2 copy-start
  29.1 8.7 %collective-permute-start.1 = (bf16[64,4096]{1,0:T(8,128)(2,1)S(1)}, bf16[64,4096]{1,0:T(8,128)(2,1)S(1)}, u32[]{:S(2)}, u32[]{:S(2)}) collective-permute-start(bf16[64,4096]{1,0:T(8,128)(2,1)S(1)} %get-tuple-element.42.refs_0_), channel_id=1, source_target_pairs={{0,32},{1,97},{32,64},{33,1},{64,96},{65,33},{96,0},{97,65},{2,34}... | collective-permute-start | bytes 1572872 | tf_op jit(solution)/shard_map/ppermute | solution.py:35
  37.7 11.0 %collective-permute-start.6 = (bf16[64,4096]{1,0:T(8,128)(2,1)S(1)}, bf16[64,4096]{1,0:T(8,128)(2,1)S(1)}, u32[]{:S(2)}, u32[]{:S(2)}) collective-permute-start(bf16[64,4096]{1,0:T(8,128)(2,1)S(1)} %collective-permute-done.1.refs_0_), channel_id=1, source_target_pairs={{0,32},{1,97},{32,64},{33,1},{64,96},{65,33},{96,0},{97,65},{2,34}... | collective-permute-start | bytes 1572872 | tf_op jit(solution)/shard_map/ppermute | solution.py:35
  40.9 16.1 %collective-permute-start.2 = (bf16[64,4096]{1,0:T(8,128)(2,1)S(1)}, bf16[64,4096]{1,0:T(8,128)(2,1)S(1)}, u32[]{:S(2)}, u32[]{:S(2)}) collective-permute-start(bf16[64,4096]{1,0:T(8,128)(2,1)S(1)} %get-tuple-element.42.refs_0_), channel_id=1, source_target_pairs={{0,96},{1,33},{32,0},{33,65},{64,32},{65,97},{96,64},{97,1},{2,98}... | collective-permute-start | bytes 1572872 | tf_op jit(solution)/shard_map/ppermute | solution.py:35
  48.7 15.5 %collective-permute-start.7 = (bf16[64,4096]{1,0:T(8,128)(2,1)S(1)}, bf16[64,4096]{1,0:T(8,128)(2,1)S(1)}, u32[]{:S(2)}, u32[]{:S(2)}) collective-permute-start(bf16[64,4096]{1,0:T(8,128)(2,1)S(1)} %collective-permute-done.6.refs_0_), channel_id=1, source_target_pairs={{0,1},{1,0},{2,3},{3,2},{4,5},{5,4},{6,7},{7,6},{8,9},{9,8},{10,11... | collective-permute-start | bytes 1572872 | tf_op jit(solution)/shard_map/ppermute | solution.py:39
  56.4 14.5 %collective-permute-start = (bf16[64,4096]{1,0:T(8,128)(2,1)S(1)}, bf16[64,4096]{1,0:T(8,128)(2,1)S(1)}, u32[]{:S(2)}, u32[]{:S(2)}) collective-permute-start(bf16[64,4096]{1,0:T(8,128)(2,1)S(1)} %get-tuple-element.42.refs_0_), channel_id=1, source_target_pairs={{0,1},{1,0},{2,3},{3,2},{4,5},{5,4},{6,7},{7,6},{8,9},{9,8},{10,11... | collective-permute-start | bytes 1572872 | tf_op jit(solution)/shard_map/ppermute | solution.py:39
  56.4 18.0 %collective-permute-start.3 = (bf16[64,4096]{1,0:T(8,128)(2,1)S(1)}, bf16[64,4096]{1,0:T(8,128)(2,1)S(1)}, u32[]{:S(2)}, u32[]{:S(2)}) collective-permute-start(bf16[64,4096]{1,0:T(8,128)(2,1)S(1)} %collective-permute-done.1.refs_0_), channel_id=1, source_target_pairs={{0,1},{1,0},{2,3},{3,2},{4,5},{5,4},{6,7},{7,6},{8,9},{9,8},{10,11... | collective-permute-start | bytes 1572872 | tf_op jit(solution)/shard_map/ppermute | solution.py:39
  56.9 17.5 %collective-permute-start.4 = (bf16[64,4096]{1,0:T(8,128)(2,1)S(1)}, bf16[64,4096]{1,0:T(8,128)(2,1)S(1)}, u32[]{:S(2)}, u32[]{:S(2)}) collective-permute-start(bf16[64,4096]{1,0:T(8,128)(2,1)S(1)} %collective-permute-done.2.refs_1_), channel_id=1, source_target_pairs={{0,1},{1,0},{2,3},{3,2},{4,5},{5,4},{6,7},{7,6},{8,9},{9,8},{10,11... | collective-permute-start | bytes 1572872 | tf_op jit(solution)/shard_map/ppermute | solution.py:39
  70.3 15.8 %collective-permute-start.8 = (bf16[64,4096]{1,0:T(8,128)(2,1)S(1)}, bf16[64,4096]{1,0:T(8,128)(2,1)S(1)}, u32[]{:S(2)}, u32[]{:S(2)}) collective-permute-start(bf16[64,4096]{1,0:T(8,128)(2,1)S(1)} %get-tuple-element.52), channel_id=1, source_target_pairs={{0,1},{1,0},{2,3},{3,2},{4,5},{5,4},{6,7},{7,6},{8,9},{9,8},{10,11... | collective-permute-start | bytes 1572872 | tf_op jit(solution)/shard_map/ppermute | solution.py:39
  84.5 16.1 %collective-permute-start.5 = (bf16[192,4096]{1,0:T(8,128)(2,1)S(1)}, bf16[192,4096]{1,0:T(8,128)(2,1)S(1)}, u32[]{:S(2)}, u32[]{:S(2)}) collective-permute-start(bf16[192,4096]{1,0:T(8,128)(2,1)S(1)} %get-tuple-element.49), channel_id=1, source_target_pairs={{0,1},{1,0},{2,3},{3,2},{4,5},{5,4},{6,7},{7,6},{8,9},{9,8},{10,11... | collective-permute-start | bytes 4718600 | tf_op jit(solution)/shard_map/ppermute | solution.py:39
  84.6 13.1 %collective-permute-start.12 = (bf16[64,4096]{1,0:T(8,128)(2,1)S(1)}, bf16[64,4096]{1,0:T(8,128)(2,1)S(1)}, u32[]{:S(2)}, u32[]{:S(2)}) collective-permute-start(bf16[64,4096]{1,0:T(8,128)(2,1)S(1)} %get-tuple-element.56.refs_0_), channel_id=1, source_target_pairs={{0,32},{1,97},{32,64},{33,1},{64,96},{65,33},{96,0},{97,65},{2,34}... | collective-permute-start | bytes 1572872 | tf_op jit(solution)/shard_map/ppermute | solution.py:35
  84.7 15.6 %collective-permute-start.13 = (bf16[64,4096]{1,0:T(8,128)(2,1)S(1)}, bf16[64,4096]{1,0:T(8,128)(2,1)S(1)}, u32[]{:S(2)}, u32[]{:S(2)}) collective-permute-start(bf16[64,4096]{1,0:T(8,128)(2,1)S(1)} %get-tuple-element.56.refs_0_), channel_id=1, source_target_pairs={{0,96},{1,33},{32,0},{33,65},{64,32},{65,97},{96,64},{97,1},{2,98}... | collective-permute-start | bytes 1572872 | tf_op jit(solution)/shard_map/ppermute | solution.py:35
  86.2 18.0 %collective-permute-start.9 = (bf16[64,4096]{1,0:T(8,128)(2,1)S(1)}, bf16[64,4096]{1,0:T(8,128)(2,1)S(1)}, u32[]{:S(2)}, u32[]{:S(2)}) collective-permute-start(bf16[64,4096]{1,0:T(8,128)(2,1)S(1)} %add_convert_fusion.5), channel_id=1, source_target_pairs={{0,32},{1,97},{32,64},{33,1},{64,96},{65,33},{96,0},{97,65},{2,34}... | collective-permute-start | bytes 1572872 | tf_op jit(solution)/shard_map/ppermute | solution.py:35
  97.7 8.4 %collective-permute-start.14 = (bf16[64,4096]{1,0:T(8,128)(2,1)S(1)}, bf16[64,4096]{1,0:T(8,128)(2,1)S(1)}, u32[]{:S(2)}, u32[]{:S(2)}) collective-permute-start(bf16[64,4096]{1,0:T(8,128)(2,1)S(1)} %collective-permute-done.12.refs_0_), channel_id=1, source_target_pairs={{0,1},{1,0},{2,3},{3,2},{4,5},{5,4},{6,7},{7,6},{8,9},{9,8},{10,11... | collective-permute-start | bytes 1572872 | tf_op jit(solution)/shard_map/ppermute | solution.py:39
  100.3 5.8 %collective-permute-start.15 = (bf16[64,4096]{1,0:T(8,128)(2,1)S(1)}, bf16[64,4096]{1,0:T(8,128)(2,1)S(1)}, u32[]{:S(2)}, u32[]{:S(2)}) collective-permute-start(bf16[64,4096]{1,0:T(8,128)(2,1)S(1)} %collective-permute-done.13.refs_1_), channel_id=1, source_target_pairs={{0,1},{1,0},{2,3},{3,2},{4,5},{5,4},{6,7},{7,6},{8,9},{9,8},{10,11... | collective-permute-start | bytes 1572872 | tf_op jit(solution)/shard_map/ppermute | solution.py:39
  104.4 11.7 %collective-permute-start.10 = (bf16[64,4096]{1,0:T(8,128)(2,1)S(1)}, bf16[64,4096]{1,0:T(8,128)(2,1)S(1)}, u32[]{:S(2)}, u32[]{:S(2)}) collective-permute-start(bf16[64,4096]{1,0:T(8,128)(2,1)S(1)} %add_convert_fusion.4), channel_id=1, source_target_pairs={{0,32},{1,97},{32,64},{33,1},{64,96},{65,33},{96,0},{97,65},{2,34}... | collective-permute-start | bytes 1572872 | tf_op jit(solution)/shard_map/ppermute | solution.py:35
  105.5 14.2 %collective-permute-start.11 = (bf16[64,4096]{1,0:T(8,128)(2,1)S(1)}, bf16[64,4096]{1,0:T(8,128)(2,1)S(1)}, u32[]{:S(2)}, u32[]{:S(2)}) collective-permute-start(bf16[64,4096]{1,0:T(8,128)(2,1)S(1)} %add_convert_fusion.3), channel_id=1, source_target_pairs={{0,96},{1,33},{32,0},{33,65},{64,32},{65,97},{96,64},{97,1},{2,98}... | collective-permute-start | bytes 1572872 | tf_op jit(solution)/shard_map/ppermute | solution.py:35
  119.6 8.3 %collective-permute-start.21 = (bf16[64,4096]{1,0:T(8,128)(2,1)S(1)}, bf16[64,4096]{1,0:T(8,128)(2,1)S(1)}, u32[]{:S(2)}, u32[]{:S(2)}) collective-permute-start(bf16[64,4096]{1,0:T(8,128)(2,1)S(1)} %collective-permute-done.12.refs_0_), channel_id=1, source_target_pairs={{0,32},{1,97},{32,64},{33,1},{64,96},{65,33},{96,0},{97,65},{2,34}... | collective-permute-start | bytes 1572872 | tf_op jit(solution)/shard_map/ppermute | solution.py:35
  119.6 16.7 %collective-permute-start.19 = (bf16[64,4096]{1,0:T(8,128)(2,1)S(1)}, bf16[64,4096]{1,0:T(8,128)(2,1)S(1)}, u32[]{:S(2)}, u32[]{:S(2)}) collective-permute-start(bf16[64,4096]{1,0:T(8,128)(2,1)S(1)} %get-tuple-element.56.refs_0_), channel_id=1, source_target_pairs={{0,1},{1,0},{2,3},{3,2},{4,5},{5,4},{6,7},{7,6},{8,9},{9,8},{10,11... | collective-permute-start | bytes 1572872 | tf_op jit(solution)/shard_map/ppermute | solution.py:39
  128.0 21.6 %collective-permute-start.22 = (bf16[64,4096]{1,0:T(8,128)(2,1)S(1)}, bf16[64,4096]{1,0:T(8,128)(2,1)S(1)}, u32[]{:S(2)}, u32[]{:S(2)}) collective-permute-start(bf16[64,4096]{1,0:T(8,128)(2,1)S(1)} %collective-permute-done.21.refs_0_), channel_id=1, source_target_pairs={{0,1},{1,0},{2,3},{3,2},{4,5},{5,4},{6,7},{7,6},{8,9},{9,8},{10,11... | collective-permute-start | bytes 1572872 | tf_op jit(solution)/shard_map/ppermute | solution.py:39
  132.6 1.2 collective-permute-start.16
  133.8 2.5 %collective-permute-start.17 = (f32[8,128]{1,0:T(8,128)S(1)}, f32[8,128]{1,0:T(8,128)S(1)}, u32[]{:S(2)}, u32[]{:S(2)}) collective-permute-start(f32[8,128]{1,0:T(8,128)S(1)} %add.68), channel_id=1, source_target_pairs={{0,32},{32,0},{64,96},{96,64},{1,33},{33,1},{65,97},{97,65},{2,34}... | collective-permute-start | bytes 12296 | tf_op jit(solution)/shard_map/ppermute | solution.py:44
  136.3 3.7 %collective-permute-start.18 = (f32[8,128]{1,0:T(8,128)S(1)}, f32[8,128]{1,0:T(8,128)S(1)}, u32[]{:S(2)}, u32[]{:S(2)}) collective-permute-start(f32[8,128]{1,0:T(8,128)S(1)} %add.69), channel_id=1, source_target_pairs={{0,96},{96,0},{32,64},{64,32},{1,97},{97,1},{33,65},{65,33},{2,98}... | collective-permute-start | bytes 12296 | tf_op jit(solution)/shard_map/ppermute | solution.py:45
  147.0 12.3 %collective-permute-start.20 = (bf16[192,4096]{1,0:T(8,128)(2,1)S(1)}, bf16[192,4096]{1,0:T(8,128)(2,1)S(1)}, u32[]{:S(2)}, u32[]{:S(2)}) collective-permute-start(bf16[192,4096]{1,0:T(8,128)(2,1)S(1)} %get-tuple-element.68), channel_id=1, source_target_pairs={{0,1},{1,0},{2,3},{3,2},{4,5},{5,4},{6,7},{7,6},{8,9},{9,8},{10,11... | collective-permute-start | bytes 4718600 | tf_op jit(solution)/shard_map/ppermute | solution.py:39
  155.6 2.0 collective-permute-start.23
  157.7 13.2 %collective-permute-start.24 = (bf16[64,4096]{1,0:T(8,128)(2,1)S(1)}, bf16[64,4096]{1,0:T(8,128)(2,1)S(1)}, u32[]{:S(2)}, u32[]{:S(2)}) collective-permute-start(bf16[64,4096]{1,0:T(8,128)(2,1)S(1)} %add_convert_fusion.2), channel_id=1, source_target_pairs={{0,32},{1,97},{32,64},{33,1},{64,96},{65,33},{96,0},{97,65},{2,34}... | collective-permute-start | bytes 1572872 | tf_op jit(solution)/shard_map/ppermute | solution.py:35
  159.5 26.4 %collective-permute-start.26 = (bf16[64,4096]{1,0:T(8,128)(2,1)S(1)}, bf16[64,4096]{1,0:T(8,128)(2,1)S(1)}, u32[]{:S(2)}, u32[]{:S(2)}) collective-permute-start(bf16[64,4096]{1,0:T(8,128)(2,1)S(1)} %add_convert_fusion), channel_id=1, source_target_pairs={{0,96},{1,33},{32,0},{33,65},{64,32},{65,97},{96,64},{97,1},{2,98}... | collective-permute-start | bytes 1572872 | tf_op jit(solution)/shard_map/ppermute | solution.py:35
  171.1 14.7 %collective-permute-start.25 = (bf16[64,4096]{1,0:T(8,128)(2,1)S(1)}, bf16[64,4096]{1,0:T(8,128)(2,1)S(1)}, u32[]{:S(2)}, u32[]{:S(2)}) collective-permute-start(bf16[64,4096]{1,0:T(8,128)(2,1)S(1)} %add_convert_fusion.1), channel_id=1, source_target_pairs={{0,32},{1,97},{32,64},{33,1},{64,96},{65,33},{96,0},{97,65},{2,34}... | collective-permute-start | bytes 1572872 | tf_op jit(solution)/shard_map/ppermute | solution.py:35
  187.0 20.3 %copy-start.2 = (s32[2,64]{1,0:T(2,128)S(1)}, s32[2,64]{1,0:T(2,128)}, u32[]{:S(2)}) copy-start(s32[2,64]{1,0:T(2,128)} %refs_2_.3) | copy-start | bytes 1540
  201.1 3.1 %collective-permute-start.27 = (f32[16,128]{1,0:T(8,128)S(1)}, f32[16,128]{1,0:T(8,128)S(1)}, u32[]{:S(2)}, u32[]{:S(2)}) collective-permute-start(f32[16,128]{1,0:T(8,128)S(1)} %convert_element_type.59), channel_id=1, source_target_pairs={{0,1},{1,0},{2,3},{3,2},{4,5},{5,4},{6,7},{7,6},{8,9},{9,8},{10,11... | collective-permute-start | bytes 24584 | tf_op jit(solution)/shard_map/ppermute | solution.py:39
  204.2 2.5 %collective-permute-start.28 = (f32[16,128]{1,0:T(8,128)S(1)}, f32[16,128]{1,0:T(8,128)S(1)}, u32[]{:S(2)}, u32[]{:S(2)}) collective-permute-start(f32[16,128]{1,0:T(8,128)S(1)} %convert_add_fusion), channel_id=1, source_target_pairs={{0,32},{32,0},{64,96},{96,64},{1,33},{33,1},{65,97},{97,65},{2,34}... | collective-permute-start | bytes 24584 | tf_op jit(solution)/shard_map/ppermute | solution.py:44
  206.7 3.7 %collective-permute-start.29 = (f32[16,128]{1,0:T(8,128)S(1)}, f32[16,128]{1,0:T(8,128)S(1)}, u32[]{:S(2)}, u32[]{:S(2)}) collective-permute-start(f32[16,128]{1,0:T(8,128)S(1)} %add.78), channel_id=1, source_target_pairs={{0,96},{96,0},{32,64},{64,32},{1,97},{97,1},{33,65},{65,33},{2,98}... | collective-permute-start | bytes 24584 | tf_op jit(solution)/shard_map/ppermute | solution.py:45
  (1 other events, 0.7 us)

commit v2 on v1

--- a/solution.py
+++ b/solution.py
@@ -20,7 +20,6 @@
 
 
 WHOLE = pl.BlockSpec(memory_space=pltpu.VMEM)
-SCALAR = pl.BlockSpec(memory_space=pltpu.SMEM)
 HBM = pl.BlockSpec(memory_space=pltpu.HBM)
 f32 = jnp.float32
 bf16 = jnp.bfloat16
@@ -90,6 +89,10 @@
     slot = (s // 8) * 4 + s % 4
     hit = jnp.where((s // 4) % 2 == which, slot, -1) == target
     return jnp.where(hit, 1.0, 0.0).astype(bf16)
+
+
+def mark_kernel(src, out):
+    out[...] = src[...]
 
 
 def positions(ids, experts):
@@ -169,22 +172,17 @@
     rows = parts[0].shape[0]
     for i, part in enumerate(parts):
         x[i * rows : (i + 1) * rows, :] = part[...]
-    tile = 128
-
-    def step(i, carry):
-        at = pl.ds(pl.multiple_of(i * tile, tile), tile)
+    for lo in range(0, wg.shape[2], 128):
+        at = slice(lo, lo + 128)
         w = jnp.concatenate([wg[0, :, at], wu[0, :, at]], axis=1)
         both = jnp.dot(x[...], w, preferred_element_type=f32)
-        g = both[:, :tile]
-        u = both[:, tile:]
+        g = both[:, :128]
+        u = both[:, 128:]
         if keep:
             outs[0][:, at] = g
             outs[1][:, at] = u
         else:
             outs[0][:, at] = silu_mul(g, u)
-        return carry
-
-    lax.fori_loop(0, wg.shape[2] // tile, step, 0)
 
 
 def gate_up(parts, w_gate, w_up, keep):
@@ -201,9 +199,13 @@
     )
 
 
+def clip_of(sumsq, count, width):
+    return jnp.minimum(1.0, clip_target / jnp.sqrt((sumsq + width) / (width * (count + 1.0))))
+
+
 def down_kernel(*refs, groups, keep):
     if keep:
-        clip = refs[0][0, 0]
+        clip = clip_of(refs[0][:1, :1], refs[0][:1, 1:2], refs[-2].shape[1])
         parts = refs[1 : 1 + 2 * groups]
         sizes = [parts[2 * i].shape[0] // 2 for i in range(groups)]
     else:
@@ -232,18 +234,17 @@
         oth[:, cols] = y[rows:].astype(oth.dtype)
         return carry
 
-    lax.fori_loop(0, w.shape[2] // tile, step, 0)
-
-
-def down(groups, w_down, n, clip):
-    keep = clip is not None
+    steps = w.shape[2] // tile
+    lax.fori_loop(0, steps, step, 0, unroll=steps if rows == n else 4)
+
+
+def down(groups, w_down, n, stats):
+    keep = stats is not None
     rows = sum(g[0].shape[0] for g in groups) // 2
     k, width = w_down.shape[1:]
     args = [a for g in groups for a in g]
-    specs = [WHOLE] * (len(args) + 1)
     if keep:
-        args = [clip] + args
-        specs = [SCALAR] + specs
+        args = [stats] + args
     return call(
         functools.partial(down_kernel, groups=len(groups), keep=keep),
         [shape_of(n, width, dtype=f32)] * (rows // n) + [shape_of(rows, width)],
@@ -251,7 +252,6 @@
         *args,
         w_down,
         scratch=[pltpu.VMEM((2 * rows, k), bf16)],
-        specs=specs,
     )
 
 
@@ -339,14 +339,10 @@
     experts = lax.axis_size(PLANE)
     tie = lax.optimization_barrier
 
-    def clip_of(sumsq, count):
-        return jnp.minimum(
-            1.0, clip_target / jnp.sqrt((sumsq + width) / (width * (count + 1.0)))
-        )
-
     arrived = exchange(pack(tokens, expert_of, experts))
     mine, counts = split(arrived, micros, width)
     w_gate, w_up, w_down = load(w_gate, w_up, w_down)
+    (counts,) = call(mark_kernel, [shape_of(*counts.shape, dtype=f32)], MIB, counts)
 
     def spread_near(m):
         a = along_x(mine[m], 1)
@@ -365,11 +361,11 @@
     def spread_last(m, far):
         return gate_up([far, swap_core(far)], w_gate, w_up, m > 0)
 
-    def collect(m, own, near, far, clip, fill_in):
-        mid, send_far = down([far], w_down, n, clip)
+    def collect(m, own, near, far, stats, fill_in):
+        mid, send_far = down([far], w_down, n, stats)
         mid = mid + swap_core(send_far).astype(f32)
         relay = along_x(mid.astype(bf16), 1)
-        mine_o, a_o, b_o, send = down([own, near], w_down, n, clip)
+        mine_o, a_o, b_o, send = down([own, near], w_down, n, stats)
         got = swap_core(send)
         to_a = (a_o + got[n : 2 * n].astype(f32)).astype(bf16)
         from_b = along_x(to_a, -1)
@@ -390,24 +386,23 @@
         ao = swap_core(a1)
         bo = swap_core(b1)
         near1 = gate_up([a1, b1, ao, bo], w_gate, w_up, True)
-        from_a, from_b, near1, a = tie((from_a, from_b, near1, a1))
-        far1 = along_x(a, 1)
+        from_a, from_b, near1 = tie((from_a, from_b, near1))
+        far1 = along_x(a1, 1)
         return from_a, from_b, (near1, far1)
 
     (out0, stats), (near1, far1) = collect(0, own0, near0, far0, None, gates_of_1)
     stats = line_sum(stats)
     far1 = spread_last(1, far1)
-    clip = clip_of(stats[:1, :1], stats[:1, 1:2])
 
     def return_0(from_a, from_b):
         back = exchange(out0)
         from_a, from_b, back = tie((from_a, from_b, back))
         return from_a, from_b, back
 
-    (out1,), back0 = collect(1, own1, near1, far1, clip, return_0)
+    (out1,), back0 = collect(1, own1, near1, far1, stats, return_0)
     back1 = exchange(out1)
     got = line_sum(back1[:: 2 * n // experts, width // 2 :].astype(f32))
-    scale = clip_of(got[:, 0] + got[:, 1] + got[:, 2], got[:, 3])
+    scale = clip_of(got[:, 0] + got[:, 1] + got[:, 2], got[:, 3], width)
     (out,) = call(
         functools.partial(unpack_kernel, experts=experts),
         [shape_of(micros, n, width)],

time: 213 us -> 187 us (0.88)
  Pallas kernels: 52.1 us -> 39.7 us
  waiting for transfers between devices: 64.3 us -> 55.6 us
  blocking collectives: 52.6 us -> 49.1 us
    pallas_call x16 -> x17, Pallas kernels: 52.1 us -> 39.7 us  [call(): pl.pallas_call(kernel, in_specs=specs or [WHOLE] * len(args), out_specs=[...]
    ppermute x12, waiting for transfers between devices: 54.2 us -> 46.9 us  [along_x(): return lax.ppermute(v, (X, CORE), pairs)]
    all_to_all x3, blocking collectives: 52.6 us -> 49.1 us  [exchange(): lax.all_to_all(v.reshape(experts, rows // experts, width), PLANE, 0, 0, t...]
    ppermute x14, waiting for transfers between devices: 3.9 us -> 1.68 us  [swap_core(): return lax.ppermute(v, CORE, [(0, 1), (1, 0)])]
  transfers between devices with their start and end apart: 30 -> 30, of which waited for: 15 -> 15; matrix products, arithmetic and copies ran while one was open for 1% -> 0% of each run, Pallas kernels for 24% -> 20%
where the time goes in v2:
time: 187 us; the launch traced here: 186 us
  waiting for transfers between devices  55.6 us (30%)
  blocking collectives  49.1 us (26%)
  Pallas kernels  39.7 us (21%)
  starting transfers between devices  37.1 us (20%)
  local copies, waits for them, and re-layouts  1.98 us (1%)
    all_to_all x3, blocking collectives, exchange(): lax.all_to_all(v.reshape(experts, rows // experts, width), PLANE, 0, 0, t...  49.1 us
    ppermute x12, waiting for transfers between devices, along_x(): return lax.ppermute(v, (X, CORE), pairs)  46.9 us
    pallas_call x17, Pallas kernels, call(): pl.pallas_call(kernel, in_specs=specs or [WHOLE] * len(args), out_specs=[...  39.7 us
    ppermute x14, starting transfers between devices, swap_core(): return lax.ppermute(v, CORE, [(0, 1), (1, 0)])  20.8 us
    ppermute x12, starting transfers between devices, along_x(): return lax.ppermute(v, (X, CORE), pairs)  14.9 us
    ppermute x2, waiting for transfers between devices, line_sum(): v = v + lax.ppermute(v, X, [(0, 1), (1, 0), (2, 3), (3, 2)])  4.95 us
  transfers between devices with their start and end apart: 30, of which 15 were waited for; matrix products, arithmetic and copies ran while one was open for 0% of the time, Pallas kernels for 20%

profile of v2, /device:TPU:1, one launch (start us, length us, event | category | flops | bytes accessed | tf_op | source)
XLA Modules:
  0.0 185.9 jit_solution(2208958984302334895)
XLA Ops:
  3.4 25.2 %all_to_all.15 = bf16[16,8,4224]{2,1,0:T(8,128)(2,1)S(1)} all-to-all(bf16[16,8,4224]{2,1,0:T(8,128)(2,1)S(1)} %bitcast.7), channel_id=1, replica_groups=mesh['dp'=4,'expert_0'=4,'expert_1'=4,'expert_2'=2] {'expert_0','expert_1'}, dimensions={0} | all-to-all | bytes 2162688 | tf_op jit(solution)/shard_map/all_to_all | solution.py:333
  29.1 2.5 %collective-permute-start.1 = (bf16[64,4096]{1,0:T(8,128)(2,1)S(1)}, bf16[64,4096]{1,0:T(8,128)(2,1)S(1)}, u32[]{:S(2)}, u32[]{:S(2)}) collective-permute-start(bf16[64,4096]{1,0:T(8,128)(2,1)S(1)} %get-tuple-element.41.refs_0_), channel_id=1, source_target_pairs={{0,32},{1,97},{32,64},{33,1},{64,96},{65,33},{96,0},{97,65},{2,34}... | collective-permute-start | bytes 1572872 | tf_op jit(solution)/shard_map/ppermute | solution.py:34
  31.6 6.1 %collective-permute-done.1.refs_0_ = bf16[64,4096]{1,0:T(8,128)(2,1)S(1)} collective-permute-done((bf16[64,4096]{1,0:T(8,128)(2,1)S(1)}, bf16[64,4096]{1,0:T(8,128)(2,1)S(1)}, u32[]{:S(2)}, u32[]{:S(2)}) %collective-permute-start.1) | collective-permute-done | bytes 524320 | tf_op jit(solution)/shard_map/ppermute | solution.py:34
  37.7 3.1 %collective-permute-start.6 = (bf16[64,4096]{1,0:T(8,128)(2,1)S(1)}, bf16[64,4096]{1,0:T(8,128)(2,1)S(1)}, u32[]{:S(2)}, u32[]{:S(2)}) collective-permute-start(bf16[64,4096]{1,0:T(8,128)(2,1)S(1)} %collective-permute-done.1.refs_0_), channel_id=1, source_target_pairs={{0,32},{1,97},{32,64},{33,1},{64,96},{65,33},{96,0},{97,65},{2,34}... | collective-permute-start | bytes 1572872 | tf_op jit(solution)/shard_map/ppermute | solution.py:34
  40.9 7.9 %collective-permute-done.6.refs_0_ = bf16[64,4096]{1,0:T(8,128)(2,1)S(1)} collective-permute-done((bf16[64,4096]{1,0:T(8,128)(2,1)S(1)}, bf16[64,4096]{1,0:T(8,128)(2,1)S(1)}, u32[]{:S(2)}, u32[]{:S(2)}) %collective-permute-start.6) | collective-permute-done | bytes 524320 | tf_op jit(solution)/shard_map/ppermute | solution.py:34
  48.7 7.7 %collective-permute-start.7 = (bf16[64,4096]{1,0:T(8,128)(2,1)S(1)}, bf16[64,4096]{1,0:T(8,128)(2,1)S(1)}, u32[]{:S(2)}, u32[]{:S(2)}) collective-permute-start(bf16[64,4096]{1,0:T(8,128)(2,1)S(1)} %collective-permute-done.6.refs_0_), channel_id=1, source_target_pairs={{0,1},{1,0},{2,3},{3,2},{4,5},{5,4},{6,7},{7,6},{8,9},{9,8},{10,11... | collective-permute-start | bytes 1572872 | tf_op jit(solution)/shard_map/ppermute | solution.py:38
  56.9 7.3 %shard_map.70 = (bf16[1,4096,896]{2,1,0:T(8,128)(2,1)S(1)}, bf16[1,4096,896]{2,1,0:T(8,128)(2,1)S(1)}, bf16[1,896,4096]{2,1,0:T(8,128)(2,1)S(1)}) custom-call(bf16[1,4096,896]{2,1,0:T(8,128)(2,1)} %refs_0_.1, bf16[1,4096,896]{2,1,0:T(8,128)(2,1)} %refs_1_.1, bf16[1,896,4096]{2,1,0:T(8,128)(2,1)} %refs_2_.2), custom_call_target="tpu_custom_call" | custom-call | tf_op jit(solution)/shard_map/pallas_call | solution.py:48
  64.2 2.1 %shard_map.74.refs_0_ = bf16[128,896]{1,0:T(8,128)(2,1)S(1)} custom-call(bf16[64,4096]{1,0:T(8,128)(2,1)S(1)} %collective-permute-done.6.refs_0_, bf16[64,4096]{1,0:T(8,128)(2,1)S(1)} %collective-permute-done.7.refs_1_, bf16[1,4096,896]{2,1,0:T(8,128)(2,1)S(1)} %get-tuple-element.42.refs_2_.refs_4_, bf16[1,4096,896]{2,1,0:T(8,128)(2,1)S(1)} %get-tuple-element.43.refs_3_.refs_5_), custom_call_target="tpu_custom_call" | custom-call | tf_op jit(solution)/shard_map/pallas_call | solution.py:48
  68.4 2.1 %shard_map.71.refs_0_ = bf16[128,896]{1,0:T(8,128)(2,1)S(1)} custom-call(bf16[64,4096]{1,0:T(8,128)(2,1)S(1)} %get-tuple-element.41.refs_0_, bf16[64,4096]{1,0:T(8,128)(2,1)S(1)} %collective-permute-done.refs_1_, bf16[1,4096,896]{2,1,0:T(8,128)(2,1)S(1)} %get-tuple-element.42.refs_2_.refs_4_, bf16[1,4096,896]{2,1,0:T(8,128)(2,1)S(1)} %get-tuple-element.43.refs_3_.refs_5_), custom_call_target="tpu_custom_call" | custom-call | tf_op jit(solution)/shard_map/pallas_call | solution.py:48
  70.6 4.0 %shard_map.72.refs_1_ = bf16[256,896]{1,0:T(8,128)(2,1)S(1)} custom-call(bf16[64,4096]{1,0:T(8,128)(2,1)S(1)} %collective-permute-done.1.refs_0_, bf16[64,4096]{1,0:T(8,128)(2,1)S(1)} %collective-permute-done.2.refs_1_, bf16[64,4096]{1,0:T(8,128)(2,1)S(1)} %collective-permute-done.3.refs_2_, bf16[64,4096]{1,0:T(8,128)(2,1)S(1)} %collective-permute-done.4.refs_3_, ...), custom_call_target="tpu_custom_call" | custom-call | tf_op jit(solution)/shard_map/pallas_call | solution.py:48
  74.6 3.7 %shard_map.73 = (f32[64,4096]{1,0:T(8,128)S(1)}, f32[64,4096]{1,0:T(8,128)S(1)}, f32[64,4096]{1,0:T(8,128)S(1)}, bf16[192,4096]{1,0:T(8,128)(2,1)S(1)}) custom-call(bf16[128,896]{1,0:T(8,128)(2,1)S(1)} %shard_map.71.refs_0_, bf16[256,896]{1,0:T(8,128)(2,1)S(1)} %shard_map.72.refs_1_, bf16[1,896,4096]{2,1,0:T(8,128)(2,1)S(1)} %get-tuple-element.46.refs_2_.refs_1_.refs_5_.refs_3_), custom_call_target="tpu_custom_call" | custom-call | tf_op jit(solution)/shard_map/pallas_call | solution.py:48
  78.4 2.7 %collective-permute-start.12 = (bf16[64,4096]{1,0:T(8,128)(2,1)S(1)}, bf16[64,4096]{1,0:T(8,128)(2,1)S(1)}, u32[]{:S(2)}, u32[]{:S(2)}) collective-permute-start(bf16[64,4096]{1,0:T(8,128)(2,1)S(1)} %get-tuple-element.55.refs_0_), channel_id=1, source_target_pairs={{0,32},{1,97},{32,64},{33,1},{64,96},{65,33},{96,0},{97,65},{2,34}... | collective-permute-start | bytes 1572872 | tf_op jit(solution)/shard_map/ppermute | solution.py:34
  81.3 10.3 %collective-permute-done.12.refs_0_ = bf16[64,4096]{1,0:T(8,128)(2,1)S(1)} collective-permute-done((bf16[64,4096]{1,0:T(8,128)(2,1)S(1)}, bf16[64,4096]{1,0:T(8,128)(2,1)S(1)}, u32[]{:S(2)}, u32[]{:S(2)}) %collective-permute-start.12) | collective-permute-done | bytes 524320 | tf_op jit(solution)/shard_map/ppermute | solution.py:34
  91.6 2.3 %collective-permute-start.21 = (bf16[64,4096]{1,0:T(8,128)(2,1)S(1)}, bf16[64,4096]{1,0:T(8,128)(2,1)S(1)}, u32[]{:S(2)}, u32[]{:S(2)}) collective-permute-start(bf16[64,4096]{1,0:T(8,128)(2,1)S(1)} %collective-permute-done.12.refs_0_), channel_id=1, source_target_pairs={{0,32},{1,97},{32,64},{33,1},{64,96},{65,33},{96,0},{97,65},{2,34}... | collective-permute-start | bytes 1572872 | tf_op jit(solution)/shard_map/ppermute | solution.py:34
  94.4 3.7 %collective-permute-done.9 = bf16[64,4096]{1,0:T(8,128)(2,1)S(1)} collective-permute-done((bf16[64,4096]{1,0:T(8,128)(2,1)S(1)}, bf16[64,4096]{1,0:T(8,128)(2,1)S(1)}, u32[]{:S(2)}, u32[]{:S(2)}) %collective-permute-start.9) | collective-permute-done | bytes 524320 | tf_op jit(solution)/shard_map/ppermute | solution.py:34
  99.9 4.3 %collective-permute-done.21.refs_0_ = bf16[64,4096]{1,0:T(8,128)(2,1)S(1)} collective-permute-done((bf16[64,4096]{1,0:T(8,128)(2,1)S(1)}, bf16[64,4096]{1,0:T(8,128)(2,1)S(1)}, u32[]{:S(2)}, u32[]{:S(2)}) %collective-permute-start.21) | collective-permute-done | bytes 524320 | tf_op jit(solution)/shard_map/ppermute | solution.py:34
  104.2 2.0 %collective-permute-start.22 = (bf16[64,4096]{1,0:T(8,128)(2,1)S(1)}, bf16[64,4096]{1,0:T(8,128)(2,1)S(1)}, u32[]{:S(2)}, u32[]{:S(2)}) collective-permute-start(bf16[64,4096]{1,0:T(8,128)(2,1)S(1)} %collective-permute-done.21.refs_0_), channel_id=1, source_target_pairs={{0,1},{1,0},{2,3},{3,2},{4,5},{5,4},{6,7},{7,6},{8,9},{9,8},{10,11... | collective-permute-start | bytes 1572872 | tf_op jit(solution)/shard_map/ppermute | solution.py:38
  106.2 3.9 %shard_map.76 = (f32[256,896]{1,0:T(8,128)S(1)}, f32[256,896]{1,0:T(8,128)S(1)}) custom-call(bf16[64,4096]{1,0:T(8,128)(2,1)S(1)} %collective-permute-done.12.refs_0_, bf16[64,4096]{1,0:T(8,128)(2,1)S(1)} %collective-permute-done.13.refs_1_, bf16[64,4096]{1,0:T(8,128)(2,1)S(1)} %collective-permute-done.14.refs_2_, ...), custom_call_target="tpu_custom_call" | custom-call | tf_op jit(solution)/shard_map/pallas_call | solution.py:48
  110.2 4.8 %collective-permute-done.10.near_a = bf16[64,4096]{1,0:T(8,128)(2,1)S(1)} collective-permute-done((bf16[64,4096]{1,0:T(8,128)(2,1)S(1)}, bf16[64,4096]{1,0:T(8,128)(2,1)S(1)}, u32[]{:S(2)}, u32[]{:S(2)}) %collective-permute-start.10) | collective-permute-done | bytes 524320 | tf_op jit(solution)/shard_map/ppermute | solution.py:34
  118.4 2.5 %collective-permute-done.17 = f32[8,128]{1,0:T(8,128)S(1)} collective-permute-done((f32[8,128]{1,0:T(8,128)S(1)}, f32[8,128]{1,0:T(8,128)S(1)}, u32[]{:S(2)}, u32[]{:S(2)}) %collective-permute-start.17) | collective-permute-done | bytes 4128 | tf_op jit(solution)/shard_map/ppermute | solution.py:43
  121.5 2.1 %shard_map.81 = (f32[128,896]{1,0:T(8,128)S(1)}, f32[128,896]{1,0:T(8,128)S(1)}) custom-call(bf16[64,4096]{1,0:T(8,128)(2,1)S(1)} %collective-permute-done.21.refs_0_, bf16[64,4096]{1,0:T(8,128)(2,1)S(1)} %collective-permute-done.22.refs_1_, bf16[1,4096,896]{2,1,0:T(8,128)(2,1)S(1)} %get-tuple-element.42.refs_2_.refs_4_, ...), custom_call_target="tpu_custom_call" | custom-call | tf_op jit(solution)/shard_map/pallas_call | solution.py:48
  126.0 2.7 %collective-permute-start.23 = (bf16[64,4096]{1,0:T(8,128)(2,1)S(1)}, bf16[64,4096]{1,0:T(8,128)(2,1)S(1)}, u32[]{:S(2)}, u32[]{:S(2)}) collective-permute-start(bf16[64,4096]{1,0:T(8,128)(2,1)S(1)} %get-tuple-element.71), channel_id=1, source_target_pairs={{0,1},{1,0},{2,3},{3,2},{4,5},{5,4},{6,7},{7,6},{8,9},{9,8},{10,11... | collective-permute-start | bytes 1572872 | tf_op jit(solution)/shard_map/ppermute | solution.py:38
  128.7 2.1 %shard_map.79 = (f32[128,896]{1,0:T(8,128)S(1)}, f32[128,896]{1,0:T(8,128)S(1)}) custom-call(bf16[64,4096]{1,0:T(8,128)(2,1)S(1)} %get-tuple-element.55.refs_0_, bf16[64,4096]{1,0:T(8,128)(2,1)S(1)} %collective-permute-done.19.refs_1_, bf16[1,4096,896]{2,1,0:T(8,128)(2,1)S(1)} %get-tuple-element.42.refs_2_.refs_4_, ...), custom_call_target="tpu_custom_call" | custom-call | tf_op jit(solution)/shard_map/pallas_call | solution.py:48
  130.8 4.2 %shard_map.80 = (f32[64,4096]{1,0:T(8,128)S(1)}, f32[64,4096]{1,0:T(8,128)S(1)}, f32[64,4096]{1,0:T(8,128)S(1)}, bf16[192,4096]{1,0:T(8,128)(2,1)S(1)}) custom-call(f32[8,128]{1,0:T(8,128)S(1)} %add.64.refs_0_, f32[128,896]{1,0:T(8,128)S(1)} %get-tuple-element.62.refs_1_, f32[128,896]{1,0:T(8,128)S(1)} %get-tuple-element.63.refs_2_, ...), custom_call_target="tpu_custom_call" | custom-call | tf_op jit(solution)/shard_map/pallas_call | solution.py:48
  136.0 7.7 %collective-permute-done.24 = bf16[64,4096]{1,0:T(8,128)(2,1)S(1)} collective-permute-done((bf16[64,4096]{1,0:T(8,128)(2,1)S(1)}, bf16[64,4096]{1,0:T(8,128)(2,1)S(1)}, u32[]{:S(2)}, u32[]{:S(2)}) %collective-permute-start.24) | collective-permute-done | bytes 524320 | tf_op jit(solution)/shard_map/ppermute | solution.py:34
  143.9 1.8 collective-permute-start.25
  145.9 11.8 %all_to_all.16 = bf16[16,8,2048]{2,1,0:T(8,128)(2,1)S(1)} all-to-all(bf16[16,8,2048]{2,1,0:T(8,128)(2,1)S(1)} %bitcast.10), channel_id=1, replica_groups=mesh['dp'=4,'expert_0'=4,'expert_1'=4,'expert_2'=2] {'expert_0','expert_1'}, dimensions={0} | all-to-all | bytes 1048576 | tf_op jit(solution)/shard_map/all_to_all | solution.py:333
  157.7 2.0 %collective-permute-done.26.near_b = bf16[64,4096]{1,0:T(8,128)(2,1)S(1)} collective-permute-done((bf16[64,4096]{1,0:T(8,128)(2,1)S(1)}, bf16[64,4096]{1,0:T(8,128)(2,1)S(1)}, u32[]{:S(2)}, u32[]{:S(2)}) %collective-permute-start.26) | collective-permute-done | bytes 524320 | tf_op jit(solution)/shard_map/ppermute | solution.py:34
  161.0 12.1 %all_to_all.17 = bf16[16,8,2176]{2,1,0:T(8,128)(2,1)S(1)} all-to-all(bf16[16,8,2176]{2,1,0:T(8,128)(2,1)S(1)} %bitcast.8), channel_id=1, replica_groups=mesh['dp'=4,'expert_0'=4,'expert_1'=4,'expert_2'=2] {'expert_0','expert_1'}, dimensions={0} | all-to-all | bytes 1114112 | tf_op jit(solution)/shard_map/all_to_all | solution.py:333
  173.1 5.0 %collective-permute-start.27 = (f32[16,128]{1,0:T(8,128)S(1)}, f32[16,128]{1,0:T(8,128)S(1)}, u32[]{:S(2)}, u32[]{:S(2)}) collective-permute-start(f32[16,128]{1,0:T(8,128)S(1)} %convert_element_type.59), channel_id=1, source_target_pairs={{0,1},{1,0},{2,3},{3,2},{4,5},{5,4},{6,7},{7,6},{8,9},{9,8},{10,11... | collective-permute-start | bytes 24584 | tf_op jit(solution)/shard_map/ppermute | solution.py:38
  178.9 2.5 %collective-permute-done.28 = f32[16,128]{1,0:T(8,128)S(1)} collective-permute-done((f32[16,128]{1,0:T(8,128)S(1)}, f32[16,128]{1,0:T(8,128)S(1)}, u32[]{:S(2)}, u32[]{:S(2)}) %collective-permute-start.28) | collective-permute-done | bytes 8224 | tf_op jit(solution)/shard_map/ppermute | solution.py:43
  182.2 1.8 shard_map.84
  (70 shorter events, 21.0 us)
Async XLA Ops:
  0.6 1.2 copy-start
  29.1 8.7 %collective-permute-start.1 = (bf16[64,4096]{1,0:T(8,128)(2,1)S(1)}, bf16[64,4096]{1,0:T(8,128)(2,1)S(1)}, u32[]{:S(2)}, u32[]{:S(2)}) collective-permute-start(bf16[64,4096]{1,0:T(8,128)(2,1)S(1)} %get-tuple-element.41.refs_0_), channel_id=1, source_target_pairs={{0,32},{1,97},{32,64},{33,1},{64,96},{65,33},{96,0},{97,65},{2,34}... | collective-permute-start | bytes 1572872 | tf_op jit(solution)/shard_map/ppermute | solution.py:34
  37.7 11.0 %collective-permute-start.6 = (bf16[64,4096]{1,0:T(8,128)(2,1)S(1)}, bf16[64,4096]{1,0:T(8,128)(2,1)S(1)}, u32[]{:S(2)}, u32[]{:S(2)}) collective-permute-start(bf16[64,4096]{1,0:T(8,128)(2,1)S(1)} %collective-permute-done.1.refs_0_), channel_id=1, source_target_pairs={{0,32},{1,97},{32,64},{33,1},{64,96},{65,33},{96,0},{97,65},{2,34}... | collective-permute-start | bytes 1572872 | tf_op jit(solution)/shard_map/ppermute | solution.py:34
  40.9 15.6 %collective-permute-start.2 = (bf16[64,4096]{1,0:T(8,128)(2,1)S(1)}, bf16[64,4096]{1,0:T(8,128)(2,1)S(1)}, u32[]{:S(2)}, u32[]{:S(2)}) collective-permute-start(bf16[64,4096]{1,0:T(8,128)(2,1)S(1)} %get-tuple-element.41.refs_0_), channel_id=1, source_target_pairs={{0,96},{1,33},{32,0},{33,65},{64,32},{65,97},{96,64},{97,1},{2,98}... | collective-permute-start | bytes 1572872 | tf_op jit(solution)/shard_map/ppermute | solution.py:34
  48.7 15.5 %collective-permute-start.7 = (bf16[64,4096]{1,0:T(8,128)(2,1)S(1)}, bf16[64,4096]{1,0:T(8,128)(2,1)S(1)}, u32[]{:S(2)}, u32[]{:S(2)}) collective-permute-start(bf16[64,4096]{1,0:T(8,128)(2,1)S(1)} %collective-permute-done.6.refs_0_), channel_id=1, source_target_pairs={{0,1},{1,0},{2,3},{3,2},{4,5},{5,4},{6,7},{7,6},{8,9},{9,8},{10,11... | collective-permute-start | bytes 1572872 | tf_op jit(solution)/shard_map/ppermute | solution.py:38
  56.4 12.0 %collective-permute-start = (bf16[64,4096]{1,0:T(8,128)(2,1)S(1)}, bf16[64,4096]{1,0:T(8,128)(2,1)S(1)}, u32[]{:S(2)}, u32[]{:S(2)}) collective-permute-start(bf16[64,4096]{1,0:T(8,128)(2,1)S(1)} %get-tuple-element.41.refs_0_), channel_id=1, source_target_pairs={{0,1},{1,0},{2,3},{3,2},{4,5},{5,4},{6,7},{7,6},{8,9},{9,8},{10,11... | collective-permute-start | bytes 1572872 | tf_op jit(solution)/shard_map/ppermute | solution.py:38
  56.4 14.2 %collective-permute-start.4 = (bf16[64,4096]{1,0:T(8,128)(2,1)S(1)}, bf16[64,4096]{1,0:T(8,128)(2,1)S(1)}, u32[]{:S(2)}, u32[]{:S(2)}) collective-permute-start(bf16[64,4096]{1,0:T(8,128)(2,1)S(1)} %collective-permute-done.2.refs_1_), channel_id=1, source_target_pairs={{0,1},{1,0},{2,3},{3,2},{4,5},{5,4},{6,7},{7,6},{8,9},{9,8},{10,11... | collective-permute-start | bytes 1572872 | tf_op jit(solution)/shard_map/ppermute | solution.py:38
  56.9 13.7 %collective-permute-start.3 = (bf16[64,4096]{1,0:T(8,128)(2,1)S(1)}, bf16[64,4096]{1,0:T(8,128)(2,1)S(1)}, u32[]{:S(2)}, u32[]{:S(2)}) collective-permute-start(bf16[64,4096]{1,0:T(8,128)(2,1)S(1)} %collective-permute-done.1.refs_0_), channel_id=1, source_target_pairs={{0,1},{1,0},{2,3},{3,2},{4,5},{5,4},{6,7},{7,6},{8,9},{9,8},{10,11... | collective-permute-start | bytes 1572872 | tf_op jit(solution)/shard_map/ppermute | solution.py:38
  67.7 13.4 %collective-permute-start.8 = (bf16[64,4096]{1,0:T(8,128)(2,1)S(1)}, bf16[64,4096]{1,0:T(8,128)(2,1)S(1)}, u32[]{:S(2)}, u32[]{:S(2)}) collective-permute-start(bf16[64,4096]{1,0:T(8,128)(2,1)S(1)} %get-tuple-element.51), channel_id=1, source_target_pairs={{0,1},{1,0},{2,3},{3,2},{4,5},{5,4},{6,7},{7,6},{8,9},{9,8},{10,11... | collective-permute-start | bytes 1572872 | tf_op jit(solution)/shard_map/ppermute | solution.py:38
  78.3 19.8 %collective-permute-start.5 = (bf16[192,4096]{1,0:T(8,128)(2,1)S(1)}, bf16[192,4096]{1,0:T(8,128)(2,1)S(1)}, u32[]{:S(2)}, u32[]{:S(2)}) collective-permute-start(bf16[192,4096]{1,0:T(8,128)(2,1)S(1)} %get-tuple-element.48), channel_id=1, source_target_pairs={{0,1},{1,0},{2,3},{3,2},{4,5},{5,4},{6,7},{7,6},{8,9},{9,8},{10,11... | collective-permute-start | bytes 4718600 | tf_op jit(solution)/shard_map/ppermute | solution.py:38
  78.4 15.6 %collective-permute-start.13 = (bf16[64,4096]{1,0:T(8,128)(2,1)S(1)}, bf16[64,4096]{1,0:T(8,128)(2,1)S(1)}, u32[]{:S(2)}, u32[]{:S(2)}) collective-permute-start(bf16[64,4096]{1,0:T(8,128)(2,1)S(1)} %get-tuple-element.55.refs_0_), channel_id=1, source_target_pairs={{0,96},{1,33},{32,0},{33,65},{64,32},{65,97},{96,64},{97,1},{2,98}... | collective-permute-start | bytes 1572872 | tf_op jit(solution)/shard_map/ppermute | solution.py:34
  78.4 13.2 %collective-permute-start.12 = (bf16[64,4096]{1,0:T(8,128)(2,1)S(1)}, bf16[64,4096]{1,0:T(8,128)(2,1)S(1)}, u32[]{:S(2)}, u32[]{:S(2)}) collective-permute-start(bf16[64,4096]{1,0:T(8,128)(2,1)S(1)} %get-tuple-element.55.refs_0_), channel_id=1, source_target_pairs={{0,32},{1,97},{32,64},{33,1},{64,96},{65,33},{96,0},{97,65},{2,34}... | collective-permute-start | bytes 1572872 | tf_op jit(solution)/shard_map/ppermute | solution.py:34
  81.2 16.8 %collective-permute-start.9 = (bf16[64,4096]{1,0:T(8,128)(2,1)S(1)}, bf16[64,4096]{1,0:T(8,128)(2,1)S(1)}, u32[]{:S(2)}, u32[]{:S(2)}) collective-permute-start(bf16[64,4096]{1,0:T(8,128)(2,1)S(1)} %add_convert_fusion.5), channel_id=1, source_target_pairs={{0,32},{1,97},{32,64},{33,1},{64,96},{65,33},{96,0},{97,65},{2,34}... | collective-permute-start | bytes 1572872 | tf_op jit(solution)/shard_map/ppermute | solution.py:34
  91.6 12.5 %collective-permute-start.21 = (bf16[64,4096]{1,0:T(8,128)(2,1)S(1)}, bf16[64,4096]{1,0:T(8,128)(2,1)S(1)}, u32[]{:S(2)}, u32[]{:S(2)}) collective-permute-start(bf16[64,4096]{1,0:T(8,128)(2,1)S(1)} %collective-permute-done.12.refs_0_), channel_id=1, source_target_pairs={{0,32},{1,97},{32,64},{33,1},{64,96},{65,33},{96,0},{97,65},{2,34}... | collective-permute-start | bytes 1572872 | tf_op jit(solution)/shard_map/ppermute | solution.py:34
  93.9 12.3 %collective-permute-start.14 = (bf16[64,4096]{1,0:T(8,128)(2,1)S(1)}, bf16[64,4096]{1,0:T(8,128)(2,1)S(1)}, u32[]{:S(2)}, u32[]{:S(2)}) collective-permute-start(bf16[64,4096]{1,0:T(8,128)(2,1)S(1)} %collective-permute-done.12.refs_0_), channel_id=1, source_target_pairs={{0,1},{1,0},{2,3},{3,2},{4,5},{5,4},{6,7},{7,6},{8,9},{9,8},{10,11... | collective-permute-start | bytes 1572872 | tf_op jit(solution)/shard_map/ppermute | solution.py:38
  94.0 12.2 %collective-permute-start.15 = (bf16[64,4096]{1,0:T(8,128)(2,1)S(1)}, bf16[64,4096]{1,0:T(8,128)(2,1)S(1)}, u32[]{:S(2)}, u32[]{:S(2)}) collective-permute-start(bf16[64,4096]{1,0:T(8,128)(2,1)S(1)} %collective-permute-done.13.refs_1_), channel_id=1, source_target_pairs={{0,1},{1,0},{2,3},{3,2},{4,5},{5,4},{6,7},{7,6},{8,9},{9,8},{10,11... | collective-permute-start | bytes 1572872 | tf_op jit(solution)/shard_map/ppermute | solution.py:38
  98.2 16.7 %collective-permute-start.10 = (bf16[64,4096]{1,0:T(8,128)(2,1)S(1)}, bf16[64,4096]{1,0:T(8,128)(2,1)S(1)}, u32[]{:S(2)}, u32[]{:S(2)}) collective-permute-start(bf16[64,4096]{1,0:T(8,128)(2,1)S(1)} %add_convert_fusion.4), channel_id=1, source_target_pairs={{0,32},{1,97},{32,64},{33,1},{64,96},{65,33},{96,0},{97,65},{2,34}... | collective-permute-start | bytes 1572872 | tf_op jit(solution)/shard_map/ppermute | solution.py:34
  99.8 15.2 %collective-permute-start.11 = (bf16[64,4096]{1,0:T(8,128)(2,1)S(1)}, bf16[64,4096]{1,0:T(8,128)(2,1)S(1)}, u32[]{:S(2)}, u32[]{:S(2)}) collective-permute-start(bf16[64,4096]{1,0:T(8,128)(2,1)S(1)} %add_convert_fusion.3), channel_id=1, source_target_pairs={{0,96},{1,33},{32,0},{33,65},{64,32},{65,97},{96,64},{97,1},{2,98}... | collective-permute-start | bytes 1572872 | tf_op jit(solution)/shard_map/ppermute | solution.py:34
  104.2 17.3 %collective-permute-start.22 = (bf16[64,4096]{1,0:T(8,128)(2,1)S(1)}, bf16[64,4096]{1,0:T(8,128)(2,1)S(1)}, u32[]{:S(2)}, u32[]{:S(2)}) collective-permute-start(bf16[64,4096]{1,0:T(8,128)(2,1)S(1)} %collective-permute-done.21.refs_0_), channel_id=1, source_target_pairs={{0,1},{1,0},{2,3},{3,2},{4,5},{5,4},{6,7},{7,6},{8,9},{9,8},{10,11... | collective-permute-start | bytes 1572872 | tf_op jit(solution)/shard_map/ppermute | solution.py:38
  106.2 22.6 %collective-permute-start.19 = (bf16[64,4096]{1,0:T(8,128)(2,1)S(1)}, bf16[64,4096]{1,0:T(8,128)(2,1)S(1)}, u32[]{:S(2)}, u32[]{:S(2)}) collective-permute-start(bf16[64,4096]{1,0:T(8,128)(2,1)S(1)} %get-tuple-element.55.refs_0_), channel_id=1, source_target_pairs={{0,1},{1,0},{2,3},{3,2},{4,5},{5,4},{6,7},{7,6},{8,9},{9,8},{10,11... | collective-permute-start | bytes 1572872 | tf_op jit(solution)/shard_map/ppermute | solution.py:38
  116.2 2.2 %collective-permute-start.16 = (f32[8,128]{1,0:T(8,128)S(1)}, f32[8,128]{1,0:T(8,128)S(1)}, u32[]{:S(2)}, u32[]{:S(2)}) collective-permute-start(f32[8,128]{1,0:T(8,128)S(1)} %get-tuple-element.61), channel_id=1, source_target_pairs={{0,1},{1,0},{2,3},{3,2},{4,5},{5,4},{6,7},{7,6},{8,9},{9,8},{10,11... | collective-permute-start | bytes 12296 | tf_op jit(solution)/shard_map/ppermute | solution.py:38
  118.4 2.5 %collective-permute-start.17 = (f32[8,128]{1,0:T(8,128)S(1)}, f32[8,128]{1,0:T(8,128)S(1)}, u32[]{:S(2)}, u32[]{:S(2)}) collective-permute-start(f32[8,128]{1,0:T(8,128)S(1)} %add.62), channel_id=1, source_target_pairs={{0,32},{32,0},{64,96},{96,64},{1,33},{33,1},{65,97},{97,65},{2,34}... | collective-permute-start | bytes 12296 | tf_op jit(solution)/shard_map/ppermute | solution.py:43
  120.9 3.7 %collective-permute-start.18 = (f32[8,128]{1,0:T(8,128)S(1)}, f32[8,128]{1,0:T(8,128)S(1)}, u32[]{:S(2)}, u32[]{:S(2)}) collective-permute-start(f32[8,128]{1,0:T(8,128)S(1)} %add.63), channel_id=1, source_target_pairs={{0,96},{96,0},{32,64},{64,32},{1,97},{97,1},{33,65},{65,33},{2,98}... | collective-permute-start | bytes 12296 | tf_op jit(solution)/shard_map/ppermute | solution.py:44
  126.0 9.2 %collective-permute-start.23 = (bf16[64,4096]{1,0:T(8,128)(2,1)S(1)}, bf16[64,4096]{1,0:T(8,128)(2,1)S(1)}, u32[]{:S(2)}, u32[]{:S(2)}) collective-permute-start(bf16[64,4096]{1,0:T(8,128)(2,1)S(1)} %get-tuple-element.71), channel_id=1, source_target_pairs={{0,1},{1,0},{2,3},{3,2},{4,5},{5,4},{6,7},{7,6},{8,9},{9,8},{10,11... | collective-permute-start | bytes 1572872 | tf_op jit(solution)/shard_map/ppermute | solution.py:38
  135.1 8.6 %collective-permute-start.20 = (bf16[192,4096]{1,0:T(8,128)(2,1)S(1)}, bf16[192,4096]{1,0:T(8,128)(2,1)S(1)}, u32[]{:S(2)}, u32[]{:S(2)}) collective-permute-start(bf16[192,4096]{1,0:T(8,128)(2,1)S(1)} %get-tuple-element.67), channel_id=1, source_target_pairs={{0,1},{1,0},{2,3},{3,2},{4,5},{5,4},{6,7},{7,6},{8,9},{9,8},{10,11... | collective-permute-start | bytes 4718600 | tf_op jit(solution)/shard_map/ppermute | solution.py:38
  135.3 8.4 %collective-permute-start.24 = (bf16[64,4096]{1,0:T(8,128)(2,1)S(1)}, bf16[64,4096]{1,0:T(8,128)(2,1)S(1)}, u32[]{:S(2)}, u32[]{:S(2)}) collective-permute-start(bf16[64,4096]{1,0:T(8,128)(2,1)S(1)} %add_convert_fusion.2), channel_id=1, source_target_pairs={{0,32},{1,97},{32,64},{33,1},{64,96},{65,33},{96,0},{97,65},{2,34}... | collective-permute-start | bytes 1572872 | tf_op jit(solution)/shard_map/ppermute | solution.py:34
  143.9 13.9 %collective-permute-start.25 = (bf16[64,4096]{1,0:T(8,128)(2,1)S(1)}, bf16[64,4096]{1,0:T(8,128)(2,1)S(1)}, u32[]{:S(2)}, u32[]{:S(2)}) collective-permute-start(bf16[64,4096]{1,0:T(8,128)(2,1)S(1)} %add_convert_fusion.1), channel_id=1, source_target_pairs={{0,32},{1,97},{32,64},{33,1},{64,96},{65,33},{96,0},{97,65},{2,34}... | collective-permute-start | bytes 1572872 | tf_op jit(solution)/shard_map/ppermute | solution.py:34
  145.9 13.9 %collective-permute-start.26 = (bf16[64,4096]{1,0:T(8,128)(2,1)S(1)}, bf16[64,4096]{1,0:T(8,128)(2,1)S(1)}, u32[]{:S(2)}, u32[]{:S(2)}) collective-permute-start(bf16[64,4096]{1,0:T(8,128)(2,1)S(1)} %add_convert_fusion), channel_id=1, source_target_pairs={{0,96},{1,33},{32,0},{33,65},{64,32},{65,97},{96,64},{97,1},{2,98}... | collective-permute-start | bytes 1572872 | tf_op jit(solution)/shard_map/ppermute | solution.py:34
  161.0 21.3 %copy-start.2 = (s32[2,64]{1,0:T(2,128)S(1)}, s32[2,64]{1,0:T(2,128)}, u32[]{:S(2)}) copy-start(s32[2,64]{1,0:T(2,128)} %refs_2_.3) | copy-start | bytes 1540
  173.1 5.8 %collective-permute-start.27 = (f32[16,128]{1,0:T(8,128)S(1)}, f32[16,128]{1,0:T(8,128)S(1)}, u32[]{:S(2)}, u32[]{:S(2)}) collective-permute-start(f32[16,128]{1,0:T(8,128)S(1)} %convert_element_type.59), channel_id=1, source_target_pairs={{0,1},{1,0},{2,3},{3,2},{4,5},{5,4},{6,7},{7,6},{8,9},{9,8},{10,11... | collective-permute-start | bytes 24584 | tf_op jit(solution)/shard_map/ppermute | solution.py:38
  178.9 2.5 %collective-permute-start.28 = (f32[16,128]{1,0:T(8,128)S(1)}, f32[16,128]{1,0:T(8,128)S(1)}, u32[]{:S(2)}, u32[]{:S(2)}) collective-permute-start(f32[16,128]{1,0:T(8,128)S(1)} %convert_add_fusion), channel_id=1, source_target_pairs={{0,32},{32,0},{64,96},{96,64},{1,33},{33,1},{65,97},{97,65},{2,34}... | collective-permute-start | bytes 24584 | tf_op jit(solution)/shard_map/ppermute | solution.py:43
  181.4 3.7 %collective-permute-start.29 = (f32[16,128]{1,0:T(8,128)S(1)}, f32[16,128]{1,0:T(8,128)S(1)}, u32[]{:S(2)}, u32[]{:S(2)}) collective-permute-start(f32[16,128]{1,0:T(8,128)S(1)} %add.70), channel_id=1, source_target_pairs={{0,96},{96,0},{32,64},{64,32},{1,97},{97,1},{33,65},{65,33},{2,98}... | collective-permute-start | bytes 24584 | tf_op jit(solution)/shard_map/ppermute | solution.py:44
  (1 other events, 0.7 us)

commit v3 on v2

--- a/solution.py
+++ b/solution.py
@@ -365,13 +365,15 @@
         mid, send_far = down([far], w_down, n, stats)
         mid = mid + swap_core(send_far).astype(f32)
         relay = along_x(mid.astype(bf16), 1)
-        mine_o, a_o, b_o, send = down([own, near], w_down, n, stats)
+        a_o, b_o, send = down([near], w_down, n, stats)
         got = swap_core(send)
-        to_a = (a_o + got[n : 2 * n].astype(f32)).astype(bf16)
+        to_a = (a_o + got[:n].astype(f32)).astype(bf16)
         from_b = along_x(to_a, -1)
         got_b, relay = tie((got, relay))
-        to_b = (b_o + got_b[2 * n :].astype(f32) + relay.astype(f32)).astype(bf16)
+        to_b = (b_o + got_b[n:].astype(f32) + relay.astype(f32)).astype(bf16)
         from_a = along_x(to_b, 1)
+        mine_o, send = down([own], w_down, n, stats)
+        got = swap_core(send)
         from_a, from_b, extra = fill_in(from_a, from_b)
         last = m + 1 == micros
         return finish(mine_o, got, from_a, from_b, counts, m, last), extra

time: 187 us -> 184 us (0.984)
  waiting for transfers between devices: 55.6 us -> 38.9 us
  starting transfers between devices: 37.1 us -> 46.4 us
  blocking collectives: 49.1 us -> 53.2 us
    ppermute x12, waiting for transfers between devices: 46.9 us -> 31.6 us  [along_x(): return lax.ppermute(v, (X, CORE), pairs)]
    ppermute x12, starting transfers between devices: 14.9 us -> 21.6 us  [along_x(): return lax.ppermute(v, (X, CORE), pairs)]
    all_to_all x3, blocking collectives: 49.1 us -> 53.2 us  [exchange(): lax.all_to_all(v.reshape(experts, rows // experts, width), PLANE, 0, 0, t...]
    ppermute x2, starting transfers between devices: 1.33 us -> 3.39 us  [line_sum(): return v + lax.ppermute(v, X, [(0, 3), (3, 0), (1, 2), (2, 1)])]
    pallas_call x17 -> x19, Pallas kernels: 39.7 us -> 40 us  [call(): pl.pallas_call(kernel, in_specs=specs or [WHOLE] * len(args), out_specs=[...]
    ppermute x14 -> x16, starting transfers between devices: 20.8 us -> 20.6 us  [swap_core(): return lax.ppermute(v, CORE, [(0, 1), (1, 0)])]
  transfers between devices with their start and end apart: 30 -> 32, of which waited for: 15 -> 11; matrix products, arithmetic and copies ran while one was open for 0% -> 0% of each run, Pallas kernels for 20% -> 20%
where the time goes in v3:
time: 184 us; the launch traced here: 183 us
  blocking collectives  53.2 us (29%)
  starting transfers between devices  46.4 us (25%)
  Pallas kernels  40 us (22%)
  waiting for transfers between devices  38.9 us (21%)
  local copies, waits for them, and re-layouts  1.98 us (1%)
    all_to_all x3, blocking collectives, exchange(): lax.all_to_all(v.reshape(experts, rows // experts, width), PLANE, 0, 0, t...  53.2 us
    pallas_call x19, Pallas kernels, call(): pl.pallas_call(kernel, in_specs=specs or [WHOLE] * len(args), out_specs=[...  40 us
    ppermute x12, waiting for transfers between devices, along_x(): return lax.ppermute(v, (X, CORE), pairs)  31.6 us
    ppermute x12, starting transfers between devices, along_x(): return lax.ppermute(v, (X, CORE), pairs)  21.6 us
    ppermute x16, starting transfers between devices, swap_core(): return lax.ppermute(v, CORE, [(0, 1), (1, 0)])  20.6 us
    ppermute x2, waiting for transfers between devices, line_sum(): v = v + lax.ppermute(v, X, [(0, 1), (1, 0), (2, 3), (3, 2)])  4.19 us
  transfers between devices with their start and end apart: 32, of which 11 were waited for; matrix products, arithmetic and copies ran while one was open for 0% of the time, Pallas kernels for 20%

profile of v3, /device:TPU:1, one launch (start us, length us, event | category | flops | bytes accessed | tf_op | source)
XLA Modules:
  0.0 182.9 jit_solution(9250602535696543385)
XLA Ops:
  3.4 25.2 %all_to_all.15 = bf16[16,8,4224]{2,1,0:T(8,128)(2,1)S(1)} all-to-all(bf16[16,8,4224]{2,1,0:T(8,128)(2,1)S(1)} %bitcast.7), channel_id=1, replica_groups=mesh['dp'=4,'expert_0'=4,'expert_1'=4,'expert_2'=2] {'expert_0','expert_1'}, dimensions={0} | all-to-all | bytes 2162688 | tf_op jit(solution)/shard_map/all_to_all | solution.py:333
  29.1 2.5 %collective-permute-start.2 = (bf16[64,4096]{1,0:T(8,128)(2,1)S(1)}, bf16[64,4096]{1,0:T(8,128)(2,1)S(1)}, u32[]{:S(2)}, u32[]{:S(2)}) collective-permute-start(bf16[64,4096]{1,0:T(8,128)(2,1)S(1)} %get-tuple-element.43.refs_0_), channel_id=1, source_target_pairs={{0,32},{1,97},{32,64},{33,1},{64,96},{65,33},{96,0},{97,65},{2,34}... | collective-permute-start | bytes 1572872 | tf_op jit(solution)/shard_map/ppermute | solution.py:34
  31.6 9.0 %collective-permute-done.2.refs_0_ = bf16[64,4096]{1,0:T(8,128)(2,1)S(1)} collective-permute-done((bf16[64,4096]{1,0:T(8,128)(2,1)S(1)}, bf16[64,4096]{1,0:T(8,128)(2,1)S(1)}, u32[]{:S(2)}, u32[]{:S(2)}) %collective-permute-start.2) | collective-permute-done | bytes 524320 | tf_op jit(solution)/shard_map/ppermute | solution.py:34
  40.6 3.4 %collective-permute-start.7 = (bf16[64,4096]{1,0:T(8,128)(2,1)S(1)}, bf16[64,4096]{1,0:T(8,128)(2,1)S(1)}, u32[]{:S(2)}, u32[]{:S(2)}) collective-permute-start(bf16[64,4096]{1,0:T(8,128)(2,1)S(1)} %collective-permute-done.2.refs_0_), channel_id=1, source_target_pairs={{0,32},{1,97},{32,64},{33,1},{64,96},{65,33},{96,0},{97,65},{2,34}... | collective-permute-start | bytes 1572872 | tf_op jit(solution)/shard_map/ppermute | solution.py:34
  44.0 2.3 %collective-permute-done.3.refs_1_ = bf16[64,4096]{1,0:T(8,128)(2,1)S(1)} collective-permute-done((bf16[64,4096]{1,0:T(8,128)(2,1)S(1)}, bf16[64,4096]{1,0:T(8,128)(2,1)S(1)}, u32[]{:S(2)}, u32[]{:S(2)}) %collective-permute-start.3) | collective-permute-done | bytes 524320 | tf_op jit(solution)/shard_map/ppermute | solution.py:34
  46.8 3.4 %collective-permute-done.7.refs_0_ = bf16[64,4096]{1,0:T(8,128)(2,1)S(1)} collective-permute-done((bf16[64,4096]{1,0:T(8,128)(2,1)S(1)}, bf16[64,4096]{1,0:T(8,128)(2,1)S(1)}, u32[]{:S(2)}, u32[]{:S(2)}) %collective-permute-start.7) | collective-permute-done | bytes 524320 | tf_op jit(solution)/shard_map/ppermute | solution.py:34
  50.2 6.9 %collective-permute-start.8 = (bf16[64,4096]{1,0:T(8,128)(2,1)S(1)}, bf16[64,4096]{1,0:T(8,128)(2,1)S(1)}, u32[]{:S(2)}, u32[]{:S(2)}) collective-permute-start(bf16[64,4096]{1,0:T(8,128)(2,1)S(1)} %collective-permute-done.7.refs_0_), channel_id=1, source_target_pairs={{0,1},{1,0},{2,3},{3,2},{4,5},{5,4},{6,7},{7,6},{8,9},{9,8},{10,11... | collective-permute-start | bytes 1572872 | tf_op jit(solution)/shard_map/ppermute | solution.py:38
  57.1 7.3 %shard_map.70 = (bf16[1,4096,896]{2,1,0:T(8,128)(2,1)S(1)}, bf16[1,4096,896]{2,1,0:T(8,128)(2,1)S(1)}, bf16[1,896,4096]{2,1,0:T(8,128)(2,1)S(1)}) custom-call(bf16[1,4096,896]{2,1,0:T(8,128)(2,1)} %refs_0_.1, bf16[1,4096,896]{2,1,0:T(8,128)(2,1)} %refs_1_.1, bf16[1,896,4096]{2,1,0:T(8,128)(2,1)} %refs_2_.2), custom_call_target="tpu_custom_call" | custom-call | tf_op jit(solution)/shard_map/pallas_call | solution.py:48
  64.4 4.0 %shard_map.73.refs_0_ = bf16[256,896]{1,0:T(8,128)(2,1)S(1)} custom-call(bf16[64,4096]{1,0:T(8,128)(2,1)S(1)} %collective-permute-done.2.refs_0_, bf16[64,4096]{1,0:T(8,128)(2,1)S(1)} %collective-permute-done.3.refs_1_, bf16[64,4096]{1,0:T(8,128)(2,1)S(1)} %collective-permute-done.4.refs_2_, bf16[64,4096]{1,0:T(8,128)(2,1)S(1)} %collective-permute-done.5.refs_3_, ...), custom_call_target="tpu_custom_call" | custom-call | tf_op jit(solution)/shard_map/pallas_call | solution.py:48
  68.5 2.7 %collective-permute-start.13 = (bf16[64,4096]{1,0:T(8,128)(2,1)S(1)}, bf16[64,4096]{1,0:T(8,128)(2,1)S(1)}, u32[]{:S(2)}, u32[]{:S(2)}) collective-permute-start(bf16[64,4096]{1,0:T(8,128)(2,1)S(1)} %get-tuple-element.58.refs_0_), channel_id=1, source_target_pairs={{0,32},{1,97},{32,64},{33,1},{64,96},{65,33},{96,0},{97,65},{2,34}... | collective-permute-start | bytes 1572872 | tf_op jit(solution)/shard_map/ppermute | solution.py:34
  71.1 2.1 %shard_map.75.refs_0_ = bf16[128,896]{1,0:T(8,128)(2,1)S(1)} custom-call(bf16[64,4096]{1,0:T(8,128)(2,1)S(1)} %collective-permute-done.7.refs_0_, bf16[64,4096]{1,0:T(8,128)(2,1)S(1)} %collective-permute-done.8.refs_1_, bf16[1,4096,896]{2,1,0:T(8,128)(2,1)S(1)} %get-tuple-element.44.refs_2_.refs_4_, bf16[1,4096,896]{2,1,0:T(8,128)(2,1)S(1)} %get-tuple-element.45.refs_3_.refs_5_), custom_call_target="tpu_custom_call" | custom-call | tf_op jit(solution)/shard_map/pallas_call | solution.py:48
  74.7 2.6 %shard_map.74 = (f32[64,4096]{1,0:T(8,128)S(1)}, f32[64,4096]{1,0:T(8,128)S(1)}, bf16[128,4096]{1,0:T(8,128)(2,1)S(1)}) custom-call(bf16[256,896]{1,0:T(8,128)(2,1)S(1)} %shard_map.73.refs_0_, bf16[1,896,4096]{2,1,0:T(8,128)(2,1)S(1)} %get-tuple-element.46.refs_1_.refs_3_), custom_call_target="tpu_custom_call" | custom-call | tf_op jit(solution)/shard_map/pallas_call | solution.py:48
  77.9 4.2 %collective-permute-done.13.refs_0_ = bf16[64,4096]{1,0:T(8,128)(2,1)S(1)} collective-permute-done((bf16[64,4096]{1,0:T(8,128)(2,1)S(1)}, bf16[64,4096]{1,0:T(8,128)(2,1)S(1)}, u32[]{:S(2)}, u32[]{:S(2)}) %collective-permute-start.13) | collective-permute-done | bytes 524320 | tf_op jit(solution)/shard_map/ppermute | solution.py:34
  84.2 3.0 %collective-permute-start.10 = (bf16[64,4096]{1,0:T(8,128)(2,1)S(1)}, bf16[64,4096]{1,0:T(8,128)(2,1)S(1)}, u32[]{:S(2)}, u32[]{:S(2)}) collective-permute-start(bf16[64,4096]{1,0:T(8,128)(2,1)S(1)} %add_convert_fusion.5), channel_id=1, source_target_pairs={{0,32},{1,97},{32,64},{33,1},{64,96},{65,33},{96,0},{97,65},{2,34}... | collective-permute-start | bytes 1572872 | tf_op jit(solution)/shard_map/ppermute | solution.py:34
  87.3 8.7 %collective-permute-done.10 = bf16[64,4096]{1,0:T(8,128)(2,1)S(1)} collective-permute-done((bf16[64,4096]{1,0:T(8,128)(2,1)S(1)}, bf16[64,4096]{1,0:T(8,128)(2,1)S(1)}, u32[]{:S(2)}, u32[]{:S(2)}) %collective-permute-start.10) | collective-permute-done | bytes 524320 | tf_op jit(solution)/shard_map/ppermute | solution.py:34
  96.2 2.7 %collective-permute-start.11 = (bf16[64,4096]{1,0:T(8,128)(2,1)S(1)}, bf16[64,4096]{1,0:T(8,128)(2,1)S(1)}, u32[]{:S(2)}, u32[]{:S(2)}) collective-permute-start(bf16[64,4096]{1,0:T(8,128)(2,1)S(1)} %add_convert_fusion.4), channel_id=1, source_target_pairs={{0,32},{1,97},{32,64},{33,1},{64,96},{65,33},{96,0},{97,65},{2,34}... | collective-permute-start | bytes 1572872 | tf_op jit(solution)/shard_map/ppermute | solution.py:34
  99.0 2.1 %shard_map.71.refs_0_ = bf16[128,896]{1,0:T(8,128)(2,1)S(1)} custom-call(bf16[64,4096]{1,0:T(8,128)(2,1)S(1)} %get-tuple-element.43.refs_0_, bf16[64,4096]{1,0:T(8,128)(2,1)S(1)} %collective-permute-done.refs_1_, bf16[1,4096,896]{2,1,0:T(8,128)(2,1)S(1)} %get-tuple-element.44.refs_2_.refs_4_, bf16[1,4096,896]{2,1,0:T(8,128)(2,1)S(1)} %get-tuple-element.45.refs_3_.refs_5_), custom_call_target="tpu_custom_call" | custom-call | tf_op jit(solution)/shard_map/pallas_call | solution.py:48
  102.4 3.4 %collective-permute-start.1 = (bf16[64,4096]{1,0:T(8,128)(2,1)S(1)}, bf16[64,4096]{1,0:T(8,128)(2,1)S(1)}, u32[]{:S(2)}, u32[]{:S(2)}) collective-permute-start(bf16[64,4096]{1,0:T(8,128)(2,1)S(1)} %get-tuple-element.48), channel_id=1, source_target_pairs={{0,1},{1,0},{2,3},{3,2},{4,5},{5,4},{6,7},{7,6},{8,9},{9,8},{10,11... | collective-permute-start | bytes 1572872 | tf_op jit(solution)/shard_map/ppermute | solution.py:38
  105.9 3.9 %shard_map.77 = (f32[256,896]{1,0:T(8,128)S(1)}, f32[256,896]{1,0:T(8,128)S(1)}) custom-call(bf16[64,4096]{1,0:T(8,128)(2,1)S(1)} %collective-permute-done.13.refs_0_, bf16[64,4096]{1,0:T(8,128)(2,1)S(1)} %collective-permute-done.14.refs_1_, bf16[64,4096]{1,0:T(8,128)(2,1)S(1)} %collective-permute-done.15.refs_2_, ...), custom_call_target="tpu_custom_call" | custom-call | tf_op jit(solution)/shard_map/pallas_call | solution.py:48
  116.1 2.9 %collective-permute-start.19 = (f32[8,128]{1,0:T(8,128)S(1)}, f32[8,128]{1,0:T(8,128)S(1)}, u32[]{:S(2)}, u32[]{:S(2)}) collective-permute-start(f32[8,128]{1,0:T(8,128)S(1)} %add.63), channel_id=1, source_target_pairs={{0,96},{96,0},{32,64},{64,32},{1,97},{97,1},{33,65},{65,33},{2,98}... | collective-permute-start | bytes 12296 | tf_op jit(solution)/shard_map/ppermute | solution.py:44
  119.0 2.1 %shard_map.81 = (f32[128,896]{1,0:T(8,128)S(1)}, f32[128,896]{1,0:T(8,128)S(1)}) custom-call(bf16[64,4096]{1,0:T(8,128)(2,1)S(1)} %collective-permute-done.21.refs_0_, bf16[64,4096]{1,0:T(8,128)(2,1)S(1)} %collective-permute-done.22.refs_1_, bf16[1,4096,896]{2,1,0:T(8,128)(2,1)S(1)} %get-tuple-element.44.refs_2_.refs_4_, ...), custom_call_target="tpu_custom_call" | custom-call | tf_op jit(solution)/shard_map/pallas_call | solution.py:48
  122.5 1.9 %collective-permute-start.23 = (bf16[64,4096]{1,0:T(8,128)(2,1)S(1)}, bf16[64,4096]{1,0:T(8,128)(2,1)S(1)}, u32[]{:S(2)}, u32[]{:S(2)}) collective-permute-start(bf16[64,4096]{1,0:T(8,128)(2,1)S(1)} %get-tuple-element.72), channel_id=1, source_target_pairs={{0,1},{1,0},{2,3},{3,2},{4,5},{5,4},{6,7},{7,6},{8,9},{9,8},{10,11... | collective-permute-start | bytes 1572872 | tf_op jit(solution)/shard_map/ppermute | solution.py:38
  124.5 3.0 %shard_map.80 = (f32[64,4096]{1,0:T(8,128)S(1)}, f32[64,4096]{1,0:T(8,128)S(1)}, bf16[128,4096]{1,0:T(8,128)(2,1)S(1)}) custom-call(f32[8,128]{1,0:T(8,128)S(1)} %add.64.refs_0_, f32[256,896]{1,0:T(8,128)S(1)} %get-tuple-element.65.refs_1_, f32[256,896]{1,0:T(8,128)S(1)} %get-tuple-element.66.refs_2_, bf16[1,896,4096]{2,1,0:T(8,128)(2,1)S(1)} %get-tuple-element.46.refs_1_.refs_3_), custom_call_target="tpu_custom_call" | custom-call | tf_op jit(solution)/shard_map/pallas_call | solution.py:48
  128.1 2.5 %collective-permute-start.24 = (bf16[64,4096]{1,0:T(8,128)(2,1)S(1)}, bf16[64,4096]{1,0:T(8,128)(2,1)S(1)}, u32[]{:S(2)}, u32[]{:S(2)}) collective-permute-start(bf16[64,4096]{1,0:T(8,128)(2,1)S(1)} %add_convert_fusion.2), channel_id=1, source_target_pairs={{0,32},{1,97},{32,64},{33,1},{64,96},{65,33},{96,0},{97,65},{2,34}... | collective-permute-start | bytes 1572872 | tf_op jit(solution)/shard_map/ppermute | solution.py:34
  130.6 2.1 %shard_map.83 = (f32[128,896]{1,0:T(8,128)S(1)}, f32[128,896]{1,0:T(8,128)S(1)}) custom-call(bf16[64,4096]{1,0:T(8,128)(2,1)S(1)} %get-tuple-element.58.refs_0_, bf16[64,4096]{1,0:T(8,128)(2,1)S(1)} %collective-permute-done.27.refs_1_, bf16[1,4096,896]{2,1,0:T(8,128)(2,1)S(1)} %get-tuple-element.44.refs_2_.refs_4_, ...), custom_call_target="tpu_custom_call" | custom-call | tf_op jit(solution)/shard_map/pallas_call | solution.py:48
  132.7 4.0 %collective-permute-done.24 = bf16[64,4096]{1,0:T(8,128)(2,1)S(1)} collective-permute-done((bf16[64,4096]{1,0:T(8,128)(2,1)S(1)}, bf16[64,4096]{1,0:T(8,128)(2,1)S(1)}, u32[]{:S(2)}, u32[]{:S(2)}) %collective-permute-start.24) | collective-permute-done | bytes 524320 | tf_op jit(solution)/shard_map/ppermute | solution.py:34
  136.9 3.2 %collective-permute-start.25 = (bf16[64,4096]{1,0:T(8,128)(2,1)S(1)}, bf16[64,4096]{1,0:T(8,128)(2,1)S(1)}, u32[]{:S(2)}, u32[]{:S(2)}) collective-permute-start(bf16[64,4096]{1,0:T(8,128)(2,1)S(1)} %add_convert_fusion.1), channel_id=1, source_target_pairs={{0,32},{1,97},{32,64},{33,1},{64,96},{65,33},{96,0},{97,65},{2,34}... | collective-permute-start | bytes 1572872 | tf_op jit(solution)/shard_map/ppermute | solution.py:34
  141.8 2.1 %collective-permute-start.28 = (bf16[64,4096]{1,0:T(8,128)(2,1)S(1)}, bf16[64,4096]{1,0:T(8,128)(2,1)S(1)}, u32[]{:S(2)}, u32[]{:S(2)}) collective-permute-start(bf16[64,4096]{1,0:T(8,128)(2,1)S(1)} %get-tuple-element.81), channel_id=1, source_target_pairs={{0,1},{1,0},{2,3},{3,2},{4,5},{5,4},{6,7},{7,6},{8,9},{9,8},{10,11... | collective-permute-start | bytes 1572872 | tf_op jit(solution)/shard_map/ppermute | solution.py:38
  143.9 14.0 %all_to_all.16 = bf16[16,8,2048]{2,1,0:T(8,128)(2,1)S(1)} all-to-all(bf16[16,8,2048]{2,1,0:T(8,128)(2,1)S(1)} %bitcast.10), channel_id=1, replica_groups=mesh['dp'=4,'expert_0'=4,'expert_1'=4,'expert_2'=2] {'expert_0','expert_1'}, dimensions={0} | all-to-all | bytes 1048576 | tf_op jit(solution)/shard_map/all_to_all | solution.py:333
  159.0 14.1 %all_to_all.17 = bf16[16,8,2176]{2,1,0:T(8,128)(2,1)S(1)} all-to-all(bf16[16,8,2176]{2,1,0:T(8,128)(2,1)S(1)} %bitcast.8), channel_id=1, replica_groups=mesh['dp'=4,'expert_0'=4,'expert_1'=4,'expert_2'=2] {'expert_0','expert_1'}, dimensions={0} | all-to-all | bytes 1114112 | tf_op jit(solution)/shard_map/all_to_all | solution.py:333
  173.1 2.0 %collective-permute-start.29 = (f32[16,128]{1,0:T(8,128)S(1)}, f32[16,128]{1,0:T(8,128)S(1)}, u32[]{:S(2)}, u32[]{:S(2)}) collective-permute-start(f32[16,128]{1,0:T(8,128)S(1)} %convert_element_type.59), channel_id=1, source_target_pairs={{0,1},{1,0},{2,3},{3,2},{4,5},{5,4},{6,7},{7,6},{8,9},{9,8},{10,11... | collective-permute-start | bytes 24584 | tf_op jit(solution)/shard_map/ppermute | solution.py:38
  176.0 2.5 %collective-permute-done.30 = f32[16,128]{1,0:T(8,128)S(1)} collective-permute-done((f32[16,128]{1,0:T(8,128)S(1)}, f32[16,128]{1,0:T(8,128)S(1)}, u32[]{:S(2)}, u32[]{:S(2)}) %collective-permute-start.30) | collective-permute-done | bytes 8224 | tf_op jit(solution)/shard_map/ppermute | solution.py:43
  (76 shorter events, 26.2 us)
Async XLA Ops:
  29.1 11.6 %collective-permute-start.2 = (bf16[64,4096]{1,0:T(8,128)(2,1)S(1)}, bf16[64,4096]{1,0:T(8,128)(2,1)S(1)}, u32[]{:S(2)}, u32[]{:S(2)}) collective-permute-start(bf16[64,4096]{1,0:T(8,128)(2,1)S(1)} %get-tuple-element.43.refs_0_), channel_id=1, source_target_pairs={{0,32},{1,97},{32,64},{33,1},{64,96},{65,33},{96,0},{97,65},{2,34}... | collective-permute-start | bytes 1572872 | tf_op jit(solution)/shard_map/ppermute | solution.py:34
  31.6 14.7 %collective-permute-start.3 = (bf16[64,4096]{1,0:T(8,128)(2,1)S(1)}, bf16[64,4096]{1,0:T(8,128)(2,1)S(1)}, u32[]{:S(2)}, u32[]{:S(2)}) collective-permute-start(bf16[64,4096]{1,0:T(8,128)(2,1)S(1)} %get-tuple-element.43.refs_0_), channel_id=1, source_target_pairs={{0,96},{1,33},{32,0},{33,65},{64,32},{65,97},{96,64},{97,1},{2,98}... | collective-permute-start | bytes 1572872 | tf_op jit(solution)/shard_map/ppermute | solution.py:34
  40.6 9.5 %collective-permute-start.7 = (bf16[64,4096]{1,0:T(8,128)(2,1)S(1)}, bf16[64,4096]{1,0:T(8,128)(2,1)S(1)}, u32[]{:S(2)}, u32[]{:S(2)}) collective-permute-start(bf16[64,4096]{1,0:T(8,128)(2,1)S(1)} %collective-permute-done.2.refs_0_), channel_id=1, source_target_pairs={{0,32},{1,97},{32,64},{33,1},{64,96},{65,33},{96,0},{97,65},{2,34}... | collective-permute-start | bytes 1572872 | tf_op jit(solution)/shard_map/ppermute | solution.py:34
  46.3 18.1 %collective-permute-start.5 = (bf16[64,4096]{1,0:T(8,128)(2,1)S(1)}, bf16[64,4096]{1,0:T(8,128)(2,1)S(1)}, u32[]{:S(2)}, u32[]{:S(2)}) collective-permute-start(bf16[64,4096]{1,0:T(8,128)(2,1)S(1)} %collective-permute-done.3.refs_1_), channel_id=1, source_target_pairs={{0,1},{1,0},{2,3},{3,2},{4,5},{5,4},{6,7},{7,6},{8,9},{9,8},{10,11... | collective-permute-start | bytes 1572872 | tf_op jit(solution)/shard_map/ppermute | solution.py:38
  46.7 17.7 %collective-permute-start.4 = (bf16[64,4096]{1,0:T(8,128)(2,1)S(1)}, bf16[64,4096]{1,0:T(8,128)(2,1)S(1)}, u32[]{:S(2)}, u32[]{:S(2)}) collective-permute-start(bf16[64,4096]{1,0:T(8,128)(2,1)S(1)} %collective-permute-done.2.refs_0_), channel_id=1, source_target_pairs={{0,1},{1,0},{2,3},{3,2},{4,5},{5,4},{6,7},{7,6},{8,9},{9,8},{10,11... | collective-permute-start | bytes 1572872 | tf_op jit(solution)/shard_map/ppermute | solution.py:38
  50.2 21.0 %collective-permute-start.8 = (bf16[64,4096]{1,0:T(8,128)(2,1)S(1)}, bf16[64,4096]{1,0:T(8,128)(2,1)S(1)}, u32[]{:S(2)}, u32[]{:S(2)}) collective-permute-start(bf16[64,4096]{1,0:T(8,128)(2,1)S(1)} %collective-permute-done.7.refs_0_), channel_id=1, source_target_pairs={{0,1},{1,0},{2,3},{3,2},{4,5},{5,4},{6,7},{7,6},{8,9},{9,8},{10,11... | collective-permute-start | bytes 1572872 | tf_op jit(solution)/shard_map/ppermute | solution.py:38
  68.4 15.1 %collective-permute-start.14 = (bf16[64,4096]{1,0:T(8,128)(2,1)S(1)}, bf16[64,4096]{1,0:T(8,128)(2,1)S(1)}, u32[]{:S(2)}, u32[]{:S(2)}) collective-permute-start(bf16[64,4096]{1,0:T(8,128)(2,1)S(1)} %get-tuple-element.58.refs_0_), channel_id=1, source_target_pairs={{0,96},{1,33},{32,0},{33,65},{64,32},{65,97},{96,64},{97,1},{2,98}... | collective-permute-start | bytes 1572872 | tf_op jit(solution)/shard_map/ppermute | solution.py:34
  68.5 13.6 %collective-permute-start.13 = (bf16[64,4096]{1,0:T(8,128)(2,1)S(1)}, bf16[64,4096]{1,0:T(8,128)(2,1)S(1)}, u32[]{:S(2)}, u32[]{:S(2)}) collective-permute-start(bf16[64,4096]{1,0:T(8,128)(2,1)S(1)} %get-tuple-element.58.refs_0_), channel_id=1, source_target_pairs={{0,32},{1,97},{32,64},{33,1},{64,96},{65,33},{96,0},{97,65},{2,34}... | collective-permute-start | bytes 1572872 | tf_op jit(solution)/shard_map/ppermute | solution.py:34
  74.6 9.5 %collective-permute-start.9 = (bf16[64,4096]{1,0:T(8,128)(2,1)S(1)}, bf16[64,4096]{1,0:T(8,128)(2,1)S(1)}, u32[]{:S(2)}, u32[]{:S(2)}) collective-permute-start(bf16[64,4096]{1,0:T(8,128)(2,1)S(1)} %get-tuple-element.54), channel_id=1, source_target_pairs={{0,1},{1,0},{2,3},{3,2},{4,5},{5,4},{6,7},{7,6},{8,9},{9,8},{10,11... | collective-permute-start | bytes 1572872 | tf_op jit(solution)/shard_map/ppermute | solution.py:38
  77.2 7.0 %collective-permute-start.6 = (bf16[128,4096]{1,0:T(8,128)(2,1)S(1)}, bf16[128,4096]{1,0:T(8,128)(2,1)S(1)}, u32[]{:S(2)}, u32[]{:S(2)}) collective-permute-start(bf16[128,4096]{1,0:T(8,128)(2,1)S(1)} %get-tuple-element.52), channel_id=1, source_target_pairs={{0,1},{1,0},{2,3},{3,2},{4,5},{5,4},{6,7},{7,6},{8,9},{9,8},{10,11... | collective-permute-start | bytes 3145736 | tf_op jit(solution)/shard_map/ppermute | solution.py:38
  77.8 18.4 %collective-permute-start = (bf16[64,4096]{1,0:T(8,128)(2,1)S(1)}, bf16[64,4096]{1,0:T(8,128)(2,1)S(1)}, u32[]{:S(2)}, u32[]{:S(2)}) collective-permute-start(bf16[64,4096]{1,0:T(8,128)(2,1)S(1)} %get-tuple-element.43.refs_0_), channel_id=1, source_target_pairs={{0,1},{1,0},{2,3},{3,2},{4,5},{5,4},{6,7},{7,6},{8,9},{9,8},{10,11... | collective-permute-start | bytes 1572872 | tf_op jit(solution)/shard_map/ppermute | solution.py:38
  82.1 23.7 %collective-permute-start.21 = (bf16[64,4096]{1,0:T(8,128)(2,1)S(1)}, bf16[64,4096]{1,0:T(8,128)(2,1)S(1)}, u32[]{:S(2)}, u32[]{:S(2)}) collective-permute-start(bf16[64,4096]{1,0:T(8,128)(2,1)S(1)} %collective-permute-done.13.refs_0_), channel_id=1, source_target_pairs={{0,32},{1,97},{32,64},{33,1},{64,96},{65,33},{96,0},{97,65},{2,34}... | collective-permute-start | bytes 1572872 | tf_op jit(solution)/shard_map/ppermute | solution.py:34
  83.5 22.4 %collective-permute-start.15 = (bf16[64,4096]{1,0:T(8,128)(2,1)S(1)}, bf16[64,4096]{1,0:T(8,128)(2,1)S(1)}, u32[]{:S(2)}, u32[]{:S(2)}) collective-permute-start(bf16[64,4096]{1,0:T(8,128)(2,1)S(1)} %collective-permute-done.13.refs_0_), channel_id=1, source_target_pairs={{0,1},{1,0},{2,3},{3,2},{4,5},{5,4},{6,7},{7,6},{8,9},{9,8},{10,11... | collective-permute-start | bytes 1572872 | tf_op jit(solution)/shard_map/ppermute | solution.py:38
  84.0 18.4 %collective-permute-start.16 = (bf16[64,4096]{1,0:T(8,128)(2,1)S(1)}, bf16[64,4096]{1,0:T(8,128)(2,1)S(1)}, u32[]{:S(2)}, u32[]{:S(2)}) collective-permute-start(bf16[64,4096]{1,0:T(8,128)(2,1)S(1)} %collective-permute-done.14.refs_1_), channel_id=1, source_target_pairs={{0,1},{1,0},{2,3},{3,2},{4,5},{5,4},{6,7},{7,6},{8,9},{9,8},{10,11... | collective-permute-start | bytes 1572872 | tf_op jit(solution)/shard_map/ppermute | solution.py:38
  84.2 11.8 %collective-permute-start.10 = (bf16[64,4096]{1,0:T(8,128)(2,1)S(1)}, bf16[64,4096]{1,0:T(8,128)(2,1)S(1)}, u32[]{:S(2)}, u32[]{:S(2)}) collective-permute-start(bf16[64,4096]{1,0:T(8,128)(2,1)S(1)} %add_convert_fusion.5), channel_id=1, source_target_pairs={{0,32},{1,97},{32,64},{33,1},{64,96},{65,33},{96,0},{97,65},{2,34}... | collective-permute-start | bytes 1572872 | tf_op jit(solution)/shard_map/ppermute | solution.py:34
  96.0 13.8 %collective-permute-start.12 = (bf16[64,4096]{1,0:T(8,128)(2,1)S(1)}, bf16[64,4096]{1,0:T(8,128)(2,1)S(1)}, u32[]{:S(2)}, u32[]{:S(2)}) collective-permute-start(bf16[64,4096]{1,0:T(8,128)(2,1)S(1)} %add_convert_fusion.3), channel_id=1, source_target_pairs={{0,96},{1,33},{32,0},{33,65},{64,32},{65,97},{96,64},{97,1},{2,98}... | collective-permute-start | bytes 1572872 | tf_op jit(solution)/shard_map/ppermute | solution.py:34
  96.2 13.7 %collective-permute-start.11 = (bf16[64,4096]{1,0:T(8,128)(2,1)S(1)}, bf16[64,4096]{1,0:T(8,128)(2,1)S(1)}, u32[]{:S(2)}, u32[]{:S(2)}) collective-permute-start(bf16[64,4096]{1,0:T(8,128)(2,1)S(1)} %add_convert_fusion.4), channel_id=1, source_target_pairs={{0,32},{1,97},{32,64},{33,1},{64,96},{65,33},{96,0},{97,65},{2,34}... | collective-permute-start | bytes 1572872 | tf_op jit(solution)/shard_map/ppermute | solution.py:34
  102.4 7.5 %collective-permute-start.1 = (bf16[64,4096]{1,0:T(8,128)(2,1)S(1)}, bf16[64,4096]{1,0:T(8,128)(2,1)S(1)}, u32[]{:S(2)}, u32[]{:S(2)}) collective-permute-start(bf16[64,4096]{1,0:T(8,128)(2,1)S(1)} %get-tuple-element.48), channel_id=1, source_target_pairs={{0,1},{1,0},{2,3},{3,2},{4,5},{5,4},{6,7},{7,6},{8,9},{9,8},{10,11... | collective-permute-start | bytes 1572872 | tf_op jit(solution)/shard_map/ppermute | solution.py:38
  105.8 13.2 %collective-permute-start.22 = (bf16[64,4096]{1,0:T(8,128)(2,1)S(1)}, bf16[64,4096]{1,0:T(8,128)(2,1)S(1)}, u32[]{:S(2)}, u32[]{:S(2)}) collective-permute-start(bf16[64,4096]{1,0:T(8,128)(2,1)S(1)} %collective-permute-done.21.refs_0_), channel_id=1, source_target_pairs={{0,1},{1,0},{2,3},{3,2},{4,5},{5,4},{6,7},{7,6},{8,9},{9,8},{10,11... | collective-permute-start | bytes 1572872 | tf_op jit(solution)/shard_map/ppermute | solution.py:38
  111.0 2.6 %collective-permute-start.17 = (f32[8,128]{1,0:T(8,128)S(1)}, f32[8,128]{1,0:T(8,128)S(1)}, u32[]{:S(2)}, u32[]{:S(2)}) collective-permute-start(f32[8,128]{1,0:T(8,128)S(1)} %get-tuple-element.64), channel_id=1, source_target_pairs={{0,1},{1,0},{2,3},{3,2},{4,5},{5,4},{6,7},{7,6},{8,9},{9,8},{10,11... | collective-permute-start | bytes 12296 | tf_op jit(solution)/shard_map/ppermute | solution.py:38
  113.6 2.5 %collective-permute-start.18 = (f32[8,128]{1,0:T(8,128)S(1)}, f32[8,128]{1,0:T(8,128)S(1)}, u32[]{:S(2)}, u32[]{:S(2)}) collective-permute-start(f32[8,128]{1,0:T(8,128)S(1)} %add.62), channel_id=1, source_target_pairs={{0,32},{32,0},{64,96},{96,64},{1,33},{33,1},{65,97},{97,65},{2,34}... | collective-permute-start | bytes 12296 | tf_op jit(solution)/shard_map/ppermute | solution.py:43
  116.1 5.0 %collective-permute-start.19 = (f32[8,128]{1,0:T(8,128)S(1)}, f32[8,128]{1,0:T(8,128)S(1)}, u32[]{:S(2)}, u32[]{:S(2)}) collective-permute-start(f32[8,128]{1,0:T(8,128)S(1)} %add.63), channel_id=1, source_target_pairs={{0,96},{96,0},{32,64},{64,32},{1,97},{97,1},{33,65},{65,33},{2,98}... | collective-permute-start | bytes 12296 | tf_op jit(solution)/shard_map/ppermute | solution.py:44
  122.5 5.5 %collective-permute-start.23 = (bf16[64,4096]{1,0:T(8,128)(2,1)S(1)}, bf16[64,4096]{1,0:T(8,128)(2,1)S(1)}, u32[]{:S(2)}, u32[]{:S(2)}) collective-permute-start(bf16[64,4096]{1,0:T(8,128)(2,1)S(1)} %get-tuple-element.72), channel_id=1, source_target_pairs={{0,1},{1,0},{2,3},{3,2},{4,5},{5,4},{6,7},{7,6},{8,9},{9,8},{10,11... | collective-permute-start | bytes 1572872 | tf_op jit(solution)/shard_map/ppermute | solution.py:38
  124.4 6.2 %collective-permute-start.27 = (bf16[64,4096]{1,0:T(8,128)(2,1)S(1)}, bf16[64,4096]{1,0:T(8,128)(2,1)S(1)}, u32[]{:S(2)}, u32[]{:S(2)}) collective-permute-start(bf16[64,4096]{1,0:T(8,128)(2,1)S(1)} %get-tuple-element.58.refs_0_), channel_id=1, source_target_pairs={{0,1},{1,0},{2,3},{3,2},{4,5},{5,4},{6,7},{7,6},{8,9},{9,8},{10,11... | collective-permute-start | bytes 1572872 | tf_op jit(solution)/shard_map/ppermute | solution.py:38
  127.5 9.3 %collective-permute-start.20 = (bf16[128,4096]{1,0:T(8,128)(2,1)S(1)}, bf16[128,4096]{1,0:T(8,128)(2,1)S(1)}, u32[]{:S(2)}, u32[]{:S(2)}) collective-permute-start(bf16[128,4096]{1,0:T(8,128)(2,1)S(1)} %get-tuple-element.68), channel_id=1, source_target_pairs={{0,1},{1,0},{2,3},{3,2},{4,5},{5,4},{6,7},{7,6},{8,9},{9,8},{10,11... | collective-permute-start | bytes 3145736 | tf_op jit(solution)/shard_map/ppermute | solution.py:38
  128.1 8.6 %collective-permute-start.24 = (bf16[64,4096]{1,0:T(8,128)(2,1)S(1)}, bf16[64,4096]{1,0:T(8,128)(2,1)S(1)}, u32[]{:S(2)}, u32[]{:S(2)}) collective-permute-start(bf16[64,4096]{1,0:T(8,128)(2,1)S(1)} %add_convert_fusion.2), channel_id=1, source_target_pairs={{0,32},{1,97},{32,64},{33,1},{64,96},{65,33},{96,0},{97,65},{2,34}... | collective-permute-start | bytes 1572872 | tf_op jit(solution)/shard_map/ppermute | solution.py:34
  136.9 20.9 %collective-permute-start.25 = (bf16[64,4096]{1,0:T(8,128)(2,1)S(1)}, bf16[64,4096]{1,0:T(8,128)(2,1)S(1)}, u32[]{:S(2)}, u32[]{:S(2)}) collective-permute-start(bf16[64,4096]{1,0:T(8,128)(2,1)S(1)} %add_convert_fusion.1), channel_id=1, source_target_pairs={{0,32},{1,97},{32,64},{33,1},{64,96},{65,33},{96,0},{97,65},{2,34}... | collective-permute-start | bytes 1572872 | tf_op jit(solution)/shard_map/ppermute | solution.py:34
  140.3 17.6 %collective-permute-start.26 = (bf16[64,4096]{1,0:T(8,128)(2,1)S(1)}, bf16[64,4096]{1,0:T(8,128)(2,1)S(1)}, u32[]{:S(2)}, u32[]{:S(2)}) collective-permute-start(bf16[64,4096]{1,0:T(8,128)(2,1)S(1)} %add_convert_fusion), channel_id=1, source_target_pairs={{0,96},{1,33},{32,0},{33,65},{64,32},{65,97},{96,64},{97,1},{2,98}... | collective-permute-start | bytes 1572872 | tf_op jit(solution)/shard_map/ppermute | solution.py:34
  141.8 16.1 %collective-permute-start.28 = (bf16[64,4096]{1,0:T(8,128)(2,1)S(1)}, bf16[64,4096]{1,0:T(8,128)(2,1)S(1)}, u32[]{:S(2)}, u32[]{:S(2)}) collective-permute-start(bf16[64,4096]{1,0:T(8,128)(2,1)S(1)} %get-tuple-element.81), channel_id=1, source_target_pairs={{0,1},{1,0},{2,3},{3,2},{4,5},{5,4},{6,7},{7,6},{8,9},{9,8},{10,11... | collective-permute-start | bytes 1572872 | tf_op jit(solution)/shard_map/ppermute | solution.py:38
  173.1 2.9 %collective-permute-start.29 = (f32[16,128]{1,0:T(8,128)S(1)}, f32[16,128]{1,0:T(8,128)S(1)}, u32[]{:S(2)}, u32[]{:S(2)}) collective-permute-start(f32[16,128]{1,0:T(8,128)S(1)} %convert_element_type.59), channel_id=1, source_target_pairs={{0,1},{1,0},{2,3},{3,2},{4,5},{5,4},{6,7},{7,6},{8,9},{9,8},{10,11... | collective-permute-start | bytes 24584 | tf_op jit(solution)/shard_map/ppermute | solution.py:38
  176.0 2.5 %collective-permute-start.30 = (f32[16,128]{1,0:T(8,128)S(1)}, f32[16,128]{1,0:T(8,128)S(1)}, u32[]{:S(2)}, u32[]{:S(2)}) collective-permute-start(f32[16,128]{1,0:T(8,128)S(1)} %convert_add_fusion), channel_id=1, source_target_pairs={{0,32},{32,0},{64,96},{96,64},{1,33},{33,1},{65,97},{97,65},{2,34}... | collective-permute-start | bytes 24584 | tf_op jit(solution)/shard_map/ppermute | solution.py:43
  178.5 3.7 %collective-permute-start.31 = (f32[16,128]{1,0:T(8,128)S(1)}, f32[16,128]{1,0:T(8,128)S(1)}, u32[]{:S(2)}, u32[]{:S(2)}) collective-permute-start(f32[16,128]{1,0:T(8,128)S(1)} %add.70), channel_id=1, source_target_pairs={{0,96},{96,0},{32,64},{64,32},{1,97},{97,1},{33,65},{65,33},{2,98}... | collective-permute-start | bytes 24584 | tf_op jit(solution)/shard_map/ppermute | solution.py:44
  (3 other events, 40.6 us)

commit v4 on v3

--- a/solution.py
+++ b/solution.py
@@ -39,8 +39,11 @@
 
 
 def line_sum(v):
-    v = v + swap_core(v)
-    v = v + lax.ppermute(v, X, [(0, 1), (1, 0), (2, 3), (3, 2)])
+    near = swap_core(v)
+    cores = [(x, c) for x in range(lax.axis_size(X)) for c in range(2)]
+    across = lax.ppermute(v, (X, CORE), [(2 * x + c, 2 * (x ^ 1) + c) for x, c in cores])
+    corner = lax.ppermute(v, (X, CORE), [(2 * x + c, 2 * (x ^ 1) + 1 - c) for x, c in cores])
+    v = (v + near) + (across + corner)
     return v + lax.ppermute(v, X, [(0, 3), (3, 0), (1, 2), (2, 1)])
 
 

time: 184 us -> 183 us (level)
  waiting for transfers between devices: 38.9 us -> 36.6 us
    ppermute x2 -> x4, starting transfers between devices: 0.77 us -> 6.74 us  [the longest x2 5.95 us: line_sum(): lax.ppermute(v, (X, CORE), [(2 * x + c, 2 * (x ^ 1) + 1 - c) for x, c in...]
    ppermute x16, starting transfers between devices: 20.6 us -> 16.4 us  [swap_core(): return lax.ppermute(v, CORE, [(0, 1), (1, 0)])]
    ppermute x2 -> x4, waiting for transfers between devices: 4.19 us -> 3.57 us  [the longest x2 2.2 us: line_sum(): lax.ppermute(v, (X, CORE), [(2 * x + c, 2 * (x ^ 1) + 1 - c) for x, c in...]
  transfers between devices with their start and end apart: 32 -> 34, of which waited for: 11 -> 10; matrix products, arithmetic and copies ran while one was open for 0% -> 0% of each run, Pallas kernels for 20% -> 20%
where the time goes in v4:
time: 183 us; the launch traced here: 182 us
  blocking collectives  53.2 us (29%)
  starting transfers between devices  47.9 us (26%)
  Pallas kernels  40 us (22%)
  waiting for transfers between devices  36.6 us (20%)
  local copies, waits for them, and re-layouts  1.98 us (1%)
    all_to_all x3, blocking collectives, exchange(): lax.all_to_all(v.reshape(experts, rows // experts, width), PLANE, 0, 0, t...  53.2 us
    pallas_call x19, Pallas kernels, call(): pl.pallas_call(kernel, in_specs=specs or [WHOLE] * len(args), out_specs=[...  40 us
    ppermute x12, waiting for transfers between devices, along_x(): return lax.ppermute(v, (X, CORE), pairs)  31.6 us
    ppermute x12, starting transfers between devices, along_x(): return lax.ppermute(v, (X, CORE), pairs)  21.6 us
    ppermute x16, starting transfers between devices, swap_core(): return lax.ppermute(v, CORE, [(0, 1), (1, 0)])  16.4 us
    ppermute x2, starting transfers between devices, line_sum(): lax.ppermute(v, (X, CORE), [(2 * x + c, 2 * (x ^ 1) + 1 - c) for x, c in...  5.95 us
  transfers between devices with their start and end apart: 34, of which 10 were waited for; matrix products, arithmetic and copies ran while one was open for 0% of the time, Pallas kernels for 20%

profile of v4, /device:TPU:1, one launch (start us, length us, event | category | flops | bytes accessed | tf_op | source)
XLA Modules:
  0.0 182.1 jit_solution(2961871395840396450)
XLA Ops:
  3.4 25.2 %all_to_all.15 = bf16[16,8,4224]{2,1,0:T(8,128)(2,1)S(1)} all-to-all(bf16[16,8,4224]{2,1,0:T(8,128)(2,1)S(1)} %bitcast.7), channel_id=1, replica_groups=mesh['dp'=4,'expert_0'=4,'expert_1'=4,'expert_2'=2] {'expert_0','expert_1'}, dimensions={0} | all-to-all | bytes 2162688 | tf_op jit(solution)/shard_map/all_to_all | solution.py:336
  29.1 2.5 %collective-permute-start.2 = (bf16[64,4096]{1,0:T(8,128)(2,1)S(1)}, bf16[64,4096]{1,0:T(8,128)(2,1)S(1)}, u32[]{:S(2)}, u32[]{:S(2)}) collective-permute-start(bf16[64,4096]{1,0:T(8,128)(2,1)S(1)} %get-tuple-element.43.refs_0_), channel_id=1, source_target_pairs={{0,32},{1,97},{32,64},{33,1},{64,96},{65,33},{96,0},{97,65},{2,34}... | collective-permute-start | bytes 1572872 | tf_op jit(solution)/shard_map/ppermute | solution.py:34
  31.6 9.0 %collective-permute-done.2.refs_0_ = bf16[64,4096]{1,0:T(8,128)(2,1)S(1)} collective-permute-done((bf16[64,4096]{1,0:T(8,128)(2,1)S(1)}, bf16[64,4096]{1,0:T(8,128)(2,1)S(1)}, u32[]{:S(2)}, u32[]{:S(2)}) %collective-permute-start.2) | collective-permute-done | bytes 524320 | tf_op jit(solution)/shard_map/ppermute | solution.py:34
  40.6 3.4 %collective-permute-start.7 = (bf16[64,4096]{1,0:T(8,128)(2,1)S(1)}, bf16[64,4096]{1,0:T(8,128)(2,1)S(1)}, u32[]{:S(2)}, u32[]{:S(2)}) collective-permute-start(bf16[64,4096]{1,0:T(8,128)(2,1)S(1)} %collective-permute-done.2.refs_0_), channel_id=1, source_target_pairs={{0,32},{1,97},{32,64},{33,1},{64,96},{65,33},{96,0},{97,65},{2,34}... | collective-permute-start | bytes 1572872 | tf_op jit(solution)/shard_map/ppermute | solution.py:34
  44.0 2.3 %collective-permute-done.3.refs_1_ = bf16[64,4096]{1,0:T(8,128)(2,1)S(1)} collective-permute-done((bf16[64,4096]{1,0:T(8,128)(2,1)S(1)}, bf16[64,4096]{1,0:T(8,128)(2,1)S(1)}, u32[]{:S(2)}, u32[]{:S(2)}) %collective-permute-start.3) | collective-permute-done | bytes 524320 | tf_op jit(solution)/shard_map/ppermute | solution.py:34
  46.8 3.4 %collective-permute-done.7.refs_0_ = bf16[64,4096]{1,0:T(8,128)(2,1)S(1)} collective-permute-done((bf16[64,4096]{1,0:T(8,128)(2,1)S(1)}, bf16[64,4096]{1,0:T(8,128)(2,1)S(1)}, u32[]{:S(2)}, u32[]{:S(2)}) %collective-permute-start.7) | collective-permute-done | bytes 524320 | tf_op jit(solution)/shard_map/ppermute | solution.py:34
  50.2 6.9 %collective-permute-start.8 = (bf16[64,4096]{1,0:T(8,128)(2,1)S(1)}, bf16[64,4096]{1,0:T(8,128)(2,1)S(1)}, u32[]{:S(2)}, u32[]{:S(2)}) collective-permute-start(bf16[64,4096]{1,0:T(8,128)(2,1)S(1)} %collective-permute-done.7.refs_0_), channel_id=1, source_target_pairs={{0,1},{1,0},{2,3},{3,2},{4,5},{5,4},{6,7},{7,6},{8,9},{9,8},{10,11... | collective-permute-start | bytes 1572872 | tf_op jit(solution)/shard_map/ppermute | solution.py:38
  57.1 7.3 %shard_map.70 = (bf16[1,4096,896]{2,1,0:T(8,128)(2,1)S(1)}, bf16[1,4096,896]{2,1,0:T(8,128)(2,1)S(1)}, bf16[1,896,4096]{2,1,0:T(8,128)(2,1)S(1)}) custom-call(bf16[1,4096,896]{2,1,0:T(8,128)(2,1)} %refs_0_.1, bf16[1,4096,896]{2,1,0:T(8,128)(2,1)} %refs_1_.1, bf16[1,896,4096]{2,1,0:T(8,128)(2,1)} %refs_2_.2), custom_call_target="tpu_custom_call" | custom-call | tf_op jit(solution)/shard_map/pallas_call | solution.py:51
  64.4 4.0 %shard_map.73.refs_0_ = bf16[256,896]{1,0:T(8,128)(2,1)S(1)} custom-call(bf16[64,4096]{1,0:T(8,128)(2,1)S(1)} %collective-permute-done.2.refs_0_, bf16[64,4096]{1,0:T(8,128)(2,1)S(1)} %collective-permute-done.3.refs_1_, bf16[64,4096]{1,0:T(8,128)(2,1)S(1)} %collective-permute-done.4.refs_2_, bf16[64,4096]{1,0:T(8,128)(2,1)S(1)} %collective-permute-done.5.refs_3_, ...), custom_call_target="tpu_custom_call" | custom-call | tf_op jit(solution)/shard_map/pallas_call | solution.py:51
  68.5 2.7 %collective-permute-start.13 = (bf16[64,4096]{1,0:T(8,128)(2,1)S(1)}, bf16[64,4096]{1,0:T(8,128)(2,1)S(1)}, u32[]{:S(2)}, u32[]{:S(2)}) collective-permute-start(bf16[64,4096]{1,0:T(8,128)(2,1)S(1)} %get-tuple-element.58.refs_0_), channel_id=1, source_target_pairs={{0,32},{1,97},{32,64},{33,1},{64,96},{65,33},{96,0},{97,65},{2,34}... | collective-permute-start | bytes 1572872 | tf_op jit(solution)/shard_map/ppermute | solution.py:34
  71.1 2.1 %shard_map.75.refs_0_ = bf16[128,896]{1,0:T(8,128)(2,1)S(1)} custom-call(bf16[64,4096]{1,0:T(8,128)(2,1)S(1)} %collective-permute-done.7.refs_0_, bf16[64,4096]{1,0:T(8,128)(2,1)S(1)} %collective-permute-done.8.refs_1_, bf16[1,4096,896]{2,1,0:T(8,128)(2,1)S(1)} %get-tuple-element.44.refs_2_.refs_4_, bf16[1,4096,896]{2,1,0:T(8,128)(2,1)S(1)} %get-tuple-element.45.refs_3_.refs_5_), custom_call_target="tpu_custom_call" | custom-call | tf_op jit(solution)/shard_map/pallas_call | solution.py:51
  74.7 2.6 %shard_map.74 = (f32[64,4096]{1,0:T(8,128)S(1)}, f32[64,4096]{1,0:T(8,128)S(1)}, bf16[128,4096]{1,0:T(8,128)(2,1)S(1)}) custom-call(bf16[256,896]{1,0:T(8,128)(2,1)S(1)} %shard_map.73.refs_0_, bf16[1,896,4096]{2,1,0:T(8,128)(2,1)S(1)} %get-tuple-element.46.refs_1_.refs_3_), custom_call_target="tpu_custom_call" | custom-call | tf_op jit(solution)/shard_map/pallas_call | solution.py:51
  77.9 4.2 %collective-permute-done.13.refs_0_ = bf16[64,4096]{1,0:T(8,128)(2,1)S(1)} collective-permute-done((bf16[64,4096]{1,0:T(8,128)(2,1)S(1)}, bf16[64,4096]{1,0:T(8,128)(2,1)S(1)}, u32[]{:S(2)}, u32[]{:S(2)}) %collective-permute-start.13) | collective-permute-done | bytes 524320 | tf_op jit(solution)/shard_map/ppermute | solution.py:34
  84.2 3.0 %collective-permute-start.10 = (bf16[64,4096]{1,0:T(8,128)(2,1)S(1)}, bf16[64,4096]{1,0:T(8,128)(2,1)S(1)}, u32[]{:S(2)}, u32[]{:S(2)}) collective-permute-start(bf16[64,4096]{1,0:T(8,128)(2,1)S(1)} %add_convert_fusion.5), channel_id=1, source_target_pairs={{0,32},{1,97},{32,64},{33,1},{64,96},{65,33},{96,0},{97,65},{2,34}... | collective-permute-start | bytes 1572872 | tf_op jit(solution)/shard_map/ppermute | solution.py:34
  87.3 8.7 %collective-permute-done.10 = bf16[64,4096]{1,0:T(8,128)(2,1)S(1)} collective-permute-done((bf16[64,4096]{1,0:T(8,128)(2,1)S(1)}, bf16[64,4096]{1,0:T(8,128)(2,1)S(1)}, u32[]{:S(2)}, u32[]{:S(2)}) %collective-permute-start.10) | collective-permute-done | bytes 524320 | tf_op jit(solution)/shard_map/ppermute | solution.py:34
  96.2 2.7 %collective-permute-start.11 = (bf16[64,4096]{1,0:T(8,128)(2,1)S(1)}, bf16[64,4096]{1,0:T(8,128)(2,1)S(1)}, u32[]{:S(2)}, u32[]{:S(2)}) collective-permute-start(bf16[64,4096]{1,0:T(8,128)(2,1)S(1)} %add_convert_fusion.4), channel_id=1, source_target_pairs={{0,32},{1,97},{32,64},{33,1},{64,96},{65,33},{96,0},{97,65},{2,34}... | collective-permute-start | bytes 1572872 | tf_op jit(solution)/shard_map/ppermute | solution.py:34
  99.0 2.1 %shard_map.71.refs_0_ = bf16[128,896]{1,0:T(8,128)(2,1)S(1)} custom-call(bf16[64,4096]{1,0:T(8,128)(2,1)S(1)} %get-tuple-element.43.refs_0_, bf16[64,4096]{1,0:T(8,128)(2,1)S(1)} %collective-permute-done.refs_1_, bf16[1,4096,896]{2,1,0:T(8,128)(2,1)S(1)} %get-tuple-element.44.refs_2_.refs_4_, bf16[1,4096,896]{2,1,0:T(8,128)(2,1)S(1)} %get-tuple-element.45.refs_3_.refs_5_), custom_call_target="tpu_custom_call" | custom-call | tf_op jit(solution)/shard_map/pallas_call | solution.py:51
  102.4 3.4 %collective-permute-start.1 = (bf16[64,4096]{1,0:T(8,128)(2,1)S(1)}, bf16[64,4096]{1,0:T(8,128)(2,1)S(1)}, u32[]{:S(2)}, u32[]{:S(2)}) collective-permute-start(bf16[64,4096]{1,0:T(8,128)(2,1)S(1)} %get-tuple-element.48), channel_id=1, source_target_pairs={{0,1},{1,0},{2,3},{3,2},{4,5},{5,4},{6,7},{7,6},{8,9},{9,8},{10,11... | collective-permute-start | bytes 1572872 | tf_op jit(solution)/shard_map/ppermute | solution.py:38
  105.9 3.9 %shard_map.77 = (f32[256,896]{1,0:T(8,128)S(1)}, f32[256,896]{1,0:T(8,128)S(1)}) custom-call(bf16[64,4096]{1,0:T(8,128)(2,1)S(1)} %collective-permute-done.13.refs_0_, bf16[64,4096]{1,0:T(8,128)(2,1)S(1)} %collective-permute-done.14.refs_1_, bf16[64,4096]{1,0:T(8,128)(2,1)S(1)} %collective-permute-done.15.refs_2_, ...), custom_call_target="tpu_custom_call" | custom-call | tf_op jit(solution)/shard_map/pallas_call | solution.py:51
  111.0 2.4 %collective-permute-start.19 = (f32[8,128]{1,0:T(8,128)S(1)}, f32[8,128]{1,0:T(8,128)S(1)}, u32[]{:S(2)}, u32[]{:S(2)}) collective-permute-start(f32[8,128]{1,0:T(8,128)S(1)} %get-tuple-element.64), channel_id=1, source_target_pairs={{0,33},{1,32},{32,1},{33,0},{64,97},{65,96},{96,65},{97,64},{2,35}... | collective-permute-start | bytes 12296 | tf_op jit(solution)/shard_map/ppermute | solution.py:45
  116.1 2.6 %collective-permute-start.20 = (f32[8,128]{1,0:T(8,128)S(1)}, f32[8,128]{1,0:T(8,128)S(1)}, u32[]{:S(2)}, u32[]{:S(2)}) collective-permute-start(f32[8,128]{1,0:T(8,128)S(1)} %add_add_fusion.1), channel_id=1, source_target_pairs={{0,96},{96,0},{32,64},{64,32},{1,97},{97,1},{33,65},{65,33},{2,98}... | collective-permute-start | bytes 12296 | tf_op jit(solution)/shard_map/ppermute | solution.py:47
  118.6 2.1 %shard_map.81 = (f32[128,896]{1,0:T(8,128)S(1)}, f32[128,896]{1,0:T(8,128)S(1)}) custom-call(bf16[64,4096]{1,0:T(8,128)(2,1)S(1)} %collective-permute-done.22.refs_0_, bf16[64,4096]{1,0:T(8,128)(2,1)S(1)} %collective-permute-done.23.refs_1_, bf16[1,4096,896]{2,1,0:T(8,128)(2,1)S(1)} %get-tuple-element.44.refs_2_.refs_4_, ...), custom_call_target="tpu_custom_call" | custom-call | tf_op jit(solution)/shard_map/pallas_call | solution.py:51
  123.7 3.0 %shard_map.80 = (f32[64,4096]{1,0:T(8,128)S(1)}, f32[64,4096]{1,0:T(8,128)S(1)}, bf16[128,4096]{1,0:T(8,128)(2,1)S(1)}) custom-call(f32[8,128]{1,0:T(8,128)S(1)} %add.71.refs_0_, f32[256,896]{1,0:T(8,128)S(1)} %get-tuple-element.65.refs_1_, f32[256,896]{1,0:T(8,128)S(1)} %get-tuple-element.66.refs_2_, bf16[1,896,4096]{2,1,0:T(8,128)(2,1)S(1)} %get-tuple-element.46.refs_1_.refs_3_), custom_call_target="tpu_custom_call" | custom-call | tf_op jit(solution)/shard_map/pallas_call | solution.py:51
  127.3 2.5 %collective-permute-start.25 = (bf16[64,4096]{1,0:T(8,128)(2,1)S(1)}, bf16[64,4096]{1,0:T(8,128)(2,1)S(1)}, u32[]{:S(2)}, u32[]{:S(2)}) collective-permute-start(bf16[64,4096]{1,0:T(8,128)(2,1)S(1)} %add_convert_fusion.2), channel_id=1, source_target_pairs={{0,32},{1,97},{32,64},{33,1},{64,96},{65,33},{96,0},{97,65},{2,34}... | collective-permute-start | bytes 1572872 | tf_op jit(solution)/shard_map/ppermute | solution.py:34
  129.8 2.1 %shard_map.83 = (f32[128,896]{1,0:T(8,128)S(1)}, f32[128,896]{1,0:T(8,128)S(1)}) custom-call(bf16[64,4096]{1,0:T(8,128)(2,1)S(1)} %get-tuple-element.58.refs_0_, bf16[64,4096]{1,0:T(8,128)(2,1)S(1)} %collective-permute-done.28.refs_1_, bf16[1,4096,896]{2,1,0:T(8,128)(2,1)S(1)} %get-tuple-element.44.refs_2_.refs_4_, ...), custom_call_target="tpu_custom_call" | custom-call | tf_op jit(solution)/shard_map/pallas_call | solution.py:51
  131.9 4.0 %collective-permute-done.25 = bf16[64,4096]{1,0:T(8,128)(2,1)S(1)} collective-permute-done((bf16[64,4096]{1,0:T(8,128)(2,1)S(1)}, bf16[64,4096]{1,0:T(8,128)(2,1)S(1)}, u32[]{:S(2)}, u32[]{:S(2)}) %collective-permute-start.25) | collective-permute-done | bytes 524320 | tf_op jit(solution)/shard_map/ppermute | solution.py:34
  136.1 3.2 %collective-permute-start.26 = (bf16[64,4096]{1,0:T(8,128)(2,1)S(1)}, bf16[64,4096]{1,0:T(8,128)(2,1)S(1)}, u32[]{:S(2)}, u32[]{:S(2)}) collective-permute-start(bf16[64,4096]{1,0:T(8,128)(2,1)S(1)} %add_convert_fusion.1), channel_id=1, source_target_pairs={{0,32},{1,97},{32,64},{33,1},{64,96},{65,33},{96,0},{97,65},{2,34}... | collective-permute-start | bytes 1572872 | tf_op jit(solution)/shard_map/ppermute | solution.py:34
  141.0 2.1 %collective-permute-start.29 = (bf16[64,4096]{1,0:T(8,128)(2,1)S(1)}, bf16[64,4096]{1,0:T(8,128)(2,1)S(1)}, u32[]{:S(2)}, u32[]{:S(2)}) collective-permute-start(bf16[64,4096]{1,0:T(8,128)(2,1)S(1)} %get-tuple-element.81), channel_id=1, source_target_pairs={{0,1},{1,0},{2,3},{3,2},{4,5},{5,4},{6,7},{7,6},{8,9},{9,8},{10,11... | collective-permute-start | bytes 1572872 | tf_op jit(solution)/shard_map/ppermute | solution.py:38
  143.1 14.0 %all_to_all.16 = bf16[16,8,2048]{2,1,0:T(8,128)(2,1)S(1)} all-to-all(bf16[16,8,2048]{2,1,0:T(8,128)(2,1)S(1)} %bitcast.10), channel_id=1, replica_groups=mesh['dp'=4,'expert_0'=4,'expert_1'=4,'expert_2'=2] {'expert_0','expert_1'}, dimensions={0} | all-to-all | bytes 1048576 | tf_op jit(solution)/shard_map/all_to_all | solution.py:336
  158.2 14.1 %all_to_all.17 = bf16[16,8,2176]{2,1,0:T(8,128)(2,1)S(1)} all-to-all(bf16[16,8,2176]{2,1,0:T(8,128)(2,1)S(1)} %bitcast.8), channel_id=1, replica_groups=mesh['dp'=4,'expert_0'=4,'expert_1'=4,'expert_2'=2] {'expert_0','expert_1'}, dimensions={0} | all-to-all | bytes 1114112 | tf_op jit(solution)/shard_map/all_to_all | solution.py:336
  172.4 3.6 %collective-permute-start.32 = (f32[16,128]{1,0:T(8,128)S(1)}, f32[16,128]{1,0:T(8,128)S(1)}, u32[]{:S(2)}, u32[]{:S(2)}) collective-permute-start(f32[16,128]{1,0:T(8,128)S(1)} %convert_element_type.59), channel_id=1, source_target_pairs={{0,33},{1,32},{32,1},{33,0},{64,97},{65,96},{96,65},{97,64},{2,35}... | collective-permute-start | bytes 24584 | tf_op jit(solution)/shard_map/ppermute | solution.py:45
  178.2 1.8 shard_map.86
  (78 shorter events, 24.4 us)
Async XLA Ops:
  29.1 11.6 %collective-permute-start.2 = (bf16[64,4096]{1,0:T(8,128)(2,1)S(1)}, bf16[64,4096]{1,0:T(8,128)(2,1)S(1)}, u32[]{:S(2)}, u32[]{:S(2)}) collective-permute-start(bf16[64,4096]{1,0:T(8,128)(2,1)S(1)} %get-tuple-element.43.refs_0_), channel_id=1, source_target_pairs={{0,32},{1,97},{32,64},{33,1},{64,96},{65,33},{96,0},{97,65},{2,34}... | collective-permute-start | bytes 1572872 | tf_op jit(solution)/shard_map/ppermute | solution.py:34
  31.6 14.7 %collective-permute-start.3 = (bf16[64,4096]{1,0:T(8,128)(2,1)S(1)}, bf16[64,4096]{1,0:T(8,128)(2,1)S(1)}, u32[]{:S(2)}, u32[]{:S(2)}) collective-permute-start(bf16[64,4096]{1,0:T(8,128)(2,1)S(1)} %get-tuple-element.43.refs_0_), channel_id=1, source_target_pairs={{0,96},{1,33},{32,0},{33,65},{64,32},{65,97},{96,64},{97,1},{2,98}... | collective-permute-start | bytes 1572872 | tf_op jit(solution)/shard_map/ppermute | solution.py:34
  40.6 9.5 %collective-permute-start.7 = (bf16[64,4096]{1,0:T(8,128)(2,1)S(1)}, bf16[64,4096]{1,0:T(8,128)(2,1)S(1)}, u32[]{:S(2)}, u32[]{:S(2)}) collective-permute-start(bf16[64,4096]{1,0:T(8,128)(2,1)S(1)} %collective-permute-done.2.refs_0_), channel_id=1, source_target_pairs={{0,32},{1,97},{32,64},{33,1},{64,96},{65,33},{96,0},{97,65},{2,34}... | collective-permute-start | bytes 1572872 | tf_op jit(solution)/shard_map/ppermute | solution.py:34
  46.3 18.1 %collective-permute-start.5 = (bf16[64,4096]{1,0:T(8,128)(2,1)S(1)}, bf16[64,4096]{1,0:T(8,128)(2,1)S(1)}, u32[]{:S(2)}, u32[]{:S(2)}) collective-permute-start(bf16[64,4096]{1,0:T(8,128)(2,1)S(1)} %collective-permute-done.3.refs_1_), channel_id=1, source_target_pairs={{0,1},{1,0},{2,3},{3,2},{4,5},{5,4},{6,7},{7,6},{8,9},{9,8},{10,11... | collective-permute-start | bytes 1572872 | tf_op jit(solution)/shard_map/ppermute | solution.py:38
  46.7 17.7 %collective-permute-start.4 = (bf16[64,4096]{1,0:T(8,128)(2,1)S(1)}, bf16[64,4096]{1,0:T(8,128)(2,1)S(1)}, u32[]{:S(2)}, u32[]{:S(2)}) collective-permute-start(bf16[64,4096]{1,0:T(8,128)(2,1)S(1)} %collective-permute-done.2.refs_0_), channel_id=1, source_target_pairs={{0,1},{1,0},{2,3},{3,2},{4,5},{5,4},{6,7},{7,6},{8,9},{9,8},{10,11... | collective-permute-start | bytes 1572872 | tf_op jit(solution)/shard_map/ppermute | solution.py:38
  50.2 21.0 %collective-permute-start.8 = (bf16[64,4096]{1,0:T(8,128)(2,1)S(1)}, bf16[64,4096]{1,0:T(8,128)(2,1)S(1)}, u32[]{:S(2)}, u32[]{:S(2)}) collective-permute-start(bf16[64,4096]{1,0:T(8,128)(2,1)S(1)} %collective-permute-done.7.refs_0_), channel_id=1, source_target_pairs={{0,1},{1,0},{2,3},{3,2},{4,5},{5,4},{6,7},{7,6},{8,9},{9,8},{10,11... | collective-permute-start | bytes 1572872 | tf_op jit(solution)/shard_map/ppermute | solution.py:38
  68.4 15.1 %collective-permute-start.14 = (bf16[64,4096]{1,0:T(8,128)(2,1)S(1)}, bf16[64,4096]{1,0:T(8,128)(2,1)S(1)}, u32[]{:S(2)}, u32[]{:S(2)}) collective-permute-start(bf16[64,4096]{1,0:T(8,128)(2,1)S(1)} %get-tuple-element.58.refs_0_), channel_id=1, source_target_pairs={{0,96},{1,33},{32,0},{33,65},{64,32},{65,97},{96,64},{97,1},{2,98}... | collective-permute-start | bytes 1572872 | tf_op jit(solution)/shard_map/ppermute | solution.py:34
  68.5 13.6 %collective-permute-start.13 = (bf16[64,4096]{1,0:T(8,128)(2,1)S(1)}, bf16[64,4096]{1,0:T(8,128)(2,1)S(1)}, u32[]{:S(2)}, u32[]{:S(2)}) collective-permute-start(bf16[64,4096]{1,0:T(8,128)(2,1)S(1)} %get-tuple-element.58.refs_0_), channel_id=1, source_target_pairs={{0,32},{1,97},{32,64},{33,1},{64,96},{65,33},{96,0},{97,65},{2,34}... | collective-permute-start | bytes 1572872 | tf_op jit(solution)/shard_map/ppermute | solution.py:34
  74.6 9.5 %collective-permute-start.9 = (bf16[64,4096]{1,0:T(8,128)(2,1)S(1)}, bf16[64,4096]{1,0:T(8,128)(2,1)S(1)}, u32[]{:S(2)}, u32[]{:S(2)}) collective-permute-start(bf16[64,4096]{1,0:T(8,128)(2,1)S(1)} %get-tuple-element.54), channel_id=1, source_target_pairs={{0,1},{1,0},{2,3},{3,2},{4,5},{5,4},{6,7},{7,6},{8,9},{9,8},{10,11... | collective-permute-start | bytes 1572872 | tf_op jit(solution)/shard_map/ppermute | solution.py:38
  77.2 7.0 %collective-permute-start.6 = (bf16[128,4096]{1,0:T(8,128)(2,1)S(1)}, bf16[128,4096]{1,0:T(8,128)(2,1)S(1)}, u32[]{:S(2)}, u32[]{:S(2)}) collective-permute-start(bf16[128,4096]{1,0:T(8,128)(2,1)S(1)} %get-tuple-element.52), channel_id=1, source_target_pairs={{0,1},{1,0},{2,3},{3,2},{4,5},{5,4},{6,7},{7,6},{8,9},{9,8},{10,11... | collective-permute-start | bytes 3145736 | tf_op jit(solution)/shard_map/ppermute | solution.py:38
  77.8 18.4 %collective-permute-start = (bf16[64,4096]{1,0:T(8,128)(2,1)S(1)}, bf16[64,4096]{1,0:T(8,128)(2,1)S(1)}, u32[]{:S(2)}, u32[]{:S(2)}) collective-permute-start(bf16[64,4096]{1,0:T(8,128)(2,1)S(1)} %get-tuple-element.43.refs_0_), channel_id=1, source_target_pairs={{0,1},{1,0},{2,3},{3,2},{4,5},{5,4},{6,7},{7,6},{8,9},{9,8},{10,11... | collective-permute-start | bytes 1572872 | tf_op jit(solution)/shard_map/ppermute | solution.py:38
  82.1 23.7 %collective-permute-start.22 = (bf16[64,4096]{1,0:T(8,128)(2,1)S(1)}, bf16[64,4096]{1,0:T(8,128)(2,1)S(1)}, u32[]{:S(2)}, u32[]{:S(2)}) collective-permute-start(bf16[64,4096]{1,0:T(8,128)(2,1)S(1)} %collective-permute-done.13.refs_0_), channel_id=1, source_target_pairs={{0,32},{1,97},{32,64},{33,1},{64,96},{65,33},{96,0},{97,65},{2,34}... | collective-permute-start | bytes 1572872 | tf_op jit(solution)/shard_map/ppermute | solution.py:34
  83.5 22.4 %collective-permute-start.15 = (bf16[64,4096]{1,0:T(8,128)(2,1)S(1)}, bf16[64,4096]{1,0:T(8,128)(2,1)S(1)}, u32[]{:S(2)}, u32[]{:S(2)}) collective-permute-start(bf16[64,4096]{1,0:T(8,128)(2,1)S(1)} %collective-permute-done.13.refs_0_), channel_id=1, source_target_pairs={{0,1},{1,0},{2,3},{3,2},{4,5},{5,4},{6,7},{7,6},{8,9},{9,8},{10,11... | collective-permute-start | bytes 1572872 | tf_op jit(solution)/shard_map/ppermute | solution.py:38
  84.0 18.4 %collective-permute-start.16 = (bf16[64,4096]{1,0:T(8,128)(2,1)S(1)}, bf16[64,4096]{1,0:T(8,128)(2,1)S(1)}, u32[]{:S(2)}, u32[]{:S(2)}) collective-permute-start(bf16[64,4096]{1,0:T(8,128)(2,1)S(1)} %collective-permute-done.14.refs_1_), channel_id=1, source_target_pairs={{0,1},{1,0},{2,3},{3,2},{4,5},{5,4},{6,7},{7,6},{8,9},{9,8},{10,11... | collective-permute-start | bytes 1572872 | tf_op jit(solution)/shard_map/ppermute | solution.py:38
  84.2 11.8 %collective-permute-start.10 = (bf16[64,4096]{1,0:T(8,128)(2,1)S(1)}, bf16[64,4096]{1,0:T(8,128)(2,1)S(1)}, u32[]{:S(2)}, u32[]{:S(2)}) collective-permute-start(bf16[64,4096]{1,0:T(8,128)(2,1)S(1)} %add_convert_fusion.5), channel_id=1, source_target_pairs={{0,32},{1,97},{32,64},{33,1},{64,96},{65,33},{96,0},{97,65},{2,34}... | collective-permute-start | bytes 1572872 | tf_op jit(solution)/shard_map/ppermute | solution.py:34
  96.0 13.8 %collective-permute-start.12 = (bf16[64,4096]{1,0:T(8,128)(2,1)S(1)}, bf16[64,4096]{1,0:T(8,128)(2,1)S(1)}, u32[]{:S(2)}, u32[]{:S(2)}) collective-permute-start(bf16[64,4096]{1,0:T(8,128)(2,1)S(1)} %add_convert_fusion.3), channel_id=1, source_target_pairs={{0,96},{1,33},{32,0},{33,65},{64,32},{65,97},{96,64},{97,1},{2,98}... | collective-permute-start | bytes 1572872 | tf_op jit(solution)/shard_map/ppermute | solution.py:34
  96.2 13.7 %collective-permute-start.11 = (bf16[64,4096]{1,0:T(8,128)(2,1)S(1)}, bf16[64,4096]{1,0:T(8,128)(2,1)S(1)}, u32[]{:S(2)}, u32[]{:S(2)}) collective-permute-start(bf16[64,4096]{1,0:T(8,128)(2,1)S(1)} %add_convert_fusion.4), channel_id=1, source_target_pairs={{0,32},{1,97},{32,64},{33,1},{64,96},{65,33},{96,0},{97,65},{2,34}... | collective-permute-start | bytes 1572872 | tf_op jit(solution)/shard_map/ppermute | solution.py:34
  102.4 7.5 %collective-permute-start.1 = (bf16[64,4096]{1,0:T(8,128)(2,1)S(1)}, bf16[64,4096]{1,0:T(8,128)(2,1)S(1)}, u32[]{:S(2)}, u32[]{:S(2)}) collective-permute-start(bf16[64,4096]{1,0:T(8,128)(2,1)S(1)} %get-tuple-element.48), channel_id=1, source_target_pairs={{0,1},{1,0},{2,3},{3,2},{4,5},{5,4},{6,7},{7,6},{8,9},{9,8},{10,11... | collective-permute-start | bytes 1572872 | tf_op jit(solution)/shard_map/ppermute | solution.py:38
  105.8 12.8 %collective-permute-start.23 = (bf16[64,4096]{1,0:T(8,128)(2,1)S(1)}, bf16[64,4096]{1,0:T(8,128)(2,1)S(1)}, u32[]{:S(2)}, u32[]{:S(2)}) collective-permute-start(bf16[64,4096]{1,0:T(8,128)(2,1)S(1)} %collective-permute-done.22.refs_0_), channel_id=1, source_target_pairs={{0,1},{1,0},{2,3},{3,2},{4,5},{5,4},{6,7},{7,6},{8,9},{9,8},{10,11... | collective-permute-start | bytes 1572872 | tf_op jit(solution)/shard_map/ppermute | solution.py:38
  111.0 3.7 %collective-permute-start.19 = (f32[8,128]{1,0:T(8,128)S(1)}, f32[8,128]{1,0:T(8,128)S(1)}, u32[]{:S(2)}, u32[]{:S(2)}) collective-permute-start(f32[8,128]{1,0:T(8,128)S(1)} %get-tuple-element.64), channel_id=1, source_target_pairs={{0,33},{1,32},{32,1},{33,0},{64,97},{65,96},{96,65},{97,64},{2,35}... | collective-permute-start | bytes 12296 | tf_op jit(solution)/shard_map/ppermute | solution.py:45
  113.4 2.7 %collective-permute-start.18 = (f32[8,128]{1,0:T(8,128)S(1)}, f32[8,128]{1,0:T(8,128)S(1)}, u32[]{:S(2)}, u32[]{:S(2)}) collective-permute-start(f32[8,128]{1,0:T(8,128)S(1)} %get-tuple-element.64), channel_id=1, source_target_pairs={{0,32},{1,33},{32,0},{33,1},{64,96},{65,97},{96,64},{97,65},{2,34}... | collective-permute-start | bytes 12296 | tf_op jit(solution)/shard_map/ppermute | solution.py:44
  116.1 4.6 %collective-permute-start.20 = (f32[8,128]{1,0:T(8,128)S(1)}, f32[8,128]{1,0:T(8,128)S(1)}, u32[]{:S(2)}, u32[]{:S(2)}) collective-permute-start(f32[8,128]{1,0:T(8,128)S(1)} %add_add_fusion.1), channel_id=1, source_target_pairs={{0,96},{96,0},{32,64},{64,32},{1,97},{97,1},{33,65},{65,33},{2,98}... | collective-permute-start | bytes 12296 | tf_op jit(solution)/shard_map/ppermute | solution.py:47
  122.2 5.0 %collective-permute-start.24 = (bf16[64,4096]{1,0:T(8,128)(2,1)S(1)}, bf16[64,4096]{1,0:T(8,128)(2,1)S(1)}, u32[]{:S(2)}, u32[]{:S(2)}) collective-permute-start(bf16[64,4096]{1,0:T(8,128)(2,1)S(1)} %get-tuple-element.72), channel_id=1, source_target_pairs={{0,1},{1,0},{2,3},{3,2},{4,5},{5,4},{6,7},{7,6},{8,9},{9,8},{10,11... | collective-permute-start | bytes 1572872 | tf_op jit(solution)/shard_map/ppermute | solution.py:38
  123.6 6.2 %collective-permute-start.28 = (bf16[64,4096]{1,0:T(8,128)(2,1)S(1)}, bf16[64,4096]{1,0:T(8,128)(2,1)S(1)}, u32[]{:S(2)}, u32[]{:S(2)}) collective-permute-start(bf16[64,4096]{1,0:T(8,128)(2,1)S(1)} %get-tuple-element.58.refs_0_), channel_id=1, source_target_pairs={{0,1},{1,0},{2,3},{3,2},{4,5},{5,4},{6,7},{7,6},{8,9},{9,8},{10,11... | collective-permute-start | bytes 1572872 | tf_op jit(solution)/shard_map/ppermute | solution.py:38
  126.7 9.2 %collective-permute-start.21 = (bf16[128,4096]{1,0:T(8,128)(2,1)S(1)}, bf16[128,4096]{1,0:T(8,128)(2,1)S(1)}, u32[]{:S(2)}, u32[]{:S(2)}) collective-permute-start(bf16[128,4096]{1,0:T(8,128)(2,1)S(1)} %get-tuple-element.68), channel_id=1, source_target_pairs={{0,1},{1,0},{2,3},{3,2},{4,5},{5,4},{6,7},{7,6},{8,9},{9,8},{10,11... | collective-permute-start | bytes 3145736 | tf_op jit(solution)/shard_map/ppermute | solution.py:38
  127.3 8.6 %collective-permute-start.25 = (bf16[64,4096]{1,0:T(8,128)(2,1)S(1)}, bf16[64,4096]{1,0:T(8,128)(2,1)S(1)}, u32[]{:S(2)}, u32[]{:S(2)}) collective-permute-start(bf16[64,4096]{1,0:T(8,128)(2,1)S(1)} %add_convert_fusion.2), channel_id=1, source_target_pairs={{0,32},{1,97},{32,64},{33,1},{64,96},{65,33},{96,0},{97,65},{2,34}... | collective-permute-start | bytes 1572872 | tf_op jit(solution)/shard_map/ppermute | solution.py:34
  136.1 20.9 %collective-permute-start.26 = (bf16[64,4096]{1,0:T(8,128)(2,1)S(1)}, bf16[64,4096]{1,0:T(8,128)(2,1)S(1)}, u32[]{:S(2)}, u32[]{:S(2)}) collective-permute-start(bf16[64,4096]{1,0:T(8,128)(2,1)S(1)} %add_convert_fusion.1), channel_id=1, source_target_pairs={{0,32},{1,97},{32,64},{33,1},{64,96},{65,33},{96,0},{97,65},{2,34}... | collective-permute-start | bytes 1572872 | tf_op jit(solution)/shard_map/ppermute | solution.py:34
  139.4 17.6 %collective-permute-start.27 = (bf16[64,4096]{1,0:T(8,128)(2,1)S(1)}, bf16[64,4096]{1,0:T(8,128)(2,1)S(1)}, u32[]{:S(2)}, u32[]{:S(2)}) collective-permute-start(bf16[64,4096]{1,0:T(8,128)(2,1)S(1)} %add_convert_fusion), channel_id=1, source_target_pairs={{0,96},{1,33},{32,0},{33,65},{64,32},{65,97},{96,64},{97,1},{2,98}... | collective-permute-start | bytes 1572872 | tf_op jit(solution)/shard_map/ppermute | solution.py:34
  141.0 16.1 %collective-permute-start.29 = (bf16[64,4096]{1,0:T(8,128)(2,1)S(1)}, bf16[64,4096]{1,0:T(8,128)(2,1)S(1)}, u32[]{:S(2)}, u32[]{:S(2)}) collective-permute-start(bf16[64,4096]{1,0:T(8,128)(2,1)S(1)} %get-tuple-element.81), channel_id=1, source_target_pairs={{0,1},{1,0},{2,3},{3,2},{4,5},{5,4},{6,7},{7,6},{8,9},{9,8},{10,11... | collective-permute-start | bytes 1572872 | tf_op jit(solution)/shard_map/ppermute | solution.py:38
  172.3 3.7 %collective-permute-start.31 = (f32[16,128]{1,0:T(8,128)S(1)}, f32[16,128]{1,0:T(8,128)S(1)}, u32[]{:S(2)}, u32[]{:S(2)}) collective-permute-start(f32[16,128]{1,0:T(8,128)S(1)} %convert_element_type.59), channel_id=1, source_target_pairs={{0,32},{1,33},{32,0},{33,1},{64,96},{65,97},{96,64},{97,65},{2,34}... | collective-permute-start | bytes 24584 | tf_op jit(solution)/shard_map/ppermute | solution.py:44
  172.4 5.2 %collective-permute-start.32 = (f32[16,128]{1,0:T(8,128)S(1)}, f32[16,128]{1,0:T(8,128)S(1)}, u32[]{:S(2)}, u32[]{:S(2)}) collective-permute-start(f32[16,128]{1,0:T(8,128)S(1)} %convert_element_type.59), channel_id=1, source_target_pairs={{0,33},{1,32},{32,1},{33,0},{64,97},{65,96},{96,65},{97,64},{2,35}... | collective-permute-start | bytes 24584 | tf_op jit(solution)/shard_map/ppermute | solution.py:45
  177.6 3.8 %collective-permute-start.33 = (f32[16,128]{1,0:T(8,128)S(1)}, f32[16,128]{1,0:T(8,128)S(1)}, u32[]{:S(2)}, u32[]{:S(2)}) collective-permute-start(f32[16,128]{1,0:T(8,128)S(1)} %add_add_fusion), channel_id=1, source_target_pairs={{0,96},{96,0},{32,64},{64,32},{1,97},{97,1},{33,65},{65,33},{2,98}... | collective-permute-start | bytes 24584 | tf_op jit(solution)/shard_map/ppermute | solution.py:47
  (5 other events, 44.2 us)
